TPU v7x, 128 devices: a whole 4x4x4 slice. The times are simulated.
128 devices in a mesh: gx: 2 (over core), gy: 4 (over x), gz: 16 (over z, y).
Axes of the slice: x: 4, y: 4, z: 4, core: 2. Of those that a mesh axis runs over, the one named last changes fastest.
Arguments:
- right_side: float32 [96, 192, 768], P('gx', 'gy', 'gz'), may hold values from -6 to 6
- face_coef: float32 [3, 96, 192, 768], P(None, 'gx', 'gy', 'gz'), may hold values from 0.3 to 3
- absorption: float32 [96, 192, 768], P('gx', 'gy', 'gz'), may hold values from 0.001 to 0.01
Outputs:
- solution: float32 [96, 192, 768], P('gx', 'gy', 'gz')
- residual: float32 [96, 192, 768], P('gx', 'gy', 'gz')
- relative_norm: float32 [], replicated
All inputs are finite; a program needn't handle non-finite values.
Results may differ from a plain program's by a relative error of at most 0.0003.
Values sent between devices are 32-bit elements.
A program may use at most 192 MiB of HBM per device.

v0:
```python
import jax
import jax.numpy as jnp
from jax import lax
from jax.sharding import Mesh
from jax.sharding import PartitionSpec as P

LEVELS = 5
SWEEPS = 3
BOTTOM = 6
GX_GY_GZ = ("gx", "gy", "gz_0", "gz_1")
GZ = ("gz_0", "gz_1")


cheb_low = 0.25
cheb_high = 2.0


def with_halo(value, sides, width, wrap):
    edges = {}
    for axis, dim in sides:
        devices, length = lax.axis_size(axis), value.shape[dim]
        up = [(i, (i + 1) % devices) for i in range(devices if wrap else devices - 1)]
        last = lax.slice_in_dim(value, length - width, length, axis=dim)
        leading = lax.slice_in_dim(value, 0, width, axis=dim)
        edges[dim] = lax.ppermute(last, axis, up), lax.ppermute(
            leading, axis, [(b, a) for a, b in up]
        )
    done = []
    for _, dim in sides:
        low, high = edges[dim]
        around = [(width, width) if d in done else (0, 0) for d in range(value.ndim)]
        value = jnp.concatenate([jnp.pad(low, around), value, jnp.pad(high, around)], axis=dim)
        done.append(dim)
    return value


def from_behind(value, axis, by):
    devices = lax.axis_size(axis)
    pairs = [(i, i + by) for i in range(devices) if 0 <= i + by < devices]
    return lax.ppermute(value, axis, pairs)


def over_axes(value, axes):
    for axis in axes:
        value = lax.psum(value, axis)
    return value


def apply_stencil(field, stencil, weight, padded):
    low_x = padded[:-2, 1:-1, 1:-1]
    high_x = padded[2:, 1:-1, 1:-1]
    low_y = padded[1:-1, :-2, 1:-1]
    high_y = padded[1:-1, 2:, 1:-1]
    low_z = padded[1:-1, 1:-1, :-2]
    high_z = padded[1:-1, 1:-1, 2:]
    flux = stencil[0] * (field - low_x) + stencil[3] * (field - high_x)
    flux = flux + stencil[1] * (field - low_y) + stencil[4] * (field - high_y)
    flux = flux + stencil[2] * (field - low_z) + stencil[5] * (field - high_z)
    return stencil[6] * field + weight * flux


def inverse_diagonal(stencil, weight):
    total = stencil[0] + stencil[3] + stencil[1] + stencil[4] + stencil[2] + stencil[5]
    return 1.0 / (stencil[6] + weight * total)


def chebyshev(iterate, source, stencil, weight, sweeps, from_zero, pad_field):
    centre = 0.5 * (cheb_high + cheb_low)
    half_width = 0.5 * (cheb_high - cheb_low)
    cheb_ratio = centre / half_width
    cheb_rho = 1.0 / cheb_ratio
    scaling = inverse_diagonal(stencil, weight)
    if from_zero:
        remainder = source
    else:
        remainder = source - apply_stencil(iterate, stencil, weight, pad_field(iterate))
    update = scaling * remainder * (1.0 / centre)
    for sweep in range(sweeps):
        iterate = iterate + update
        if sweep + 1 < sweeps:
            remainder = source - apply_stencil(iterate, stencil, weight, pad_field(iterate))
            next_rho = 1.0 / (2.0 * cheb_ratio - cheb_rho)
            update = next_rho * cheb_rho * update + 2.0 * next_rho / half_width * (
                scaling * remainder
            )
            cheb_rho = next_rho
    return iterate


def conjugate(source, stencil, weight, pad_field, total):
    iterate = jnp.zeros_like(source)
    remainder = source
    search = source
    norm_now = total(remainder * remainder)
    for step in range(BOTTOM):
        applied = apply_stencil(search, stencil, weight, pad_field(search))
        step_size = norm_now / total(search * applied)
        iterate = iterate + step_size * search
        if step + 1 < BOTTOM:
            remainder = remainder - step_size * applied
            norm_next = total(remainder * remainder)
            search = remainder + norm_next / norm_now * search
            norm_now = norm_next
    return iterate


def average_cells(field):
    blocks = field.reshape(field.shape[0] // 2, 2, field.shape[1] // 2, 2, field.shape[2] // 2, 2)
    return jnp.sum(blocks, axis=(1, 3, 5)) * 0.125


def average_faces(faces):
    halves = (faces.shape[1] // 2, 2, faces.shape[2] // 2, 2, faces.shape[3] // 2, 2)
    along_x = faces[0].reshape(halves)[:, 0]
    along_y = faces[1].reshape(halves)[:, :, :, 0]
    along_z = faces[2].reshape(halves)[..., 0]
    return (
        jnp.stack(
            [
                jnp.sum(along_x, axis=(2, 4)),
                jnp.sum(along_y, axis=(1, 4)),
                jnp.sum(along_z, axis=(1, 3)),
            ]
        )
        * 0.25
    )


def repeat_cells(field):
    shape = field.shape
    wide = jnp.broadcast_to(
        field[:, None, :, None, :, None], (shape[0], 2, shape[1], 2, shape[2], 2)
    )
    return wide.reshape(2 * shape[0], 2 * shape[1], 2 * shape[2])


def pad_zero(field):
    return jnp.pad(field, 1)


def halo_field(field):
    return with_halo(field, (("gx", 0), ("gy", 1), (GZ, 2)), 1, False)


def prepare(faces, cells):
    above_x = from_behind(faces[0, :1], "gx", -1)
    above_y = from_behind(faces[1, :, :1], "gy", -1)
    above_z = from_behind(faces[2, :, :, :1], GZ, -1)
    high_x = jnp.concatenate([faces[0, 1:], above_x], axis=0)
    high_y = jnp.concatenate([faces[1, :, 1:], above_y], axis=1)
    high_z = jnp.concatenate([faces[2, :, :, 1:], above_z], axis=2)
    return jnp.stack([faces[0], faces[1], faces[2], high_x, high_y, high_z, cells])


def assemble(flat, count, block):
    count_x = lax.axis_size("gx")
    count_y = lax.axis_size("gy")
    count_z = lax.axis_size(GZ)
    grid = flat.reshape(count_x, count_y, count_z, count, block[0], block[1], block[2])
    grid = jnp.transpose(grid, (3, 0, 4, 1, 5, 2, 6))
    return grid.reshape(count, count_x * block[0], count_y * block[1], count_z * block[2])


def shards(right_side, face_coef, absorption):
    source_sq = over_axes(jnp.sum(right_side * right_side), GX_GY_GZ)
    stencils = []
    faces = face_coef
    cells = absorption
    for level in range(LEVELS):
        stencils.append(prepare(faces, cells))
        if level + 1 < LEVELS:
            faces = average_faces(faces)
            cells = average_cells(cells)
    sources = []
    iterates = []
    source = right_side
    for level in range(LEVELS - 1):
        weight = 0.25**level
        iterate = chebyshev(
            jnp.zeros_like(source), source, stencils[level], weight, SWEEPS, True, halo_field
        )
        remainder = source - apply_stencil(iterate, stencils[level], weight, halo_field(iterate))
        sources.append(source)
        iterates.append(iterate)
        source = average_cells(remainder)
    coarse = stencils[LEVELS - 1]
    block = source.shape
    weight_low = 0.25 ** (LEVELS - 1)
    flat_coef = lax.all_gather(coarse.reshape(-1), GX_GY_GZ, axis=0, tiled=True)
    flat_source = lax.all_gather(source.reshape(-1), GX_GY_GZ, axis=0, tiled=True)
    whole_coef = assemble(flat_coef, 7, block)
    whole_source = assemble(flat_source, 1, block)[0]
    whole = conjugate(whole_source, whole_coef, weight_low, pad_zero, jnp.sum)
    starts = (
        lax.axis_index("gx") * block[0],
        lax.axis_index("gy") * block[1],
        lax.axis_index(GZ) * block[2],
    )
    correction = lax.dynamic_slice(whole, starts, block)
    for level in reversed(range(LEVELS - 1)):
        weight = 0.25**level
        iterate = iterates[level] + repeat_cells(correction)
        correction = chebyshev(
            iterate, sources[level], stencils[level], weight, SWEEPS, False, halo_field
        )
    residual = right_side - apply_stencil(correction, stencils[0], 1.0, halo_field(correction))
    residual_sq = over_axes(jnp.sum(residual * residual), GX_GY_GZ)
    relative_norm = jnp.sqrt(residual_sq / source_sq)
    return (correction, residual, relative_norm)


def solution(mesh):
    torus = Mesh(
        mesh.devices.reshape(mesh.shape["gx"], mesh.shape["gy"], 4, 4), ("gx", "gy", "gz_0", "gz_1")
    )
    in_specs = (P("gx", "gy", GZ), P(None, "gx", "gy", GZ), P("gx", "gy", GZ))
    out_specs = (P("gx", "gy", GZ), P("gx", "gy", GZ), P())
    return jax.shard_map(
        shards, mesh=torus, in_specs=in_specs, out_specs=out_specs, check_vma=False
    )
```

profile of v0, /device:TPU:0, one launch (start us, length us, event | category | flops | bytes accessed | tf_op | source)
XLA Modules:
  0.0 1233.2 jit_solution(8616450484737864457)
XLA Ops:
  24.3 15.4 %reshape_squeeze.37 = f32[24,2,24,2,24,2]{5,4,3,2,1,0:T(8,128)} reshape(f32[1,48,48,48]{3,2,1,0:T(8,128)} %get-tuple-element.74) | data formatting | bytes 884736 | tf_op jit(solution)/shard_map/reshape;squeeze | solution.py:115
  39.7 7.8 slice_reduce_fusion.1
  47.5 15.4 %reshape_squeeze.38 = f32[24,2,24,2,24,2]{5,4,3,2,1,0:T(8,128)} reshape(f32[1,48,48,48]{3,2,1,0:T(8,128)} %get-tuple-element.73) | data formatting | bytes 884736 | tf_op jit(solution)/shard_map/reshape;squeeze | solution.py:116
  62.8 11.8 slice_reduce_fusion
  74.6 15.4 %reshape_squeeze.36 = f32[24,2,24,2,24,2]{5,4,3,2,1,0:T(8,128)} reshape(f32[1,48,48,48]{3,2,1,0:T(8,128)} %get-tuple-element.72) | data formatting | bytes 884736 | tf_op jit(solution)/shard_map/reshape;squeeze | solution.py:114
  90.0 7.0 slice_reduce_fusion.2
  191.4 11.1 multiply_add_fusion.1
  236.2 9.9 fusion.122
  275.2 15.4 %reshape.86 = f32[24,2,24,2,24,2]{5,4,3,2,1,0:T(8,128)} reshape(f32[48,48,48]{2,1,0:T(8,128)} %param.5) | data formatting | bytes 884736 | tf_op jit(solution)/shard_map/reshape | solution.py:108
  296.3 10.8 reduce_sum.306
  320.1 10.6 fusion.97
  330.7 15.4 %reshape.87 = f32[24,2,24,2,24,2]{5,4,3,2,1,0:T(8,128)} reshape(f32[48,48,48]{2,1,0:T(8,128)} %fusion.97) | data formatting | bytes 884736 | tf_op jit(solution)/shard_map/reshape | solution.py:108
  346.1 10.8 reduce_sum.310
  388.5 6.0 collective-permute-start.34
  414.8 6.9 collective-permute-start.43
  457.8 6.4 collective-permute-start.47
  464.8 6.3 collective-permute-start.49
  511.9 7.3 collective-permute-start.64
  572.6 6.4 collective-permute-start.76
  591.6 6.4 collective-permute-start.82
  619.3 78.8 %all-reduce.106 = f32[3456]{0:T(1024)} all-reduce(f32[3456]{0:T(1024)} %dynamic-update-slice), channel_id=1, replica_groups=mesh['gx'=2,'gy'=4,'gz_0'=4,'gz_1'=4] {'gx','gy','gz_0','gz_1'}, use_global_device_ids=true, to_apply=%add.106 | all-reduce | flops 3456 | bytes 27648
  705.3 6.1 all-reduce.114.cloned.1.call-done
  917.3 6.1 collective-permute-start.127
  981.1 9.7 broadcast_in_dim.11
  990.8 17.3 %reshape.97 = f32[48,48,48]{2,1,0:T(8,128)} reshape(f32[24,2,24,2,24,2]{5,4,3,2,1,0:T(8,128)} %broadcast_in_dim.11) | data formatting | bytes 884736 | tf_op jit(solution)/shard_map/reshape | solution.py:134
  1039.3 10.7 multiply_add_fusion
  1082.5 10.8 fusion.744
  1126.0 9.9 fusion.30
  1167.9 12.2 multiply_reduce_fusion.1
  1184.6 10.8 all-reduce.110
  1195.4 19.8 %all-reduce.109 = (f32[]{:T(128)}, f32[]{:T(128)}) all-reduce(f32[]{:T(128)} %get-tuple-element.7, f32[]{:T(128)} %get-tuple-element.8), channel_id=1, replica_groups=mesh['gx'=2,'gy'=4,'gz_0'=4,'gz_1'=4] {'gz_0'}, use_global_device_ids=true, to_apply=%region_35.36 | all-reduce | flops 2 | bytes 16 | tf_op jit(solution)/shard_map/psum | solution.py:45
  1215.2 8.3 all-reduce.108
  (787 shorter events, 795.4 us)
Async XLA Ops:
  7.2 704.2 %all-reduce.114.cloned.1.call-start = ((), (), s32[]{:S(2)}) async-start(), calls=%async_computation | async-start | bytes 196608
  8.5 144.4 %collective-permute-start = (f32[1,48,48]{2,1,0:T(8,128)}, f32[1,48,48]{2,1,0:T(8,128)}, u32[]{:S(2)}, u32[]{:S(2)}) collective-permute-start(f32[1,48,48]{2,1,0:T(8,128)} %slice_bitcast_fusion.13), channel_id=1, source_target_pairs={{64,0},{65,1},{66,2},{67,3},{68,4},{69,5},{70,6},{71,7},{72,8},{73... | collective-permute-start | bytes 27656 | tf_op jit(solution)/shard_map/ppermute | solution.py:40
  11.4 141.6 %collective-permute-start.1 = (f32[48,1,48]{2,1,0:T(1,128)}, f32[48,1,48]{2,1,0:T(1,128)}, u32[]{:S(2)}, u32[]{:S(2)}) collective-permute-start(f32[48,1,48]{2,1,0:T(1,128)} %slice_bitcast_fusion.12), channel_id=1, source_target_pairs={{16,0},{32,16},{48,32},{17,1},{33,17},{49,33},{18,2},{34,18},{50,3... | collective-permute-start | bytes 27656 | tf_op jit(solution)/shard_map/ppermute | solution.py:40
  17.5 133.2 %collective-permute-start.2 = (f32[48,48,1]{1,0,2:T(8,128)}, f32[48,48,1]{1,0,2:T(8,128)}, u32[]{:S(2)}, u32[]{:S(2)}) collective-permute-start(f32[48,48,1]{1,0,2:T(8,128)} %bitcast.326), channel_id=1, source_target_pairs={{1,0},{2,1},{3,2},{4,3},{5,4},{6,5},{7,6},{8,7},{9,8},{10,9},{11,1... | collective-permute-start | bytes 27656 | tf_op jit(solution)/shard_map/ppermute | solution.py:40
  163.5 19.6 %collective-permute-start.7 = (f32[48,48,1]{1,0,2:T(8,128)}, f32[48,48,1]{1,0,2:T(8,128)}, u32[]{:S(2)}, u32[]{:S(2)}) collective-permute-start(f32[48,48,1]{1,0,2:T(8,128)} %copy.152), channel_id=1, source_target_pairs={{0,1},{1,2},{2,3},{3,4},{4,5},{5,6},{6,7},{7,8},{8,9},{9,10},{10,1... | collective-permute-start | bytes 27656 | tf_op jit(solution)/shard_map/ppermute | solution.py:25
  250.8 18.6 %collective-permute-start.22 = (f32[48,48,1]{1,0,2:T(8,128)}, f32[48,48,1]{1,0,2:T(8,128)}, u32[]{:S(2)}, u32[]{:S(2)}) collective-permute-start(f32[48,48,1]{1,0,2:T(8,128)} %copy.162), channel_id=1, source_target_pairs={{0,1},{1,2},{2,3},{3,4},{4,5},{5,6},{6,7},{7,8},{8,9},{9,10},{10,1... | collective-permute-start | bytes 27656 | tf_op jit(solution)/shard_map/ppermute | solution.py:25
  259.6 51.6 %collective-permute-start.23 = (f32[48,48,1]{1,0,2:T(8,128)}, f32[48,48,1]{1,0,2:T(8,128)}, u32[]{:S(2)}, u32[]{:S(2)}) collective-permute-start(f32[48,48,1]{1,0,2:T(8,128)} %copy.164), channel_id=1, source_target_pairs={{1,0},{2,1},{3,2},{4,3},{5,4},{6,5},{7,6},{8,7},{9,8},{10,9},{11,1... | collective-permute-start | bytes 27656 | tf_op jit(solution)/shard_map/ppermute | solution.py:25
  261.0 53.6 %collective-permute-start.20 = (f32[48,1,48]{2,1,0:T(1,128)}, f32[48,1,48]{2,1,0:T(1,128)}, u32[]{:S(2)}, u32[]{:S(2)}) collective-permute-start(f32[48,1,48]{2,1,0:T(1,128)} %get-tuple-element.104), channel_id=1, source_target_pairs={{0,16},{16,32},{32,48},{1,17},{17,33},{33,49},{2,18},{18,34},{34,5... | collective-permute-start | bytes 27656 | tf_op jit(solution)/shard_map/ppermute | solution.py:25
  266.2 50.5 %collective-permute-start.21 = (f32[48,1,48]{2,1,0:T(1,128)}, f32[48,1,48]{2,1,0:T(1,128)}, u32[]{:S(2)}, u32[]{:S(2)}) collective-permute-start(f32[48,1,48]{2,1,0:T(1,128)} %get-tuple-element.105), channel_id=1, source_target_pairs={{16,0},{32,16},{48,32},{17,1},{33,17},{49,33},{18,2},{34,18},{50,3... | collective-permute-start | bytes 27656 | tf_op jit(solution)/shard_map/ppermute | solution.py:25
  267.5 51.3 %collective-permute-start.18 = (f32[1,48,48]{2,1,0:T(8,128)}, f32[1,48,48]{2,1,0:T(8,128)}, u32[]{:S(2)}, u32[]{:S(2)}) collective-permute-start(f32[1,48,48]{2,1,0:T(8,128)} %get-tuple-element.102), channel_id=1, source_target_pairs={{0,64},{1,65},{2,66},{3,67},{4,68},{5,69},{6,70},{7,71},{8,72},{9,... | collective-permute-start | bytes 27656 | tf_op jit(solution)/shard_map/ppermute | solution.py:25
  269.4 50.7 %collective-permute-start.19 = (f32[1,48,48]{2,1,0:T(8,128)}, f32[1,48,48]{2,1,0:T(8,128)}, u32[]{:S(2)}, u32[]{:S(2)}) collective-permute-start(f32[1,48,48]{2,1,0:T(8,128)} %get-tuple-element.103), channel_id=1, source_target_pairs={{64,0},{65,1},{66,2},{67,3},{68,4},{69,5},{70,6},{71,7},{72,8},{73... | collective-permute-start | bytes 27656 | tf_op jit(solution)/shard_map/ppermute | solution.py:25
  311.2 61.7 %collective-permute-start.84 = (f32[1,3,3]{2,0,1:T(1,128)}, f32[1,3,3]{2,0,1:T(1,128)S(1)}, u32[]{:S(2)}, u32[]{:S(2)}) collective-permute-start(f32[1,3,3]{2,0,1:T(1,128)} %squeeze.183), channel_id=1, source_target_pairs={{64,0},{65,1},{66,2},{67,3},{68,4},{69,5},{70,6},{71,7},{72,8},{73... | collective-permute-start | bytes 116 | tf_op jit(solution)/shard_map/ppermute | solution.py:40
  314.7 42.3 %collective-permute-start.15 = (f32[1,24,24]{2,1,0:T(8,128)}, f32[1,24,24]{2,1,0:T(8,128)S(1)}, u32[]{:S(2)}, u32[]{:S(2)}) collective-permute-start(f32[1,24,24]{2,1,0:T(8,128)} %slice_bitcast_fusion.16), channel_id=1, source_target_pairs={{64,0},{65,1},{66,2},{67,3},{68,4},{69,5},{70,6},{71,7},{72,8},{73... | collective-permute-start | bytes 6920 | tf_op jit(solution)/shard_map/ppermute | solution.py:40
  316.7 40.2 %collective-permute-start.16 = (f32[24,1,24]{2,1,0:T(1,128)}, f32[24,1,24]{2,1,0:T(1,128)}, u32[]{:S(2)}, u32[]{:S(2)}) collective-permute-start(f32[24,1,24]{2,1,0:T(1,128)} %slice_bitcast_fusion.15), channel_id=1, source_target_pairs={{16,0},{32,16},{48,32},{17,1},{33,17},{49,33},{18,2},{34,18},{50,3... | collective-permute-start | bytes 6920 | tf_op jit(solution)/shard_map/ppermute | solution.py:40
  318.8 38.2 %collective-permute-start.17 = (f32[24,24,1]{2,1,0:T(8,128)}, f32[24,24,1]{2,1,0:T(8,128)}, u32[]{:S(2)}, u32[]{:S(2)}) collective-permute-start(f32[24,24,1]{2,1,0:T(8,128)} %slice_bitcast_fusion.3), channel_id=1, source_target_pairs={{1,0},{2,1},{3,2},{4,3},{5,4},{6,5},{7,6},{8,7},{9,8},{10,9},{11,1... | collective-permute-start | bytes 6920 | tf_op jit(solution)/shard_map/ppermute | solution.py:40
  401.5 21.5 %collective-permute-start.86 = (f32[3,3,1]{1,2,0:T(1,128)S(1)}, f32[3,3,1]{1,2,0:T(1,128)S(1)}, u32[]{:S(2)}, u32[]{:S(2)}) collective-permute-start(f32[3,3,1]{1,2,0:T(1,128)S(1)} %copy-done.72), channel_id=1, source_target_pairs={{1,0},{2,1},{3,2},{4,3},{5,4},{6,5},{7,6},{8,7},{9,8},{10,9},{11,1... | collective-permute-start | bytes 116 | tf_op jit(solution)/shard_map/ppermute | solution.py:40
  402.8 21.5 %collective-permute-start.38 = (f32[12,12,1]{1,2,0:T(1,128)S(1)}, f32[12,12,1]{1,2,0:T(1,128)S(1)}, u32[]{:S(2)}, u32[]{:S(2)}) collective-permute-start(f32[12,12,1]{1,2,0:T(1,128)S(1)} %copy-done.68), channel_id=1, source_target_pairs={{1,0},{2,1},{3,2},{4,3},{5,4},{6,5},{7,6},{8,7},{9,8},{10,9},{11,1... | collective-permute-start | bytes 1736 | tf_op jit(solution)/shard_map/ppermute | solution.py:40
  414.8 25.2 %collective-permute-start.43 = (f32[24,24,1]{2,1,0:T(8,128)}, f32[24,24,1]{2,1,0:T(8,128)}, u32[]{:S(2)}, u32[]{:S(2)}) collective-permute-start(f32[24,24,1]{2,1,0:T(8,128)} %get-tuple-element.143), channel_id=1, source_target_pairs={{0,1},{1,2},{2,3},{3,4},{4,5},{5,6},{6,7},{7,8},{8,9},{9,10},{10,1... | collective-permute-start | bytes 6920 | tf_op jit(solution)/shard_map/ppermute | solution.py:25
  421.7 19.6 %collective-permute-start.44 = (f32[24,24,1]{2,1,0:T(8,128)}, f32[24,24,1]{2,1,0:T(8,128)}, u32[]{:S(2)}, u32[]{:S(2)}) collective-permute-start(f32[24,24,1]{2,1,0:T(8,128)} %get-tuple-element.144), channel_id=1, source_target_pairs={{1,0},{2,1},{3,2},{4,3},{5,4},{6,5},{7,6},{8,7},{9,8},{10,9},{11,1... | collective-permute-start | bytes 6920 | tf_op jit(solution)/shard_map/ppermute | solution.py:25
  424.3 18.5 %collective-permute-start.39 = (f32[1,24,24]{2,1,0:T(8,128)}, f32[1,24,24]{2,1,0:T(8,128)}, u32[]{:S(2)}, u32[]{:S(2)}) collective-permute-start(f32[1,24,24]{2,1,0:T(8,128)} %get-tuple-element.145), channel_id=1, source_target_pairs={{0,64},{1,65},{2,66},{3,67},{4,68},{5,69},{6,70},{7,71},{8,72},{9,... | collective-permute-start | bytes 6920 | tf_op jit(solution)/shard_map/ppermute | solution.py:25
  438.0 35.7 %collective-permute-start.85 = (f32[3,1,3]{2,1,0:T(1,128)}, f32[3,1,3]{2,1,0:T(1,128)}, u32[]{:S(2)}, u32[]{:S(2)}) collective-permute-start(f32[3,1,3]{2,1,0:T(1,128)} %slice_bitcast_fusion.21), channel_id=1, source_target_pairs={{16,0},{32,16},{48,32},{17,1},{33,17},{49,33},{18,2},{34,18},{50,3... | collective-permute-start | bytes 116 | tf_op jit(solution)/shard_map/ppermute | solution.py:40
  457.8 20.1 %collective-permute-start.47 = (f32[12,1,12]{2,1,0:T(1,128)S(1)}, f32[12,1,12]{2,1,0:T(1,128)}, u32[]{:S(2)}, u32[]{:S(2)}) collective-permute-start(f32[12,1,12]{2,1,0:T(1,128)S(1)} %get-tuple-element.194), channel_id=1, source_target_pairs={{0,16},{16,32},{32,48},{1,17},{17,33},{33,49},{2,18},{18,34},{34,5... | collective-permute-start | bytes 1736 | tf_op jit(solution)/shard_map/ppermute | solution.py:25
  464.8 19.9 %collective-permute-start.49 = (f32[12,12,1]{2,1,0:T(8,128)}, f32[12,12,1]{2,1,0:T(8,128)}, u32[]{:S(2)}, u32[]{:S(2)}) collective-permute-start(f32[12,12,1]{2,1,0:T(8,128)} %get-tuple-element.192), channel_id=1, source_target_pairs={{0,1},{1,2},{2,3},{3,4},{4,5},{5,6},{6,7},{7,8},{8,9},{9,10},{10,1... | collective-permute-start | bytes 1736 | tf_op jit(solution)/shard_map/ppermute | solution.py:25
  502.7 19.1 %collective-permute-start.59 = (f32[6,6,1]{1,2,0:T(1,128)}, f32[6,6,1]{1,2,0:T(1,128)S(1)}, u32[]{:S(2)}, u32[]{:S(2)}) collective-permute-start(f32[6,6,1]{1,2,0:T(1,128)} %squeeze.181), channel_id=1, source_target_pairs={{1,0},{2,1},{3,2},{4,3},{5,4},{6,5},{7,6},{8,7},{9,8},{10,9},{11,1... | collective-permute-start | bytes 440 | tf_op jit(solution)/shard_map/ppermute | solution.py:40
  506.5 18.4 %collective-permute-start.62 = (f32[12,1,12]{2,1,0:T(1,128)S(1)}, f32[12,1,12]{2,1,0:T(1,128)}, u32[]{:S(2)}, u32[]{:S(2)}) collective-permute-start(f32[12,1,12]{2,1,0:T(1,128)S(1)} %get-tuple-element.184), channel_id=1, source_target_pairs={{0,16},{16,32},{32,48},{1,17},{17,33},{33,49},{2,18},{18,34},{34,5... | collective-permute-start | bytes 1736 | tf_op jit(solution)/shard_map/ppermute | solution.py:25
  511.9 22.0 %collective-permute-start.64 = (f32[12,12,1]{2,1,0:T(8,128)}, f32[12,12,1]{2,1,0:T(8,128)}, u32[]{:S(2)}, u32[]{:S(2)}) collective-permute-start(f32[12,12,1]{2,1,0:T(8,128)} %get-tuple-element.180), channel_id=1, source_target_pairs={{0,1},{1,2},{2,3},{3,4},{4,5},{5,6},{6,7},{7,8},{8,9},{9,10},{10,1... | collective-permute-start | bytes 1736 | tf_op jit(solution)/shard_map/ppermute | solution.py:25
  551.6 17.7 %collective-permute-start.70 = (f32[6,6,1]{2,1,0:T(8,128)}, f32[6,6,1]{2,1,0:T(8,128)S(1)}, u32[]{:S(2)}, u32[]{:S(2)}) collective-permute-start(f32[6,6,1]{2,1,0:T(8,128)} %get-tuple-element.232), channel_id=1, source_target_pairs={{0,1},{1,2},{2,3},{3,4},{4,5},{5,6},{6,7},{7,8},{8,9},{9,10},{10,1... | collective-permute-start | bytes 440 | tf_op jit(solution)/shard_map/ppermute | solution.py:25
  572.6 17.7 %collective-permute-start.76 = (f32[6,6,1]{2,1,0:T(8,128)S(1)}, f32[6,6,1]{2,1,0:T(8,128)S(1)}, u32[]{:S(2)}, u32[]{:S(2)}) collective-permute-start(f32[6,6,1]{2,1,0:T(8,128)S(1)} %get-tuple-element.226), channel_id=1, source_target_pairs={{0,1},{1,2},{2,3},{3,4},{4,5},{5,6},{6,7},{7,8},{8,9},{9,10},{10,1... | collective-permute-start | bytes 440 | tf_op jit(solution)/shard_map/ppermute | solution.py:25
  591.6 18.0 %collective-permute-start.82 = (f32[6,6,1]{2,1,0:T(8,128)S(1)}, f32[6,6,1]{2,1,0:T(8,128)S(1)}, u32[]{:S(2)}, u32[]{:S(2)}) collective-permute-start(f32[6,6,1]{2,1,0:T(8,128)S(1)} %get-tuple-element.220), channel_id=1, source_target_pairs={{0,1},{1,2},{2,3},{3,4},{4,5},{5,6},{6,7},{7,8},{8,9},{9,10},{10,1... | collective-permute-start | bytes 440 | tf_op jit(solution)/shard_map/ppermute | solution.py:25
  1054.8 20.4 %collective-permute-start.151 = (f32[48,48,1]{1,0,2:T(8,128)}, f32[48,48,1]{1,0,2:T(8,128)}, u32[]{:S(2)}, u32[]{:S(2)}) collective-permute-start(f32[48,48,1]{1,0,2:T(8,128)} %copy.185), channel_id=1, source_target_pairs={{0,1},{1,2},{2,3},{3,4},{4,5},{5,6},{6,7},{7,8},{8,9},{9,10},{10,1... | collective-permute-start | bytes 27656 | tf_op jit(solution)/shard_map/ppermute | solution.py:25
  1098.1 20.6 %collective-permute-start.157 = (f32[48,48,1]{1,0,2:T(8,128)}, f32[48,48,1]{1,0,2:T(8,128)}, u32[]{:S(2)}, u32[]{:S(2)}) collective-permute-start(f32[48,48,1]{1,0,2:T(8,128)} %copy.189), channel_id=1, source_target_pairs={{0,1},{1,2},{2,3},{3,4},{4,5},{5,6},{6,7},{7,8},{8,9},{9,10},{10,1... | collective-permute-start | bytes 27656 | tf_op jit(solution)/shard_map/ppermute | solution.py:25
  1140.6 19.7 %collective-permute-start.163 = (f32[48,48,1]{1,0,2:T(8,128)}, f32[48,48,1]{1,0,2:T(8,128)}, u32[]{:S(2)}, u32[]{:S(2)}) collective-permute-start(f32[48,48,1]{1,0,2:T(8,128)} %copy.193), channel_id=1, source_target_pairs={{0,1},{1,2},{2,3},{3,4},{4,5},{5,6},{6,7},{7,8},{8,9},{9,10},{10,1... | collective-permute-start | bytes 27656 | tf_op jit(solution)/shard_map/ppermute | solution.py:25
  (207 other events, 2724.8 us)
Sparse Core Ops, SparseCore 0:
  551.7 159.6 all-reduce.113
where the time goes:
time: 1260 us; the launch traced here: 1230 us
  starting transfers between devices  423 us (34%)
  local copies, waits for them, and re-layouts  370 us (29%)
  other arithmetic  232 us (18%)
  blocking collectives  122 us (10%)
  waiting for transfers between devices  52 us (4%)
  between operations  34.9 us (3%)
    ppermute x75, starting transfers between devices, with_halo(): lax.ppermute(last, axis, up)  306 us
    ppermute x75, starting transfers between devices, with_halo(): lax.ppermute(leading, axis, [(b, a) for a, b in up])  97.2 us
    unnamed x1, blocking collectives  78.8 us
    add x20, other arithmetic, chebyshev(): iterate = iterate + update  70.6 us
    slice x82, local copies, waits for them, and re-layouts, with_halo(): last = lax.slice_in_dim(value, length - width, length, axis=dim)  52.3 us
    ppermute x75, waiting for transfers between devices, with_halo(): lax.ppermute(leading, axis, [(b, a) for a, b in up])  44.9 us
    psum x4, blocking collectives, over_axes(): value = lax.psum(value, axis)  43.5 us
    reshape x5, local copies, waits for them, and re-layouts, average_cells(): field.reshape(field.shape[0] // 2, 2, field.shape[1] // 2, 2, field.shape...  38.3 us
  transfers between devices with their start and end apart: 166, of which 26 were waited for; matrix products, arithmetic and copies ran while one was open for 29% of the time, Pallas kernels for 0%

commit v1 on v0

v1 whole, which is shorter than its diff:
```python
import functools

import jax
import jax.numpy as jnp
from jax import lax
from jax.experimental import pallas as pl
from jax.experimental.pallas import tpu as pltpu
from jax.sharding import PartitionSpec as P

BOTTOM = 6
THETA = 1.125
DELTA = 0.875
SIGMA = THETA / DELTA
RHO0 = 1.0 / SIGMA
RHO1 = 1.0 / (2.0 * SIGMA - RHO0)
RHO2 = 1.0 / (2.0 * SIGMA - RHO1)
STEP1 = (RHO1 * RHO0, 2.0 * RHO1 / DELTA)
STEP2 = (RHO2 * RHO1, 2.0 * RHO2 / DELTA)

F32 = jnp.float32
MESH = pl.DeviceIdType.MESH


class Level:
    def __init__(self, n, e, ways, rows, zo, width, pack_rows):
        self.n, self.e, self.ways, self.rows, self.zo, self.width, self.ep = n, e, ways, rows, zo, width, pack_rows
        self.half = n // ways
        self.planes = self.half + 2 * e
        self.span = 128 // ways
        self.slots = self.span // width
        self.packs = -(-self.planes // self.slots)


L0 = Level(48, 4, 2, 56, 8, 4, 4)
L1 = Level(24, 8, 2, 40, 16, 8, 8)
L2 = Level(12, 9, 1, 32, 16, 16, 16)


def lanes(rows):
    return lax.broadcasted_iota(jnp.int32, (rows, 128), 1)


def gather_lanes(value, index):
    return jnp.take_along_axis(value, index, axis=1)


def roll_lanes(value, shift):
    return pltpu.roll(value, shift % 128, 1)


def roll_rows(value, shift):
    return pltpu.roll(value, shift % value.shape[0], 0)


def tile_rows(start, size):
    return pl.ds(pl.multiple_of(start, 8), size)


class Exchange:
    def __init__(self, level, first, count):
        self.level, self.first, self.count = level, first, count

    def scratch(self):
        lv, na = self.level, self.count
        shapes = [
            (na, lv.e * lv.rows, 128),
            (2, na, lv.planes * lv.ep, 128),
            (2, na, lv.planes * lv.ep, 128),
            (2, na, lv.packs * lv.rows, 128),
            (2, na, lv.packs * lv.rows, 128),
            (2, 2, na, lv.packs * lv.ep, 128),
            (2, 2, na, lv.packs * lv.ep, 128),
        ]
        return [pltpu.VMEM(s, F32) for s in shapes] + [pltpu.SemaphoreType.DMA((9,)), pltpu.SemaphoreType.DMA((9,))]

    def bind(self, here, ref, scratch):
        self.here, self.ref = here, ref
        self.xr, self.yb, self.yr, self.zb, self.zr, self.db, self.dr, self.ssem, self.rsem = scratch
        gx, gy, gz, ny, nz = here
        lv = self.level
        e, r = lv.e, lv.rows
        start = e + (1 - gx) * (lv.half - e) if lv.ways == 2 else e + (1 - gx) * (lv.n - e)
        src = ref.at[pl.ds(self.first, self.count), tile_rows(start * r, e * r), :]
        self.copies = []

        def add(src, dst, gx, gy, gz):
            i = len(self.copies)
            self.copies.append(
                pltpu.make_async_remote_copy(
                    src_ref=src,
                    dst_ref=dst,
                    send_sem=self.ssem.at[i],
                    recv_sem=self.rsem.at[i],
                    device_id=(gx, gy, gz),
                    device_id_type=MESH,
                )
            )

        add(src, self.xr, 1 - gx, gy, gz)
        ys = [lax.rem(gy + ny - 1, ny), lax.rem(gy + 1, ny)]
        zs = [lax.rem(gz + nz - 1, nz), lax.rem(gz + 1, nz)]
        for s in range(2):
            add(self.yb.at[s], self.yr.at[1 - s], gx, ys[s], gz)
        for s in range(2):
            for t in range(2):
                add(self.db.at[s, t], self.dr.at[1 - s, 1 - t], gx, ys[s], zs[t])
        for t in range(2):
            add(self.zb.at[t], self.zr.at[1 - t], gx, gy, zs[t])
        self.has_y = [jnp.where(gy > 0, 1.0, 0.0).astype(F32), jnp.where(gy < ny - 1, 1.0, 0.0).astype(F32)]
        self.has_z = [jnp.where(gz > 0, 1.0, 0.0).astype(F32), jnp.where(gz < nz - 1, 1.0, 0.0).astype(F32)]
        self.has_x = [gx.astype(F32), (1 - gx).astype(F32)]
        return self

    def start_x(self):
        self.copies[0].start()

    def finish_x(self):
        lv, ref = self.level, self.ref
        e, r = lv.e, lv.rows
        self.copies[0].wait()
        low = lanes(r) < 64

        def body(i, carry):
            a, j = i // e, i % e
            got = self.xr[a, tile_rows(j * r, r), :]
            if lv.ways == 2:
                got = roll_lanes(got, 64)
                below = roll_lanes(ref[self.first + a, tile_rows((lv.half + j) * r, r), :], 64)
                above = roll_lanes(ref[self.first + a, tile_rows((e + j) * r, r), :], 64)
                below = jnp.where(low, got * self.has_x[0], below)
                above = jnp.where(low, above, got * self.has_x[1])
            else:
                below = got * self.has_x[0]
                above = got * self.has_x[1]
            ref[self.first + a, tile_rows(j * r, r), :] = below
            ref[self.first + a, tile_rows((e + lv.half + j) * r, r), :] = above
            return carry

        lax.fori_loop(0, self.count * e, body, 0)

    def pack(self, ref, rows, out, lead):
        lv = self.level
        slot = (lanes(rows) % lv.span) // lv.width
        shifts = (lv.zo, lv.zo + lv.n - lv.e)
        for k in range(lv.packs):
            acc = [jnp.zeros((rows, 128), F32)] * 2
            for s in range(min(lv.slots, lv.planes - k * lv.slots)):
                plane = ref((k * lv.slots + s) * rows, rows)
                for t in range(2):
                    acc[t] = jnp.where(slot == s, roll_lanes(plane, s * lv.width - shifts[t]), acc[t])
            for t in range(2):
                lead(t, k * rows, acc[t])

    def start_yz(self):
        lv, ref = self.level, self.ref
        r, ep, e = lv.rows, lv.ep, lv.e

        def pack_y(a, carry):
            for p in range(lv.planes):
                self.yb[0, a, pl.ds(p * ep, e), :] = ref[self.first + a, pl.ds(p * r + e, e), :]
                self.yb[1, a, pl.ds(p * ep, e), :] = ref[self.first + a, pl.ds(p * r + lv.n, e), :]
            return carry

        lax.fori_loop(0, self.count, pack_y, 0)
        self.copies[1].start()
        self.copies[2].start()

        def pack_z(a, carry):
            def put(t, row, value):
                self.zb[t, a, pl.ds(row, r), :] = value

            self.pack(lambda row, rows: ref[self.first + a, pl.ds(row, rows), :], r, self.zb, put)
            return carry

        lax.fori_loop(0, self.count, pack_z, 0)
        self.copies[7].start()
        self.copies[8].start()

        def pack_d(i, carry):
            s, a = i // self.count, i % self.count

            def put(t, row, value):
                self.db[s, t, a, pl.ds(row, ep), :] = value

            self.pack(lambda row, rows: self.yb[s, a, pl.ds(row, rows), :], ep, self.db, put)
            return carry

        lax.fori_loop(0, 2 * self.count, pack_d, 0)
        for i in range(3, 7):
            self.copies[i].start()

    def finish_yz(self):
        lv, ref = self.level, self.ref
        r, ep, e = lv.rows, lv.ep, lv.e
        for i in range(1, 9):
            self.copies[i].wait()
        lane = lanes(r) % lv.span
        at_low = (lane >= lv.zo - e) & (lane < lv.zo)
        at_high = (lane >= lv.zo + lv.n) & (lane < lv.zo + lv.n + e)

        def unpack(a, carry):
            for p in range(lv.planes):
                for s in range(2):
                    row = p * r + (e + lv.n) * s
                    ref[self.first + a, pl.ds(row, e), :] = self.yr[s, a, pl.ds(p * ep, e), :] * self.has_y[s]
            for k in range(lv.packs):
                for t in range(2):
                    self.zr[t, a, pl.ds(k * r, r), :] = self.zr[t, a, pl.ds(k * r, r), :] * self.has_z[t]
                    for s in range(2):
                        row = k * r + (e + lv.n) * s
                        both = self.has_y[s] * self.has_z[t]
                        self.zr[t, a, pl.ds(row, e), :] = self.dr[s, t, a, pl.ds(k * ep, e), :] * both
            for k in range(lv.packs):
                got = [self.zr[t, a, pl.ds(k * r, r), :] for t in range(2)]
                for s in range(min(lv.slots, lv.planes - k * lv.slots)):
                    p = k * lv.slots + s
                    value = ref[self.first + a, pl.ds(p * r, r), :]
                    value = jnp.where(at_low, roll_lanes(got[0], lv.zo - e - s * lv.width), value)
                    value = jnp.where(at_high, roll_lanes(got[1], lv.zo + lv.n - s * lv.width), value)
                    ref[self.first + a, pl.ds(p * r, r), :] = value
            return carry

        lax.fori_loop(0, self.count, unpack, 0)


def scaling(lv, fields, inverse, extent):
    r = lv.rows

    def body(p, carry):
        row = pl.multiple_of(p * r, 8)
        cells = fields[3, pl.ds(row, r), :]
        face_z = fields[2, pl.ds(row, r), :]
        total = cells + fields[0, pl.ds(row, r), :] + fields[0, pl.ds(row + r, r), :]
        total = total + fields[1, pl.ds(row, r), :] + fields[1, pl.ds(row + 1, r), :]
        total = total + face_z + roll_lanes(face_z, -1)
        inverse[0, pl.ds(row, r), :] = jnp.where(cells > 0.0, 1.0 / total, 0.0)
        return carry

    lax.fori_loop(lv.e - extent, lv.e + lv.half + extent, body, 0, unroll=2)


def sweep(lv, fields, x, extent, emit):
    r = lv.rows
    lo, hi = lv.e - extent, lv.e + lv.half + extent

    def body(p, carry):
        here, flux = carry
        row = pl.multiple_of(p * r, 8)
        after = x[0, pl.ds(row + r, r), :]
        flux_after = fields[0, pl.ds(row + r, r), :] * (after - here)
        low_y = x[0, pl.ds(row - 1, r), :]
        high_y = x[0, pl.ds(row + 1, r), :]
        flux_y = fields[1, pl.ds(row, r), :] * (here - low_y)
        flux_y = flux_y - fields[1, pl.ds(row + 1, r), :] * (high_y - here)
        flux_z = fields[2, pl.ds(row, r), :] * (here - roll_lanes(here, 1))
        flux_z = flux_z - roll_lanes(flux_z, -1)
        applied = fields[3, pl.ds(row, r), :] * here + ((flux - flux_after) + flux_y + flux_z)
        emit(p, row, here, applied)
        return after, flux_after

    row = lo * r
    here = x[0, pl.ds(row, r), :]
    flux = fields[0, pl.ds(row, r), :] * (here - x[0, pl.ds(row - r, r), :])
    lax.fori_loop(lo, hi, body, (here, flux), unroll=2)


def step(lv, fields, inverse, x, out, d, extent, first, coefs, keep):
    r = lv.rows

    def emit(p, row, here, applied):
        scaled = inverse[0, pl.ds(row, r), :] * (fields[4, pl.ds(row, r), :] - applied)
        if first == 0:
            update = scaled * (1.0 / THETA)
        elif first == 1:
            update = coefs[0] * here + coefs[1] * scaled
        else:
            update = coefs[0] * d[0, pl.ds(row, r), :] + coefs[1] * scaled
        if keep:
            d[0, pl.ds(row, r), :] = update
        out[0, pl.ds(row, r), :] = here + update

    sweep(lv, fields, x, extent, emit)


def smooth_from_zero(lv, fields, inverse, xa, xb, d, extent):
    r = lv.rows

    def body(p, carry):
        row = pl.multiple_of(p * r, 8)
        xa[0, pl.ds(row, r), :] = inverse[0, pl.ds(row, r), :] * fields[4, pl.ds(row, r), :] * (1.0 / THETA)
        return carry

    lax.fori_loop(lv.e - extent, lv.e + lv.half + extent, body, 0, unroll=2)
    step(lv, fields, inverse, xa, xb, d, extent - 1, 1, STEP1, True)
    step(lv, fields, inverse, xb, xa, d, extent - 2, 2, STEP2, False)


def smooth(lv, fields, inverse, xa, xb, d, extent):
    step(lv, fields, inverse, xa, xb, d, extent - 1, 0, None, True)
    step(lv, fields, inverse, xb, xa, d, extent - 2, 2, STEP1, True)
    step(lv, fields, inverse, xa, xb, d, extent - 3, 2, STEP2, False)


def coarse_lanes(lv, below, rows, half):
    lane = lanes(rows)
    if below is None:
        cell, at = lane, 0
    else:
        at = (lane // below.span) * 64 if below.ways == 2 else 0
        cell = lane % below.span - below.zo
    if lv.ways == 2 and half is not None:
        at = 64 * half
    inside = (cell >= 0) & (cell < lv.n // 2)
    index = jnp.where(inside, at + lv.zo + 2 * cell, 0)
    return index, inside


def place(lv, below, put, plane, value, pair):
    rows = value.shape[0]
    if pair:
        value = value + roll_lanes(value, -1)
    halves = [None] if below is not None and below.ways == lv.ways else range(lv.ways)
    for half in halves:
        index, inside = coarse_lanes(lv, below, rows, half)
        got = jnp.where(inside, gather_lanes(value, index), 0.0)
        put(plane if half is None else plane + half * (lv.half // 2), got)


def coarsen_fields(lv, below, fields, put):
    n2, e, r = lv.n // 2, lv.e, lv.rows

    def body(i, carry):
        row = (e + 2 * i) * r + e

        def rows(a, plane, odd):
            return fields[a, pl.ds(row + plane * r + odd, n2, stride=2), :]

        put_x = functools.partial(put, 0)
        put_y = functools.partial(put, 1)
        put_z = functools.partial(put, 2)
        put_c = functools.partial(put, 3)
        place(lv, below, put_x, i, (rows(0, 0, 0) + rows(0, 0, 1)) * 0.0625, True)
        place(lv, below, put_y, i, (rows(1, 0, 0) + rows(1, 1, 0)) * 0.0625, True)
        place(lv, below, put_z, i, (rows(2, 0, 0) + rows(2, 0, 1) + rows(2, 1, 0) + rows(2, 1, 1)) * 0.0625, False)
        place(lv, below, put_c, i, (rows(3, 0, 0) + rows(3, 0, 1) + rows(3, 1, 0) + rows(3, 1, 1)) * 0.125, True)
        return carry

    lax.fori_loop(0, lv.half // 2, body, 0)


def restrict(lv, below, fields, x, sums, put):
    r, n2 = lv.rows, lv.n // 2

    def emit(p, row, here, applied):
        sums[0, pl.ds((p - lv.e) * r, r), :] = fields[4, pl.ds(row, r), :] - applied

    sweep(lv, fields, x, 0, emit)

    def body(i, carry):
        total = None
        for plane in range(2):
            for odd in range(2):
                part = sums[0, pl.ds((2 * i + plane) * r + lv.e + odd, n2, stride=2), :]
                total = part if total is None else total + part
        place(lv, below, functools.partial(put, 4), i, total * 0.125, True)
        return carry

    lax.fori_loop(0, lv.half // 2, body, 0)


def fields_put(below, fields):
    def put(field, plane, value):
        fields[field, pl.ds((below.e + plane) * below.rows + below.e, below.n), :] = value

    return put


def prolong(lv, above, e, x, reach):
    r, rows = lv.rows, lv.n // 2 + 2 * reach
    lane = lanes(rows)
    cell = lane % 64 - lv.zo + 2 * reach
    inside = (cell >= 0) & (cell < 2 * rows)
    source = above.zo - reach + cell // 2
    if above.ways == 2:
        source = source + (lane // 64) * 64
    source = jnp.where(inside, source, 0)

    def body(i, carry):
        row = (above.e - reach + i) * above.rows + above.e - reach
        value = gather_lanes(e[0, pl.ds(row, rows), :], source)
        if above.ways == 1:
            other = gather_lanes(e[0, pl.ds(row + (lv.half // 2) * above.rows, rows), :], source)
            value = jnp.where(lane < 64, value, other)
        value = jnp.where(inside, value, 0.0)
        for plane in range(2):
            at = (lv.e - 2 * reach + 2 * i + plane) * r + lv.e - 2 * reach
            for odd in range(2):
                where = pl.ds(at + odd, rows, stride=2)
                x[0, where, :] = x[0, where, :] + value
        return carry

    lax.fori_loop(0, lv.half // 2 + 2 * reach, body, 0)


def whole_operator(ny, fields, v, scale):
    rows = lax.broadcasted_iota(jnp.int32, (128, 128), 0)
    z, y = rows % 8, lanes(128) % 6
    last = 6 - scale
    y_low, y_high, z_low, z_high = y == 0, y == last, z == 0, z == last
    bottom, top = rows == 0, rows == 120 + last
    zero = jnp.zeros((128, 128), F32)

    def below_y(g):
        other = roll_lanes(v[g - 1], -last) if g else zero
        return jnp.where(y_low, other, roll_lanes(v[g], scale))

    fluxes_y = [fields(1, g) * (v[g] - below_y(g)) for g in range(ny)]
    out = []
    for g in range(ny):
        flux = fields(0, g) * (v[g] - roll_lanes(v[g], 6 * scale))
        total = flux - roll_lanes(flux, -6 * scale)
        other = roll_lanes(fluxes_y[g + 1], last) if g + 1 < ny else zero
        total = total + (fluxes_y[g] - jnp.where(y_high, other, roll_lanes(fluxes_y[g], -scale)))
        jump = 8 - last
        other = jnp.where(bottom, 0.0, roll_rows(v[g], jump))
        flux = fields(2, g) * (v[g] - jnp.where(z_low, other, roll_rows(v[g], scale)))
        other = jnp.where(top, 0.0, roll_rows(flux, -jump))
        total = total + (flux - jnp.where(z_high, other, roll_rows(flux, -scale)))
        out.append(fields(3, g) * v[g] + total)
    return out


def whole_inverse(ny, fields):
    rows = lax.broadcasted_iota(jnp.int32, (128, 128), 0)
    z, y = rows % 8, lanes(128) % 6
    zero = jnp.zeros((128, 128), F32)
    out = []
    for g in range(ny):
        face_x, face_y, face_z, cells = (fields(a, g) for a in range(4))
        total = cells + face_x + roll_lanes(face_x, -6)
        other = roll_lanes(fields(1, g + 1), 5) if g + 1 < ny else zero
        total = total + face_y + jnp.where(y == 5, other, roll_lanes(face_y, -1))
        other = jnp.where(rows == 125, 0.0, roll_rows(face_z, -3))
        total = total + face_z + jnp.where(z == 5, other, roll_rows(face_z, -1))
        out.append(jnp.where(cells > 0.0, 1.0 / total, 0.0))
    return out


def children(value, axes):
    if "y" in axes:
        value = value + roll_lanes(value, -1)
    if "x" in axes:
        value = value + roll_lanes(value, -6)
    if "z" in axes:
        value = value + roll_rows(value, -1)
    return value


def coarse_solve(ny, gathered, source, inverse, bottom, xs, ds):
    nz = 16
    fields = lambda a, g: gathered[g, :, a].reshape(128, 128)
    f = lambda g: source[g].reshape(128, 128)

    def load(ref):
        return [ref[g] for g in range(ny)]

    def residual(v):
        applied = whole_operator(ny, fields, v, 1)
        return [f(g) - applied[g] for g in range(ny)]

    for g in range(ny):
        xs[g] = inverse[g] * f(g) * (1.0 / THETA)
        ds[g] = xs[g]
    for coefs in (STEP1, STEP2):
        remainder = residual(load(xs))
        for g in range(ny):
            update = coefs[0] * ds[g] + coefs[1] * (inverse[g] * remainder[g])
            ds[g] = update
            xs[g] = xs[g] + update
    remainder = residual(load(xs))
    inside = lambda g, value: jnp.where(bottom[3, g] > 0.0, value, 0.0)
    r = [inside(g, children(remainder[g], "xyz") * 0.125) for g in range(ny)]

    def total(values):
        values = functools.reduce(lambda a, b: a + b, values)
        return jnp.sum(jnp.sum(values, axis=0, keepdims=True), axis=1, keepdims=True)

    coarse = lambda a, g: bottom[a, g]
    e = [jnp.zeros((128, 128), F32)] * ny
    norm = total([a * a for a in r])

    def body(i, carry):
        e, r, p, norm = carry
        q = [inside(g, a) for g, a in enumerate(whole_operator(ny, coarse, p, 2))]
        size = norm / total([a * b for a, b in zip(p, q)])
        e = [a + size * b for a, b in zip(e, p)]
        r = [a - size * b for a, b in zip(r, q)]
        after = total([a * a for a in r])
        p = [a + after / norm * b for a, b in zip(r, p)]
        return e, r, p, after

    e, r, p, norm = lax.fori_loop(0, BOTTOM - 1, body, (e, r, r, norm))
    q = [inside(g, a) for g, a in enumerate(whole_operator(ny, coarse, p, 2))]
    size = norm / total([a * b for a, b in zip(p, q)])
    for g in range(ny):
        value = e[g] + size * p[g]
        value = value + roll_lanes(value, 1)
        value = value + roll_lanes(value, 6)
        xs[g] = xs[g] + (value + roll_rows(value, 1))
    for number, coefs in enumerate((None, STEP1, STEP2)):
        remainder = residual(load(xs))
        for g in range(ny):
            update = inverse[g] * remainder[g]
            if number == 0:
                update = update * (1.0 / THETA)
            else:
                update = coefs[0] * ds[g] + coefs[1] * update
            ds[g] = update
            xs[g] = xs[g] + update


def coarse_fields(ny, gathered, bottom):
    fields = lambda a, g: gathered[g, :, a].reshape(128, 128)
    rows = lax.broadcasted_iota(jnp.int32, (128, 128), 0)
    lane = lanes(128)
    even = (rows % 2 == 0) & (lane % 2 == 0) & ((lane // 6) % 2 == 0) & (lane < 72)
    for g in range(ny):
        for a, axes in enumerate(("yz", "xz", "xy", "xyz")):
            factor = 0.125 if a == 3 else 0.0625
            bottom[a, g] = jnp.where(even, children(fields(a, g), axes) * factor, 0.0)


def window(lv, gx, gy, gz, ny, xs, padded, turned, corner, x):
    nz = 16
    padded[...] = jnp.zeros_like(padded)
    for g in range(ny):
        padded[g + 1, pl.ds(1, nz)] = xs[g].reshape(nz, 8, 128)
    for dy in range(3):
        tiles = padded[gy + dy, pl.ds(gz, 3)].reshape(24, 128)
        tiles = jnp.concatenate([tiles, jnp.zeros((104, 128), F32)], axis=0)
        turned[dy, pl.ds(0, 24), :] = jnp.zeros((24, 128), F32)
        turned[dy, pl.ds(24, 128), :] = tiles.T
    lane = lanes(16)
    cell = lane - lv.zo + 6
    inside = (cell >= 0) & (cell < 24)
    coarse = jnp.where(inside, cell // 2 + 3, 0)
    source = (coarse // 6) * 8 + coarse % 6

    def body(i, carry):
        base = 6 + 36 * gx + 6 * i
        corner[pl.ds(0, 3), :] = turned[0, pl.ds(base + 3, 3), :]
        corner[pl.ds(3, 6), :] = turned[1, pl.ds(base, 6), :]
        corner[pl.ds(9, 3), :] = turned[2, pl.ds(base, 3), :]
        value = jnp.where(inside, gather_lanes(corner[...], source), 0.0)[0:12]
        for plane in range(2):
            at = (lv.e - 6 + 2 * i + plane) * lv.rows + lv.e - 6
            for odd in range(2):
                where = pl.ds(at + odd, 12, stride=2)
                x[0, where, :] = x[0, where, :] + value
        return carry

    lax.fori_loop(0, 12, body, 0)


def cycle(ny, nz, names, *refs):
    refs = list(refs)
    right_hbm, faces_hbm, cells_hbm, solution_hbm, residual_hbm, norm_out = refs[:6]
    s = dict(zip(names, refs[6:]))
    gx, gy, gz = lax.axis_index("gx"), lax.axis_index("gy"), lax.axis_index("gz")
    here = (gx, gy, gz, ny, nz)

    loads = [pltpu.make_async_copy(faces_hbm.at[d], s["land"].at[d], s["load_sem"].at[d]) for d in range(3)]
    loads.append(pltpu.make_async_copy(cells_hbm, s["land"].at[3], s["load_sem"].at[3]))
    loads.append(pltpu.make_async_copy(right_hbm, s["land"].at[4], s["load_sem"].at[4]))
    for copy in loads:
        copy.start()

    def other(t):
        return lax.rem(gy + t // nz, ny), lax.rem(gz + t % nz, nz)

    barrier = pltpu.get_barrier_semaphore()

    def greet(t, carry):
        oy, oz = other(t)
        pl.semaphore_signal(barrier, inc=1, device_id=(gx, oy, oz), device_id_type=MESH)
        return carry

    pl.semaphore_signal(barrier, inc=1, device_id=(1 - gx, gy, gz), device_id_type=MESH)
    lax.fori_loop(1, ny * nz, greet, 0)

    f0, f1, f2 = s["f0"], s["f1"], s["f2"]
    ex = {k: Exchange(*v) for k, v in EXCHANGES.items()}
    for k, target in (("e0", f0), ("c1", f1), ("c2", f2), ("e1", f1), ("e2", f2), ("x0", s["x0a"])):
        ex[k].bind(here, target, [s[k + str(i)] for i in range(9)])

    low = lanes(48) < 64
    for a in range(5):
        loads[a].wait()

        def load(i, carry, a=a):
            first = jnp.pad(s["land"][a, i], ((0, 0), (0, 80)))
            second = jnp.pad(s["land"][a, i + 24], ((0, 0), (0, 80)))
            value = roll_lanes(first, L0.zo) + roll_lanes(second, 64 + L0.zo)
            f0[a, pl.ds((L0.e + i) * L0.rows + L0.e, 48), :] = value
            return carry

        lax.fori_loop(0, 24, load, 0, unroll=2)

    f1[...] = jnp.zeros_like(f1)
    f2[...] = jnp.zeros_like(f2)
    s["square"][...] = jnp.zeros_like(s["square"])

    def square(i, carry):
        value = f0[4, pl.ds((L0.e + i) * L0.rows + L0.e, 48), :]
        return carry + value * value

    squares = lax.fori_loop(0, 24, square, jnp.zeros((48, 128), F32), unroll=2)
    coarsen_fields(L0, L1, f0, fields_put(L1, f1))
    coarsen_fields(L1, L2, f1, fields_put(L2, f2))

    block = s["block"]
    block[...] = jnp.zeros_like(block)

    def block_put(field, plane, value):
        block[field, pl.ds(plane * 6, 6), :] = value

    coarsen_fields(L2, None, f2, block_put)

    def tile_of(field):
        return roll_lanes(block[field].T[0:8], gx * 36)

    own4, pair4, own1, pair1, own_n, pair_n = (s[k] for k in ("own4", "pair4", "own1", "pair1", "own_n", "pair_n"))
    for field in range(4):
        own4[field] = tile_of(field)

    pl.semaphore_wait(barrier, ny * nz)

    def partner(src, dst, i):
        return pltpu.make_async_remote_copy(
            src_ref=src,
            dst_ref=dst,
            send_sem=s["pair_send"].at[i],
            recv_sem=s["pair_recv"].at[i],
            device_id=(1 - gx, gy, gz),
            device_id_type=MESH,
        )

    def spread(src, dst, i):
        def copy(t, to):
            oy, oz = other(t if to else ny * nz - t)
            sy, sz = (gy, gz) if to else (oy, oz)
            return oy, oz, sy, sz

        def start(t, carry):
            oy, oz = other(t)
            pltpu.make_async_remote_copy(
                src_ref=src,
                dst_ref=dst.at[gy, gz],
                send_sem=s["all_send"].at[i, t],
                recv_sem=s["all_recv"].at[i, t],
                device_id=(gx, oy, oz),
                device_id_type=MESH,
            ).start()
            return carry

        def finish(t, carry):
            oy = lax.rem(gy + ny - t // nz, ny)
            oz = lax.rem(gz + nz - t % nz, nz)
            pltpu.make_async_remote_copy(
                src_ref=src,
                dst_ref=dst.at[oy, oz],
                send_sem=s["all_send"].at[i, t],
                recv_sem=s["all_recv"].at[i, t],
                device_id=(gx, oy, oz),
                device_id_type=MESH,
            ).wait()
            return carry

        return (
            lambda: lax.fori_loop(1, ny * nz, start, 0),
            lambda: lax.fori_loop(1, ny * nz, finish, 0),
        )

    ex["e0"].start_x()
    pair_coef = partner(own4, pair4, 0)
    pair_coef.start()
    ex["e0"].finish_x()
    ex["e0"].start_yz()
    ex["c1"].start_x()
    ex["c2"].start_x()
    ex["c1"].finish_x()
    ex["c2"].finish_x()
    pair_coef.wait()
    merged = s["merged4"]
    merged[...] = own4[...] + pair4[...]
    g4, g1, gn = s["g4"], s["g1"], s["gn"]
    g4[gy, gz] = merged[...]
    coef_start, coef_finish = spread(merged, g4, 0)

    ex["e0"].finish_yz()
    ex["c1"].start_yz()
    ex["c2"].start_yz()
    coef_start()
    scaling(L0, f0, s["i0"], 3)
    smooth_from_zero(L0, f0, s["i0"], s["x0a"], s["x0b"], s["d0"], 3)
    restrict(L0, L1, f0, s["x0a"], s["sums"], fields_put(L1, f1))
    ex["e1"].start_x()
    ex["x0"].start_x()
    ex["c1"].finish_yz()
    ex["c2"].finish_yz()
    ex["e1"].finish_x()
    ex["e1"].start_yz()
    ex["x0"].finish_x()
    scaling(L1, f1, s["i1"], 7)
    scaling(L2, f2, s["i2"], 8)
    ex["e1"].finish_yz()
    ex["x0"].start_yz()
    smooth_from_zero(L1, f1, s["i1"], s["x1a"], s["x1b"], s["d1"], 7)
    restrict(L1, L2, f1, s["x1a"], s["sums"], fields_put(L2, f2))
    ex["e2"].start_x()
    ex["e2"].finish_x()
    ex["e2"].start_yz()
    coef_finish()
    gathered = lambda a, g: g4[g, :, a].reshape(128, 128)
    inverse = whole_inverse(ny, gathered)
    for g in range(ny):
        s["i3"][g] = inverse[g]
    coarse_fields(ny, g4, s["bottom"])
    ex["x0"].finish_yz()
    ex["e2"].finish_yz()
    smooth_from_zero(L2, f2, s["i2"], s["x2a"], s["x2b"], s["d2"], 8)
    restrict(L2, None, f2, s["x2a"], s["sums"], block_put)
    own1[...] = tile_of(4)
    pair_source = partner(own1, pair1, 1)
    pair_source.start()
    pair_source.wait()
    s["merged1"][...] = own1[...] + pair1[...]
    g1[gy, gz] = s["merged1"][...]
    source_start, source_finish = spread(s["merged1"], g1, 1)
    source_start()
    source_finish()
    coarse_solve(ny, g4, g1, s["i3"], s["bottom"], s["x3"], s["d3"])
    window(L2, gx, gy, gz, ny, s["x3"], s["padded"], s["turned"], s["corner"], s["x2a"])
    smooth(L2, f2, s["i2"], s["x2a"], s["x2b"], s["d2"], 6)
    prolong(L1, L2, s["x2b"], s["x1a"], 3)
    smooth(L1, f1, s["i1"], s["x1a"], s["x1b"], s["d1"], 5)
    prolong(L0, L1, s["x1b"], s["x0a"], 2)
    smooth(L0, f0, s["i0"], s["x0a"], s["x0b"], s["d0"], 4)

    land = s["land"]
    r0 = L0.rows

    def unload(slot, i, value):
        for half in range(2):
            moved = roll_lanes(value, -(L0.zo + 64 * half))
            land[slot, i + 24 * half] = moved[:, 0:48]

    def out_solution(i, carry):
        unload(0, i, s["x0b"][0, pl.ds((L0.e + i) * r0 + L0.e, 48), :])
        return carry

    lax.fori_loop(0, 24, out_solution, 0, unroll=2)
    out0 = pltpu.make_async_copy(land.at[0], solution_hbm, s["out_sem"].at[0])
    out0.start()

    def final(p, row, here_x, applied):
        s["sums"][0, pl.ds((p - L0.e) * r0, r0), :] = f0[4, pl.ds(row, r0), :] - applied

    sweep(L0, f0, s["x0b"], 0, final)
    lane48 = lanes(48) % 64
    inside = (lane48 >= L0.zo) & (lane48 < L0.zo + 48)

    def out_residual(i, carry):
        value = s["sums"][0, pl.ds(i * r0 + L0.e, 48), :]
        unload(1, i, value)
        value = jnp.where(inside, value, 0.0)
        return carry + value * value

    ends = lax.fori_loop(0, 24, out_residual, jnp.zeros((48, 128), F32), unroll=2)
    out1 = pltpu.make_async_copy(land.at[1], residual_hbm, s["out_sem"].at[1])
    out1.start()

    def fold(value):
        return jnp.sum(value, axis=0, keepdims=True)

    own_n[...] = jnp.concatenate([fold(squares), fold(ends), jnp.zeros((6, 128), F32)], axis=0)
    pair_norm = partner(own_n, pair_n, 2)
    pair_norm.start()
    pair_norm.wait()
    s["merged_n"][...] = jnp.where(gx == 0, own_n[...] + pair_n[...], pair_n[...] + own_n[...])
    gn[gy, gz] = s["merged_n"][...]
    norm_start, norm_finish = spread(s["merged_n"], gn, 2)
    norm_start()
    norm_finish()
    all_n = jnp.sum(gn[...].reshape(ny * nz, 8, 128), axis=0)
    sums = jnp.sum(all_n, axis=1, keepdims=True)
    norm = jnp.sqrt(sums[1:2] / sums[0:1])
    norm_out[0, 0] = norm[0, 0]
    out0.wait()
    out1.wait()


EXCHANGES = {
    "e0": (L0, 0, 5),
    "c1": (L1, 0, 4),
    "c2": (L2, 0, 4),
    "e1": (L1, 4, 1),
    "e2": (L2, 4, 1),
    "x0": (L0, 0, 1),
}


def scratch_of(ny, nz):
    vmem = lambda *shape: pltpu.VMEM(shape, F32)
    size = lambda lv: lv.planes * lv.rows
    scratch = {"land": vmem(5, 48, 48, 48), "load_sem": pltpu.SemaphoreType.DMA((5,)), "out_sem": pltpu.SemaphoreType.DMA((2,))}
    for i, lv in enumerate((L0, L1, L2)):
        scratch[f"f{i}"] = vmem(5, size(lv), 128)
        for k in ("i", "d"):
            scratch[f"{k}{i}"] = vmem(1, size(lv), 128)
        scratch[f"x{i}a"] = vmem(1, size(lv), 128)
        scratch[f"x{i}b"] = vmem(1, size(lv), 128)
    scratch["sums"] = vmem(1, 24 * 56, 128)
    scratch["square"] = vmem(8, 128)
    scratch["block"] = vmem(5, 128, 128)
    for k in ("own4", "pair4", "merged4"):
        scratch[k] = vmem(4, 8, 128)
    for k in ("own1", "pair1", "merged1", "own_n", "pair_n", "merged_n"):
        scratch[k] = vmem(8, 128)
    scratch["g4"] = vmem(ny, nz, 4, 8, 128)
    scratch["g1"] = vmem(ny, nz, 8, 128)
    scratch["gn"] = vmem(ny, nz, 8, 128)
    for k in ("pair_send", "pair_recv"):
        scratch[k] = pltpu.SemaphoreType.DMA((3,))
    for k in ("all_send", "all_recv"):
        scratch[k] = pltpu.SemaphoreType.DMA((3, ny * nz))
    for k in ("i3", "x3", "d3"):
        scratch[k] = vmem(ny, 128, 128)
    scratch["bottom"] = vmem(4, ny, 128, 128)
    scratch["padded"] = vmem(ny + 2, nz + 2, 8, 128)
    scratch["turned"] = vmem(3, 152, 128)
    scratch["corner"] = vmem(16, 128)
    for k, v in EXCHANGES.items():
        for i, shape in enumerate(Exchange(*v).scratch()):
            scratch[k + str(i)] = shape
    return scratch


def solution(mesh):
    ny, nz = mesh.shape["gy"], mesh.shape["gz"]
    scratch = scratch_of(ny, nz)

    def shards(right_side, face_coef, absorption):
        field = jax.ShapeDtypeStruct((48, 48, 48), F32)
        solved, residual, norm = pl.pallas_call(
            functools.partial(cycle, ny, nz, tuple(scratch)),
            out_shape=(field, field, jax.ShapeDtypeStruct((1, 1), F32)),
            in_specs=[pl.BlockSpec(memory_space=pl.ANY)] * 3,
            out_specs=(
                pl.BlockSpec(memory_space=pl.ANY),
                pl.BlockSpec(memory_space=pl.ANY),
                pl.BlockSpec(memory_space=pltpu.SMEM),
            ),
            scratch_shapes=list(scratch.values()),
            compiler_params=pltpu.CompilerParams(
                collective_id=0, has_side_effects=True, vmem_limit_bytes=62 * 1024 * 1024
            ),
        )(right_side, face_coef, absorption)
        return solved, residual, norm[0, 0]

    in_specs = (P("gx", "gy", "gz"), P(None, "gx", "gy", "gz"), P("gx", "gy", "gz"))
    out_specs = (P("gx", "gy", "gz"), P("gx", "gy", "gz"), P())
    return jax.shard_map(shards, mesh=mesh, in_specs=in_specs, out_specs=out_specs, check_vma=False)
```

time: 1260 us -> 185 us (0.15); the launches traced: 1230 us -> 185 us
  starting transfers between devices: 423 us -> 0 us
  local copies, waits for them, and re-layouts: 370 us -> 3.47 us
  other arithmetic: 232 us -> 0 us
  Pallas kernels: 0 us -> 179 us
  blocking collectives: 122 us -> 0 us
  waiting for transfers between devices: 52 us -> 0 us
  between operations: 34.9 us -> 2.46 us
    ppermute x165 -> x0, starting transfers between devices: 423 us -> none  [the longest x75 306 us: with_halo(): lax.ppermute(last, axis, up)]
    pallas_call x0 -> x1, Pallas kernels: none -> 179 us  [shards(): pl.pallas_call(functools.partial(cycle, ny, nz, tuple(scratch)), out_shap...]
    reduce_sum x33 -> x0, other arithmetic: 115 us -> none  [the longest x8 35.3 us: average_cells(): return jnp.sum(blocks, axis=(1, 3, 5)) * 0.125]
    slice x111 -> x0, local copies, waits for them, and re-layouts: 104 us -> none  [the longest x82 52.3 us: with_halo(): last = lax.slice_in_dim(value, length - width, length, axis=dim)]
    add x30 -> x0, other arithmetic: 80.5 us -> none  [the longest x20 70.6 us: chebyshev(): iterate = iterate + update]
    unnamed x1 -> x0, blocking collectives: 78.8 us -> none
    reshape x12 -> x0, local copies, waits for them, and re-layouts: 71.8 us -> none  [the longest x5 38.3 us: average_cells(): field.reshape(field.shape[0] // 2, 2, field.shape[1] // 2, 2, field.shape...]
    another operation x13 -> x0, local copies, waits for them, and re-layouts: 71.1 us -> none  [the longest x4 23.3 us: average_faces(): along_z = faces[2].reshape(halves)[..., 0]]
  transfers between devices with their start and end apart: 166 -> 0, of which waited for: 26 -> 0; matrix products, arithmetic and copies ran while one was open for 29% -> 0% of each run, Pallas kernels for 0% -> 0%
where the time goes in v1:
time: 185 us
  Pallas kernels  179 us (97%)
  local copies, waits for them, and re-layouts  3.47 us (2%)
  between operations  2.46 us (1%)
    pallas_call x1, Pallas kernels, shards(): pl.pallas_call(functools.partial(cycle, ny, nz, tuple(scratch)), out_shap...  179 us

profile of v1, /device:TPU:0, one launch (start us, length us, event | category | flops | bytes accessed | tf_op | source)
XLA Modules:
  0.0 184.7 jit_solution(16266724107349917437)
XLA Ops:
  0.6 178.8 %shard_map.58 = (f32[48,48,48]{2,1,0:T(8,128)}, f32[48,48,48]{2,1,0:T(8,128)}, f32[1,1]{1,0:T(1,128)}) custom-call(f32[48,48,48]{2,1,0:T(8,128)} %refs_0_.1, f32[3,48,48,48]{3,2,1,0:T(8,128)} %refs_1_.1, f32[48,48,48]{2,1,0:T(8,128)} %refs_2_.1), custom_call_target="tpu_custom_call" | custom-call | tf_op jit(solution)/shard_map/pallas_call | solution.py:855
  179.5 0.0 copy-start
  179.5 2.5 %copy.9 = f32[48,48,48]{2,1,0:T(8,128)} copy(f32[48,48,48]{2,1,0:T(8,128)} %get-tuple-element.12) | data formatting | bytes 884736
  181.9 0.0 copy-done
  181.9 1.0 copy.10
Async XLA Ops:
  179.5 2.5 %copy-start = (f32[48,48,48]{2,1,0:T(8,128)S(1)}, f32[48,48,48]{2,1,0:T(8,128)}, u32[]{:S(2)}) copy-start(f32[48,48,48]{2,1,0:T(8,128)} %get-tuple-element.13) | copy-start | bytes 1327108

commit v2 on v1

--- a/solution.py
+++ b/solution.py
@@ -22,18 +22,19 @@
 
 
 class Level:
-    def __init__(self, n, e, ways, rows, zo, width, pack_rows):
-        self.n, self.e, self.ways, self.rows, self.zo, self.width, self.ep = n, e, ways, rows, zo, width, pack_rows
+    def __init__(self, n, e, ways, rows, zo, width, width_y, unroll):
+        self.n, self.e, self.ways, self.rows, self.zo, self.width = n, e, ways, rows, zo, width
+        self.width_y, self.unroll = width_y, unroll
         self.half = n // ways
         self.planes = self.half + 2 * e
         self.span = 128 // ways
-        self.slots = self.span // width
-        self.packs = -(-self.planes // self.slots)
-
-
-L0 = Level(48, 4, 2, 56, 8, 4, 4)
-L1 = Level(24, 8, 2, 40, 16, 8, 8)
-L2 = Level(12, 9, 1, 32, 16, 16, 16)
+        self.slots, self.slots_y = self.span // width, self.span // width_y
+        self.packs, self.packs_y = -(-self.planes // self.slots), -(-self.planes // self.slots_y)
+
+
+L0 = Level(48, 4, 2, 56, 8, 4, 64, 4)
+L1 = Level(24, 6, 2, 40, 16, 8, 32, 4)
+L2 = Level(12, 6, 1, 24, 16, 8, 16, 6)
 
 
 def lanes(rows):
@@ -54,6 +55,20 @@
 
 def tile_rows(start, size):
     return pl.ds(pl.multiple_of(start, 8), size)
+
+
+def loop(lo, hi, body, carry, unroll):
+    count = (hi - lo) // unroll
+
+    def chunk(i, carry):
+        for k in range(unroll):
+            carry = body(lo + i * unroll + k, carry)
+        return carry
+
+    carry = lax.fori_loop(0, count, chunk, carry)
+    for k in range(lo + count * unroll, hi):
+        carry = body(k, carry)
+    return carry
 
 
 class Exchange:
@@ -64,18 +79,19 @@
         lv, na = self.level, self.count
         shapes = [
             (na, lv.e * lv.rows, 128),
-            (2, na, lv.planes * lv.ep, 128),
-            (2, na, lv.planes * lv.ep, 128),
+            (2, na, lv.packs_y * lv.e, 128),
+            (2, na, lv.packs_y * lv.e, 128),
+            (2, na, lv.packs * lv.n, 128),
+            (2, na, lv.packs * lv.n, 128),
+            (2, 2, na, lv.packs * lv.e, 128),
+            (2, 2, na, lv.packs * lv.e, 128),
             (2, na, lv.packs * lv.rows, 128),
-            (2, na, lv.packs * lv.rows, 128),
-            (2, 2, na, lv.packs * lv.ep, 128),
-            (2, 2, na, lv.packs * lv.ep, 128),
         ]
         return [pltpu.VMEM(s, F32) for s in shapes] + [pltpu.SemaphoreType.DMA((9,)), pltpu.SemaphoreType.DMA((9,))]
 
     def bind(self, here, ref, scratch):
         self.here, self.ref = here, ref
-        self.xr, self.yb, self.yr, self.zb, self.zr, self.db, self.dr, self.ssem, self.rsem = scratch
+        self.xr, self.yb, self.yr, self.zb, self.zr, self.db, self.dr, self.zf, self.ssem, self.rsem = scratch
         gx, gy, gz, ny, nz = here
         lv = self.level
         e, r = lv.e, lv.rows
@@ -120,8 +136,7 @@
         self.copies[0].wait()
         low = lanes(r) < 64
 
-        def body(i, carry):
-            a, j = i // e, i % e
+        def finish(a, j):
             got = self.xr[a, tile_rows(j * r, r), :]
             if lv.ways == 2:
                 got = roll_lanes(got, 64)
@@ -134,31 +149,43 @@
                 above = got * self.has_x[1]
             ref[self.first + a, tile_rows(j * r, r), :] = below
             ref[self.first + a, tile_rows((e + lv.half + j) * r, r), :] = above
+
+        def body(a, carry):
+            for j in range(e):
+                finish(a, j)
             return carry
 
-        lax.fori_loop(0, self.count * e, body, 0)
-
-    def pack(self, ref, rows, out, lead):
+        lax.fori_loop(0, self.count, body, 0)
+
+    def pack(self, plane, rows, width, shifts, put):
         lv = self.level
-        slot = (lanes(rows) % lv.span) // lv.width
-        shifts = (lv.zo, lv.zo + lv.n - lv.e)
-        for k in range(lv.packs):
-            acc = [jnp.zeros((rows, 128), F32)] * 2
-            for s in range(min(lv.slots, lv.planes - k * lv.slots)):
-                plane = ref((k * lv.slots + s) * rows, rows)
-                for t in range(2):
-                    acc[t] = jnp.where(slot == s, roll_lanes(plane, s * lv.width - shifts[t]), acc[t])
-            for t in range(2):
-                lead(t, k * rows, acc[t])
+        slot = (lanes(rows) % lv.span) // width
+        slots = lv.span // width
+        for k in range(-(-lv.planes // slots)):
+            acc = None
+            for s in range(min(slots, lv.planes - k * slots)):
+                moved = [roll_lanes(value, s * width - shift) for value, shift in zip(plane(k * slots + s), shifts)]
+                acc = moved if s == 0 else [jnp.where(slot == s, new, old) for new, old in zip(moved, acc)]
+            put(k, acc)
 
     def start_yz(self):
         lv, ref = self.level, self.ref
-        r, ep, e = lv.rows, lv.ep, lv.e
+        r, n, e, zo = lv.rows, lv.n, lv.e, lv.zo
+        z_shifts = (zo, zo + n - e)
 
         def pack_y(a, carry):
-            for p in range(lv.planes):
-                self.yb[0, a, pl.ds(p * ep, e), :] = ref[self.first + a, pl.ds(p * r + e, e), :]
-                self.yb[1, a, pl.ds(p * ep, e), :] = ref[self.first + a, pl.ds(p * r + lv.n, e), :]
+            def plane(p):
+                return [ref[self.first + a, pl.ds(p * r + row, e), :] for row in (e, n)]
+
+            def put(k, values):
+                for s in range(2):
+                    self.yb[s, a, pl.ds(k * e, e), :] = values[s]
+
+            if lv.slots_y == 1:
+                for p in range(lv.planes):
+                    put(p, plane(p))
+            else:
+                self.pack(plane, e, lv.width_y, (zo, zo), put)
             return carry
 
         lax.fori_loop(0, self.count, pack_y, 0)
@@ -166,64 +193,74 @@
         self.copies[2].start()
 
         def pack_z(a, carry):
-            def put(t, row, value):
-                self.zb[t, a, pl.ds(row, r), :] = value
-
-            self.pack(lambda row, rows: ref[self.first + a, pl.ds(row, rows), :], r, self.zb, put)
+            def plane(p):
+                return [ref[self.first + a, pl.ds(p * r + e, n), :]] * 2
+
+            def put(k, values):
+                for t in range(2):
+                    self.zb[t, a, pl.ds(k * n, n), :] = values[t]
+
+            self.pack(plane, n, lv.width, z_shifts, put)
             return carry
 
         lax.fori_loop(0, self.count, pack_z, 0)
         self.copies[7].start()
         self.copies[8].start()
 
-        def pack_d(i, carry):
-            s, a = i // self.count, i % self.count
-
-            def put(t, row, value):
-                self.db[s, t, a, pl.ds(row, ep), :] = value
-
-            self.pack(lambda row, rows: self.yb[s, a, pl.ds(row, rows), :], ep, self.db, put)
+        def pack_d(a, carry):
+            def plane(p):
+                low, high = (ref[self.first + a, pl.ds(p * r + row, e), :] for row in (e, n))
+                return low, low, high, high
+
+            def put(k, values):
+                for i in range(4):
+                    self.db[i // 2, i % 2, a, pl.ds(k * e, e), :] = values[i]
+
+            self.pack(plane, e, lv.width, z_shifts * 2, put)
             return carry
 
-        lax.fori_loop(0, 2 * self.count, pack_d, 0)
+        lax.fori_loop(0, self.count, pack_d, 0)
         for i in range(3, 7):
             self.copies[i].start()
 
     def finish_yz(self):
         lv, ref = self.level, self.ref
-        r, ep, e = lv.rows, lv.ep, lv.e
+        r, n, e, zo = lv.rows, lv.n, lv.e, lv.zo
         for i in range(1, 9):
-            self.copies[i].wait()
+            with jax.named_scope("copy" + str(i)):
+                self.copies[i].wait()
         lane = lanes(r) % lv.span
-        at_low = (lane >= lv.zo - e) & (lane < lv.zo)
-        at_high = (lane >= lv.zo + lv.n) & (lane < lv.zo + lv.n + e)
+        at_low = (lane >= zo - e) & (lane < zo)
+        at_high = (lane >= zo + n) & (lane < zo + n + e)
 
         def unpack(a, carry):
-            for p in range(lv.planes):
-                for s in range(2):
-                    row = p * r + (e + lv.n) * s
-                    ref[self.first + a, pl.ds(row, e), :] = self.yr[s, a, pl.ds(p * ep, e), :] * self.has_y[s]
+            for s in range(2):
+                for k in range(lv.packs_y):
+                    got = self.yr[s, a, pl.ds(k * e, e), :] * self.has_y[s]
+                    for slot in range(min(lv.slots_y, lv.planes - k * lv.slots_y)):
+                        row = (k * lv.slots_y + slot) * r + (e + n) * s
+                        moved = roll_lanes(got, zo - slot * lv.width_y) if lv.slots_y > 1 else got
+                        ref[self.first + a, pl.ds(row, e), :] = moved
             for k in range(lv.packs):
                 for t in range(2):
-                    self.zr[t, a, pl.ds(k * r, r), :] = self.zr[t, a, pl.ds(k * r, r), :] * self.has_z[t]
+                    self.zf[t, a, pl.ds(k * r + e, n), :] = self.zr[t, a, pl.ds(k * n, n), :] * self.has_z[t]
                     for s in range(2):
-                        row = k * r + (e + lv.n) * s
                         both = self.has_y[s] * self.has_z[t]
-                        self.zr[t, a, pl.ds(row, e), :] = self.dr[s, t, a, pl.ds(k * ep, e), :] * both
+                        self.zf[t, a, pl.ds(k * r + (e + n) * s, e), :] = self.dr[s, t, a, pl.ds(k * e, e), :] * both
             for k in range(lv.packs):
-                got = [self.zr[t, a, pl.ds(k * r, r), :] for t in range(2)]
+                got = [self.zf[t, a, pl.ds(k * r, r), :] for t in range(2)]
                 for s in range(min(lv.slots, lv.planes - k * lv.slots)):
                     p = k * lv.slots + s
                     value = ref[self.first + a, pl.ds(p * r, r), :]
-                    value = jnp.where(at_low, roll_lanes(got[0], lv.zo - e - s * lv.width), value)
-                    value = jnp.where(at_high, roll_lanes(got[1], lv.zo + lv.n - s * lv.width), value)
+                    value = jnp.where(at_low, roll_lanes(got[0], zo - e - s * lv.width), value)
+                    value = jnp.where(at_high, roll_lanes(got[1], zo + n - s * lv.width), value)
                     ref[self.first + a, pl.ds(p * r, r), :] = value
             return carry
 
         lax.fori_loop(0, self.count, unpack, 0)
 
 
-def scaling(lv, fields, inverse, extent):
+def scaling(lv, fields, inverse, upper, extent):
     r = lv.rows
 
     def body(p, carry):
@@ -232,19 +269,21 @@
         face_z = fields[2, pl.ds(row, r), :]
         total = cells + fields[0, pl.ds(row, r), :] + fields[0, pl.ds(row + r, r), :]
         total = total + fields[1, pl.ds(row, r), :] + fields[1, pl.ds(row + 1, r), :]
-        total = total + face_z + roll_lanes(face_z, -1)
+        above = roll_lanes(face_z, -1)
+        upper[0, pl.ds(row, r), :] = above
+        total = total + face_z + above
         inverse[0, pl.ds(row, r), :] = jnp.where(cells > 0.0, 1.0 / total, 0.0)
         return carry
 
-    lax.fori_loop(lv.e - extent, lv.e + lv.half + extent, body, 0, unroll=2)
-
-
-def sweep(lv, fields, x, extent, emit):
+    loop(lv.e - extent, lv.e + lv.half + extent, body, 0, lv.unroll)
+
+
+def sweep(lv, fields, upper, x, extent, emit, carry=0):
     r = lv.rows
     lo, hi = lv.e - extent, lv.e + lv.half + extent
 
     def body(p, carry):
-        here, flux = carry
+        here, flux, kept = carry
         row = pl.multiple_of(p * r, 8)
         after = x[0, pl.ds(row + r, r), :]
         flux_after = fields[0, pl.ds(row + r, r), :] * (after - here)
@@ -253,21 +292,20 @@
         flux_y = fields[1, pl.ds(row, r), :] * (here - low_y)
         flux_y = flux_y - fields[1, pl.ds(row + 1, r), :] * (high_y - here)
         flux_z = fields[2, pl.ds(row, r), :] * (here - roll_lanes(here, 1))
-        flux_z = flux_z - roll_lanes(flux_z, -1)
+        flux_z = flux_z - upper[0, pl.ds(row, r), :] * (roll_lanes(here, -1) - here)
         applied = fields[3, pl.ds(row, r), :] * here + ((flux - flux_after) + flux_y + flux_z)
-        emit(p, row, here, applied)
-        return after, flux_after
+        return after, flux_after, emit(p, row, here, applied, kept)
 
     row = lo * r
     here = x[0, pl.ds(row, r), :]
     flux = fields[0, pl.ds(row, r), :] * (here - x[0, pl.ds(row - r, r), :])
-    lax.fori_loop(lo, hi, body, (here, flux), unroll=2)
-
-
-def step(lv, fields, inverse, x, out, d, extent, first, coefs, keep):
+    return loop(lo, hi, body, (here, flux, carry), lv.unroll)[2]
+
+
+def step(lv, fields, inverse, upper, x, out, d, extent, first, coefs, keep):
     r = lv.rows
 
-    def emit(p, row, here, applied):
+    def emit(p, row, here, applied, kept):
         scaled = inverse[0, pl.ds(row, r), :] * (fields[4, pl.ds(row, r), :] - applied)
         if first == 0:
             update = scaled * (1.0 / THETA)
@@ -278,11 +316,12 @@
         if keep:
             d[0, pl.ds(row, r), :] = update
         out[0, pl.ds(row, r), :] = here + update
-
-    sweep(lv, fields, x, extent, emit)
-
-
-def smooth_from_zero(lv, fields, inverse, xa, xb, d, extent):
+        return kept
+
+    sweep(lv, fields, upper, x, extent, emit)
+
+
+def smooth_from_zero(lv, fields, inverse, upper, xa, xb, d, extent):
     r = lv.rows
 
     def body(p, carry):
@@ -290,15 +329,15 @@
         xa[0, pl.ds(row, r), :] = inverse[0, pl.ds(row, r), :] * fields[4, pl.ds(row, r), :] * (1.0 / THETA)
         return carry
 
-    lax.fori_loop(lv.e - extent, lv.e + lv.half + extent, body, 0, unroll=2)
-    step(lv, fields, inverse, xa, xb, d, extent - 1, 1, STEP1, True)
-    step(lv, fields, inverse, xb, xa, d, extent - 2, 2, STEP2, False)
-
-
-def smooth(lv, fields, inverse, xa, xb, d, extent):
-    step(lv, fields, inverse, xa, xb, d, extent - 1, 0, None, True)
-    step(lv, fields, inverse, xb, xa, d, extent - 2, 2, STEP1, True)
-    step(lv, fields, inverse, xa, xb, d, extent - 3, 2, STEP2, False)
+    loop(lv.e - extent, lv.e + lv.half + extent, body, 0, lv.unroll)
+    step(lv, fields, inverse, upper, xa, xb, d, extent - 1, 1, STEP1, True)
+    step(lv, fields, inverse, upper, xb, xa, d, extent - 2, 2, STEP2, False)
+
+
+def smooth(lv, fields, inverse, upper, xa, xb, d, extent):
+    step(lv, fields, inverse, upper, xa, xb, d, extent - 1, 0, None, True)
+    step(lv, fields, inverse, upper, xb, xa, d, extent - 2, 2, STEP1, True)
+    step(lv, fields, inverse, upper, xa, xb, d, extent - 3, 2, STEP2, False)
 
 
 def coarse_lanes(lv, below, rows, half):
@@ -345,16 +384,17 @@
         place(lv, below, put_c, i, (rows(3, 0, 0) + rows(3, 0, 1) + rows(3, 1, 0) + rows(3, 1, 1)) * 0.125, True)
         return carry
 
-    lax.fori_loop(0, lv.half // 2, body, 0)
-
-
-def restrict(lv, below, fields, x, sums, put):
+    loop(0, lv.half // 2, body, 0, 3)
+
+
+def restrict(lv, below, fields, upper, x, sums, put):
     r, n2 = lv.rows, lv.n // 2
 
-    def emit(p, row, here, applied):
+    def emit(p, row, here, applied, kept):
         sums[0, pl.ds((p - lv.e) * r, r), :] = fields[4, pl.ds(row, r), :] - applied
-
-    sweep(lv, fields, x, 0, emit)
+        return kept
+
+    sweep(lv, fields, upper, x, 0, emit)
 
     def body(i, carry):
         total = None
@@ -365,7 +405,7 @@
         place(lv, below, functools.partial(put, 4), i, total * 0.125, True)
         return carry
 
-    lax.fori_loop(0, lv.half // 2, body, 0)
+    loop(0, lv.half // 2, body, 0, 6)
 
 
 def fields_put(below, fields):
@@ -399,7 +439,7 @@
                 x[0, where, :] = x[0, where, :] + value
         return carry
 
-    lax.fori_loop(0, lv.half // 2 + 2 * reach, body, 0)
+    loop(0, lv.half // 2 + 2 * reach, body, 0, 4)
 
 
 def whole_operator(ny, fields, v, scale):
@@ -559,7 +599,11 @@
                 x[0, where, :] = x[0, where, :] + value
         return carry
 
-    lax.fori_loop(0, 12, body, 0)
+    loop(0, 12, body, 0, 4)
+
+
+def hops(t, nz):
+    return sum(min(d, 4 - d) for d in (t // nz % 4, t % nz // 4, t % 4))
 
 
 def cycle(ny, nz, names, *refs):
@@ -568,6 +612,7 @@
     s = dict(zip(names, refs[6:]))
     gx, gy, gz = lax.axis_index("gx"), lax.axis_index("gy"), lax.axis_index("gz")
     here = (gx, gy, gz, ny, nz)
+    scope = jax.named_scope
 
     loads = [pltpu.make_async_copy(faces_hbm.at[d], s["land"].at[d], s["load_sem"].at[d]) for d in range(3)]
     loads.append(pltpu.make_async_copy(cells_hbm, s["land"].at[3], s["load_sem"].at[3]))
@@ -578,62 +623,19 @@
     def other(t):
         return lax.rem(gy + t // nz, ny), lax.rem(gz + t % nz, nz)
 
+    order = sorted(range(1, ny * nz), key=lambda t: -hops(t, nz))
     barrier = pltpu.get_barrier_semaphore()
-
-    def greet(t, carry):
-        oy, oz = other(t)
-        pl.semaphore_signal(barrier, inc=1, device_id=(gx, oy, oz), device_id_type=MESH)
-        return carry
-
-    pl.semaphore_signal(barrier, inc=1, device_id=(1 - gx, gy, gz), device_id_type=MESH)
-    lax.fori_loop(1, ny * nz, greet, 0)
+    with scope("greet"):
+        for t in order:
+            oy, oz = other(t)
+            pl.semaphore_signal(barrier, inc=1, device_id=(gx, oy, oz), device_id_type=MESH)
+        pl.semaphore_signal(barrier, inc=1, device_id=(1 - gx, gy, gz), device_id_type=MESH)
 
     f0, f1, f2 = s["f0"], s["f1"], s["f2"]
     ex = {k: Exchange(*v) for k, v in EXCHANGES.items()}
-    for k, target in (("e0", f0), ("c1", f1), ("c2", f2), ("e1", f1), ("e2", f2), ("x0", s["x0a"])):
-        ex[k].bind(here, target, [s[k + str(i)] for i in range(9)])
-
-    low = lanes(48) < 64
-    for a in range(5):
-        loads[a].wait()
-
-        def load(i, carry, a=a):
-            first = jnp.pad(s["land"][a, i], ((0, 0), (0, 80)))
-            second = jnp.pad(s["land"][a, i + 24], ((0, 0), (0, 80)))
-            value = roll_lanes(first, L0.zo) + roll_lanes(second, 64 + L0.zo)
-            f0[a, pl.ds((L0.e + i) * L0.rows + L0.e, 48), :] = value
-            return carry
-
-        lax.fori_loop(0, 24, load, 0, unroll=2)
-
-    f1[...] = jnp.zeros_like(f1)
-    f2[...] = jnp.zeros_like(f2)
-    s["square"][...] = jnp.zeros_like(s["square"])
-
-    def square(i, carry):
-        value = f0[4, pl.ds((L0.e + i) * L0.rows + L0.e, 48), :]
-        return carry + value * value
-
-    squares = lax.fori_loop(0, 24, square, jnp.zeros((48, 128), F32), unroll=2)
-    coarsen_fields(L0, L1, f0, fields_put(L1, f1))
-    coarsen_fields(L1, L2, f1, fields_put(L2, f2))
-
-    block = s["block"]
-    block[...] = jnp.zeros_like(block)
-
-    def block_put(field, plane, value):
-        block[field, pl.ds(plane * 6, 6), :] = value
-
-    coarsen_fields(L2, None, f2, block_put)
-
-    def tile_of(field):
-        return roll_lanes(block[field].T[0:8], gx * 36)
-
-    own4, pair4, own1, pair1, own_n, pair_n = (s[k] for k in ("own4", "pair4", "own1", "pair1", "own_n", "pair_n"))
-    for field in range(4):
-        own4[field] = tile_of(field)
-
-    pl.semaphore_wait(barrier, ny * nz)
+    targets = {"e0": f0, "c1": f1, "c2": f2, "e1": f1, "e2": f2, "x0": s["x0a"], "x1": s["x1a"], "x2": s["x2a"]}
+    for k, target in targets.items():
+        ex[k].bind(here, target, [s[k + str(i)] for i in range(10)])
 
     def partner(src, dst, i):
         return pltpu.make_async_remote_copy(
@@ -645,110 +647,227 @@
             device_id_type=MESH,
         )
 
-    def spread(src, dst, i):
-        def copy(t, to):
-            oy, oz = other(t if to else ny * nz - t)
-            sy, sz = (gy, gz) if to else (oy, oz)
-            return oy, oz, sy, sz
-
-        def start(t, carry):
+    def spread(src, slot, i):
+        def one(t, y, z):
             oy, oz = other(t)
-            pltpu.make_async_remote_copy(
+            return pltpu.make_async_remote_copy(
                 src_ref=src,
-                dst_ref=dst.at[gy, gz],
+                dst_ref=slot(y, z),
                 send_sem=s["all_send"].at[i, t],
                 recv_sem=s["all_recv"].at[i, t],
                 device_id=(gx, oy, oz),
                 device_id_type=MESH,
-            ).start()
+            )
+
+        def start():
+            for t in order:
+                one(t, gy, gz).start()
+
+        def finish():
+            def body(t, carry):
+                one(t, lax.rem(gy + ny - t // nz, ny), lax.rem(gz + nz - t % nz, nz)).wait()
+                return carry
+
+            lax.fori_loop(1, ny * nz, body, 0)
+
+        return start, finish
+
+    f1[...] = jnp.zeros_like(f1)
+    f2[...] = jnp.zeros_like(f2)
+    block = s["block"]
+    block[...] = jnp.zeros_like(block)
+
+    def block_put(field, plane, value):
+        block[field, pl.ds(plane * 6, 6), :] = value
+
+    for a in range(5):
+        with scope("load_wait"):
+            loads[a].wait()
+
+        def load(i, carry, a=a):
+            first = jnp.pad(s["land"][a, i], ((0, 0), (0, 80)))
+            second = jnp.pad(s["land"][a, i + 24], ((0, 0), (0, 80)))
+            value = roll_lanes(first, L0.zo) + roll_lanes(second, 64 + L0.zo)
+            f0[a, pl.ds((L0.e + i) * L0.rows + L0.e, 48), :] = value
             return carry
 
-        def finish(t, carry):
-            oy = lax.rem(gy + ny - t // nz, ny)
-            oz = lax.rem(gz + nz - t % nz, nz)
-            pltpu.make_async_remote_copy(
-                src_ref=src,
-                dst_ref=dst.at[oy, oz],
-                send_sem=s["all_send"].at[i, t],
-                recv_sem=s["all_recv"].at[i, t],
-                device_id=(gx, oy, oz),
-                device_id_type=MESH,
-            ).wait()
-            return carry
-
-        return (
-            lambda: lax.fori_loop(1, ny * nz, start, 0),
-            lambda: lax.fori_loop(1, ny * nz, finish, 0),
-        )
-
+        with scope("layout"):
+            loop(0, 24, load, 0, 6)
+
+    with scope("barrier"):
+        pl.semaphore_wait(barrier, ny * nz)
     ex["e0"].start_x()
+    with scope("coarsen_0"):
+        coarsen_fields(L0, L1, f0, fields_put(L1, f1))
+    ex["c1"].start_x()
+    with scope("e0_finish_x"):
+        ex["e0"].finish_x()
+    with scope("e0_start_yz"):
+        ex["e0"].start_yz()
+    with scope("coarsen_1"):
+        coarsen_fields(L1, L2, f1, fields_put(L2, f2))
+    ex["c2"].start_x()
+    with scope("coarsen_2"):
+        coarsen_fields(L2, None, f2, block_put)
+
+    def tile_of(field):
+        return roll_lanes(block[field].T[0:8], gx * 36)
+
+    own4, pair4, own1, pair1, own_n, pair_n = (s[k] for k in ("own4", "pair4", "own1", "pair1", "own_n", "pair_n"))
+    for field in range(4):
+        own4[field] = tile_of(field)
     pair_coef = partner(own4, pair4, 0)
     pair_coef.start()
-    ex["e0"].finish_x()
-    ex["e0"].start_yz()
-    ex["c1"].start_x()
-    ex["c2"].start_x()
-    ex["c1"].finish_x()
-    ex["c2"].finish_x()
-    pair_coef.wait()
+
+    def square(i, carry):
+        value = f0[4, pl.ds((L0.e + i) * L0.rows + L0.e, 48), :]
+        return carry + value * value
+
+    with scope("square"):
+        squares = loop(0, 24, square, jnp.zeros((48, 128), F32), 4)
+    with scope("c1_finish_x"):
+        ex["c1"].finish_x()
+    with scope("c1_start_yz"):
+        ex["c1"].start_yz()
+    with scope("c2_finish_x"):
+        ex["c2"].finish_x()
+    with scope("c2_start_yz"):
+        ex["c2"].start_yz()
+    g4, g1, gn = s["g4"], s["g1"], s["gn"]
+    with scope("pair_coef"):
+        pair_coef.wait()
     merged = s["merged4"]
     merged[...] = own4[...] + pair4[...]
-    g4, g1, gn = s["g4"], s["g1"], s["gn"]
-    g4[gy, gz] = merged[...]
-    coef_start, coef_finish = spread(merged, g4, 0)
-
-    ex["e0"].finish_yz()
-    ex["c1"].start_yz()
-    ex["c2"].start_yz()
-    coef_start()
-    scaling(L0, f0, s["i0"], 3)
-    smooth_from_zero(L0, f0, s["i0"], s["x0a"], s["x0b"], s["d0"], 3)
-    restrict(L0, L1, f0, s["x0a"], s["sums"], fields_put(L1, f1))
+    mine = pl.ds(2 * gx, 2)
+    g4[gy, gz, mine] = merged[mine]
+    coef_start, coef_finish = spread(merged.at[mine], lambda y, z: g4.at[y, z, mine], 0)
+    with scope("coef_start"):
+        coef_start()
+    with scope("e0_finish_yz"):
+        ex["e0"].finish_yz()
+    with scope("scaling_0"):
+        scaling(L0, f0, s["i0"], s["u0"], 3)
+    with scope("smooth_0"):
+        smooth_from_zero(L0, f0, s["i0"], s["u0"], s["x0a"], s["x0b"], s["d0"], 3)
+    with scope("restrict_0"):
+        restrict(L0, L1, f0, s["u0"], s["x0a"], s["sums"], fields_put(L1, f1))
     ex["e1"].start_x()
+    with scope("c1_finish_yz"):
+        ex["c1"].finish_yz()
+    with scope("e1_finish_x"):
+        ex["e1"].finish_x()
+    with scope("e1_start_yz"):
+        ex["e1"].start_yz()
     ex["x0"].start_x()
-    ex["c1"].finish_yz()
-    ex["c2"].finish_yz()
-    ex["e1"].finish_x()
-    ex["e1"].start_yz()
-    ex["x0"].finish_x()
-    scaling(L1, f1, s["i1"], 7)
-    scaling(L2, f2, s["i2"], 8)
-    ex["e1"].finish_yz()
-    ex["x0"].start_yz()
-    smooth_from_zero(L1, f1, s["i1"], s["x1a"], s["x1b"], s["d1"], 7)
-    restrict(L1, L2, f1, s["x1a"], s["sums"], fields_put(L2, f2))
+    with scope("c2_finish_yz"):
+        ex["c2"].finish_yz()
+    with scope("scaling_12"):
+        scaling(L1, f1, s["i1"], s["u1"], 4)
+        scaling(L2, f2, s["i2"], s["u2"], 5)
+    with scope("e1_finish_yz"):
+        ex["e1"].finish_yz()
+    with scope("smooth_1"):
+        smooth_from_zero(L1, f1, s["i1"], s["u1"], s["x1a"], s["x1b"], s["d1"], 3)
+    with scope("restrict_1"):
+        restrict(L1, L2, f1, s["u1"], s["x1a"], s["sums"], fields_put(L2, f2))
     ex["e2"].start_x()
-    ex["e2"].finish_x()
-    ex["e2"].start_yz()
-    coef_finish()
-    gathered = lambda a, g: g4[g, :, a].reshape(128, 128)
-    inverse = whole_inverse(ny, gathered)
-    for g in range(ny):
-        s["i3"][g] = inverse[g]
-    coarse_fields(ny, g4, s["bottom"])
-    ex["x0"].finish_yz()
-    ex["e2"].finish_yz()
-    smooth_from_zero(L2, f2, s["i2"], s["x2a"], s["x2b"], s["d2"], 8)
-    restrict(L2, None, f2, s["x2a"], s["sums"], block_put)
+    ex["x1"].start_x()
+    with scope("x0_finish_x"):
+        ex["x0"].finish_x()
+    with scope("e2_finish_x"):
+        ex["e2"].finish_x()
+    with scope("e2_start_yz"):
+        ex["e2"].start_yz()
+    with scope("coef_finish"):
+        coef_finish()
+    other_half = pltpu.make_async_remote_copy(
+        src_ref=g4.at[:, :, mine],
+        dst_ref=g4.at[:, :, mine],
+        send_sem=s["pair_send"].at[3],
+        recv_sem=s["pair_recv"].at[3],
+        device_id=(1 - gx, gy, gz),
+        device_id_type=MESH,
+    )
+    other_half.start()
+    with scope("x0_start_yz"):
+        ex["x0"].start_yz()
+    with scope("e2_finish_yz"):
+        ex["e2"].finish_yz()
+    with scope("smooth_2"):
+        smooth_from_zero(L2, f2, s["i2"], s["u2"], s["x2a"], s["x2b"], s["d2"], 3)
+    with scope("restrict_2"):
+        restrict(L2, None, f2, s["u2"], s["x2a"], s["sums"], block_put)
     own1[...] = tile_of(4)
     pair_source = partner(own1, pair1, 1)
     pair_source.start()
-    pair_source.wait()
+    ex["x2"].start_x()
+    with scope("other_half"):
+        other_half.wait()
+    with scope("pair_source"):
+        pair_source.wait()
     s["merged1"][...] = own1[...] + pair1[...]
     g1[gy, gz] = s["merged1"][...]
-    source_start, source_finish = spread(s["merged1"], g1, 1)
-    source_start()
-    source_finish()
-    coarse_solve(ny, g4, g1, s["i3"], s["bottom"], s["x3"], s["d3"])
-    window(L2, gx, gy, gz, ny, s["x3"], s["padded"], s["turned"], s["corner"], s["x2a"])
-    smooth(L2, f2, s["i2"], s["x2a"], s["x2b"], s["d2"], 6)
-    prolong(L1, L2, s["x2b"], s["x1a"], 3)
-    smooth(L1, f1, s["i1"], s["x1a"], s["x1b"], s["d1"], 5)
-    prolong(L0, L1, s["x1b"], s["x0a"], 2)
-    smooth(L0, f0, s["i0"], s["x0a"], s["x0b"], s["d0"], 4)
+    source_start, source_finish = spread(s["merged1"], lambda y, z: g1.at[y, z], 1)
+    with scope("source_start"):
+        source_start()
+    gathered = lambda a, g: g4[g, :, a].reshape(128, 128)
+    with scope("coarse_fields"):
+        inverse = whole_inverse(ny, gathered)
+        for g in range(ny):
+            s["i3"][g] = inverse[g]
+        coarse_fields(ny, g4, s["bottom"])
+    with scope("hidden"):
+        ex["x1"].finish_x()
+        ex["x1"].start_yz()
+        ex["x2"].finish_x()
+        ex["x2"].start_yz()
+        ex["x0"].finish_yz()
+    with scope("source_finish"):
+        source_finish()
+    with scope("coarse_solve"):
+        coarse_solve(ny, g4, g1, s["i3"], s["bottom"], s["x3"], s["d3"])
+    with scope("x2_finish_yz"):
+        ex["x2"].finish_yz()
+    with scope("window"):
+        window(L2, gx, gy, gz, ny, s["x3"], s["padded"], s["turned"], s["corner"], s["x2a"])
+    with scope("post_2"):
+        smooth(L2, f2, s["i2"], s["u2"], s["x2a"], s["x2b"], s["d2"], 6)
+    with scope("x1_finish_yz"):
+        ex["x1"].finish_yz()
+    with scope("prolong_1"):
+        prolong(L1, L2, s["x2b"], s["x1a"], 3)
+    with scope("post_1"):
+        smooth(L1, f1, s["i1"], s["u1"], s["x1a"], s["x1b"], s["d1"], 5)
+    with scope("prolong_0"):
+        prolong(L0, L1, s["x1b"], s["x0a"], 2)
+    with scope("post_0"):
+        smooth(L0, f0, s["i0"], s["u0"], s["x0a"], s["x0b"], s["d0"], 4)
 
     land = s["land"]
     r0 = L0.rows
+    lane48 = lanes(48) % 64
+    inside = (lane48 >= L0.zo) & (lane48 < L0.zo + 48)
+
+    def final(p, row, here_x, applied, kept):
+        s["sums"][0, pl.ds((p - L0.e) * r0, r0), :] = f0[4, pl.ds(row, r0), :] - applied
+        return kept
+
+    with scope("final"):
+        sweep(L0, f0, s["u0"], s["x0b"], 0, final)
+
+    def out_square(i, carry):
+        value = jnp.where(inside, s["sums"][0, pl.ds(i * r0 + L0.e, 48), :], 0.0)
+        return carry + value * value
+
+    with scope("square"):
+        ends = loop(0, 24, out_square, jnp.zeros((48, 128), F32), 4)
+
+    def fold(value):
+        return jnp.sum(value, axis=0, keepdims=True)
+
+    own_n[...] = jnp.concatenate([fold(squares), fold(ends), jnp.zeros((6, 128), F32)], axis=0)
+    pair_norm = partner(own_n, pair_n, 2)
+    pair_norm.start()
 
     def unload(slot, i, value):
         for half in range(2):
@@ -759,45 +878,34 @@
         unload(0, i, s["x0b"][0, pl.ds((L0.e + i) * r0 + L0.e, 48), :])
         return carry
 
-    lax.fori_loop(0, 24, out_solution, 0, unroll=2)
+    def out_residual(i, carry):
+        unload(1, i, s["sums"][0, pl.ds(i * r0 + L0.e, 48), :])
+        return carry
+
+    with scope("unload_solution"):
+        loop(0, 24, out_solution, 0, 6)
     out0 = pltpu.make_async_copy(land.at[0], solution_hbm, s["out_sem"].at[0])
     out0.start()
-
-    def final(p, row, here_x, applied):
-        s["sums"][0, pl.ds((p - L0.e) * r0, r0), :] = f0[4, pl.ds(row, r0), :] - applied
-
-    sweep(L0, f0, s["x0b"], 0, final)
-    lane48 = lanes(48) % 64
-    inside = (lane48 >= L0.zo) & (lane48 < L0.zo + 48)
-
-    def out_residual(i, carry):
-        value = s["sums"][0, pl.ds(i * r0 + L0.e, 48), :]
-        unload(1, i, value)
-        value = jnp.where(inside, value, 0.0)
-        return carry + value * value
-
-    ends = lax.fori_loop(0, 24, out_residual, jnp.zeros((48, 128), F32), unroll=2)
+    with scope("pair_norm"):
+        pair_norm.wait()
+    s["merged_n"][...] = jnp.where(gx == 0, own_n[...] + pair_n[...], pair_n[...] + own_n[...])
+    gn[gy, gz] = s["merged_n"][...]
+    norm_start, norm_finish = spread(s["merged_n"], lambda y, z: gn.at[y, z], 2)
+    with scope("norm_start"):
+        norm_start()
+    with scope("unload_residual"):
+        loop(0, 24, out_residual, 0, 6)
     out1 = pltpu.make_async_copy(land.at[1], residual_hbm, s["out_sem"].at[1])
     out1.start()
-
-    def fold(value):
-        return jnp.sum(value, axis=0, keepdims=True)
-
-    own_n[...] = jnp.concatenate([fold(squares), fold(ends), jnp.zeros((6, 128), F32)], axis=0)
-    pair_norm = partner(own_n, pair_n, 2)
-    pair_norm.start()
-    pair_norm.wait()
-    s["merged_n"][...] = jnp.where(gx == 0, own_n[...] + pair_n[...], pair_n[...] + own_n[...])
-    gn[gy, gz] = s["merged_n"][...]
-    norm_start, norm_finish = spread(s["merged_n"], gn, 2)
-    norm_start()
-    norm_finish()
+    with scope("norm_finish"):
+        norm_finish()
     all_n = jnp.sum(gn[...].reshape(ny * nz, 8, 128), axis=0)
     sums = jnp.sum(all_n, axis=1, keepdims=True)
     norm = jnp.sqrt(sums[1:2] / sums[0:1])
     norm_out[0, 0] = norm[0, 0]
-    out0.wait()
-    out1.wait()
+    with scope("out_wait"):
+        out0.wait()
+        out1.wait()
 
 
 EXCHANGES = {
@@ -807,6 +915,8 @@
     "e1": (L1, 4, 1),
     "e2": (L2, 4, 1),
     "x0": (L0, 0, 1),
+    "x1": (L1, 0, 1),
+    "x2": (L2, 0, 1),
 }
 
 
@@ -816,12 +926,11 @@
     scratch = {"land": vmem(5, 48, 48, 48), "load_sem": pltpu.SemaphoreType.DMA((5,)), "out_sem": pltpu.SemaphoreType.DMA((2,))}
     for i, lv in enumerate((L0, L1, L2)):
         scratch[f"f{i}"] = vmem(5, size(lv), 128)
-        for k in ("i", "d"):
+        for k in ("i", "d", "u"):
             scratch[f"{k}{i}"] = vmem(1, size(lv), 128)
         scratch[f"x{i}a"] = vmem(1, size(lv), 128)
         scratch[f"x{i}b"] = vmem(1, size(lv), 128)
     scratch["sums"] = vmem(1, 24 * 56, 128)
-    scratch["square"] = vmem(8, 128)
     scratch["block"] = vmem(5, 128, 128)
     for k in ("own4", "pair4", "merged4"):
         scratch[k] = vmem(4, 8, 128)
@@ -831,7 +940,7 @@
     scratch["g1"] = vmem(ny, nz, 8, 128)
     scratch["gn"] = vmem(ny, nz, 8, 128)
     for k in ("pair_send", "pair_recv"):
-        scratch[k] = pltpu.SemaphoreType.DMA((3,))
+        scratch[k] = pltpu.SemaphoreType.DMA((4,))
     for k in ("all_send", "all_recv"):
         scratch[k] = pltpu.SemaphoreType.DMA((3, ny * nz))
     for k in ("i3", "x3", "d3"):

time: 185 us -> 101 us (0.55)
  Pallas kernels: 179 us -> 94.6 us
    pallas_call x1, Pallas kernels: 179 us -> 94.6 us  [shards(): pl.pallas_call(functools.partial(cycle, ny, nz, tuple(scratch)), out_shap...]
where the time goes in v2:
time: 101 us
  Pallas kernels  94.6 us (94%)
  local copies, waits for them, and re-layouts  3.47 us (3%)
  between operations  2.46 us (2%)
    pallas_call x1, Pallas kernels, shards(): pl.pallas_call(functools.partial(cycle, ny, nz, tuple(scratch)), out_shap...  94.6 us
    unnamed x4, local copies, waits for them, and re-layouts  3.47 us

profile of v2, /device:TPU:0, one launch (start us, length us, event | category | flops | bytes accessed | tf_op | source)
XLA Modules:
  0.0 100.5 jit_solution(6756472680173901330)
XLA Ops:
  0.6 94.6 %shard_map.58 = (f32[48,48,48]{2,1,0:T(8,128)}, f32[48,48,48]{2,1,0:T(8,128)}, f32[1,1]{1,0:T(1,128)}) custom-call(f32[48,48,48]{2,1,0:T(8,128)} %refs_0_.1, f32[3,48,48,48]{3,2,1,0:T(8,128)} %refs_1_.1, f32[48,48,48]{2,1,0:T(8,128)} %refs_2_.1), custom_call_target="tpu_custom_call" | custom-call | tf_op jit(solution)/shard_map/pallas_call | solution.py:964
  95.2 0.0 copy-start
  95.2 2.5 %copy.9 = f32[48,48,48]{2,1,0:T(8,128)} copy(f32[48,48,48]{2,1,0:T(8,128)} %get-tuple-element.12) | data formatting | bytes 884736
  97.7 0.0 copy-done
  97.7 1.0 %copy.10 = f32[48,48,48]{2,1,0:T(8,128)} copy(f32[48,48,48]{2,1,0:T(8,128)S(1)} %copy-done) | data formatting | bytes 884736
Async XLA Ops:
  95.2 2.5 %copy-start = (f32[48,48,48]{2,1,0:T(8,128)S(1)}, f32[48,48,48]{2,1,0:T(8,128)}, u32[]{:S(2)}) copy-start(f32[48,48,48]{2,1,0:T(8,128)} %get-tuple-element.13) | copy-start | bytes 1327108

commit v3 on v2

--- a/solution.py
+++ b/solution.py
@@ -29,7 +29,7 @@
         self.planes = self.half + 2 * e
         self.span = 128 // ways
         self.slots, self.slots_y = self.span // width, self.span // width_y
-        self.packs, self.packs_y = -(-self.planes // self.slots), -(-self.planes // self.slots_y)
+        self.packs, self.packs_y = -(-self.half // self.slots), -(-self.half // self.slots_y)
 
 
 L0 = Level(48, 4, 2, 56, 8, 4, 64, 4)
@@ -74,66 +74,67 @@
 class Exchange:
     def __init__(self, level, first, count):
         self.level, self.first, self.count = level, first, count
+        lv = level
+        sizes = [-(-rows // 8) * 8 for rows in (lv.packs_y * lv.e, lv.packs * lv.n, lv.packs * lv.e)]
+        self.sizes = [sizes[0]] * 2 + [sizes[1]] * 2 + [sizes[2]] * 4
+        self.starts = [sum(self.sizes[:i]) for i in range(9)]
 
     def scratch(self):
         lv, na = self.level, self.count
         shapes = [
             (na, lv.e * lv.rows, 128),
-            (2, na, lv.packs_y * lv.e, 128),
-            (2, na, lv.packs_y * lv.e, 128),
-            (2, na, lv.packs * lv.n, 128),
-            (2, na, lv.packs * lv.n, 128),
-            (2, 2, na, lv.packs * lv.e, 128),
-            (2, 2, na, lv.packs * lv.e, 128),
+            (na, self.starts[8], 128),
+            (na, self.starts[8], 128),
             (2, na, lv.packs * lv.rows, 128),
         ]
-        return [pltpu.VMEM(s, F32) for s in shapes] + [pltpu.SemaphoreType.DMA((9,)), pltpu.SemaphoreType.DMA((9,))]
+        return [pltpu.VMEM(s, F32) for s in shapes] + [pltpu.SemaphoreType.DMA((2,)), pltpu.SemaphoreType.DMA((2,))]
 
     def bind(self, here, ref, scratch):
         self.here, self.ref = here, ref
-        self.xr, self.yb, self.yr, self.zb, self.zr, self.db, self.dr, self.zf, self.ssem, self.rsem = scratch
+        self.xr, self.out, self.got, self.zf, self.ssem, self.rsem = scratch
         gx, gy, gz, ny, nz = here
         lv = self.level
-        e, r = lv.e, lv.rows
-        start = e + (1 - gx) * (lv.half - e) if lv.ways == 2 else e + (1 - gx) * (lv.n - e)
-        src = ref.at[pl.ds(self.first, self.count), tile_rows(start * r, e * r), :]
-        self.copies = []
-
-        def add(src, dst, gx, gy, gz):
-            i = len(self.copies)
-            self.copies.append(
-                pltpu.make_async_remote_copy(
-                    src_ref=src,
-                    dst_ref=dst,
-                    send_sem=self.ssem.at[i],
-                    recv_sem=self.rsem.at[i],
-                    device_id=(gx, gy, gz),
-                    device_id_type=MESH,
-                )
+        start = lv.e + (1 - gx) * (lv.half - lv.e if lv.ways == 2 else lv.n - lv.e)
+
+        def copy(src, dst, i, gx, gy, gz):
+            return pltpu.make_async_remote_copy(
+                src_ref=src,
+                dst_ref=dst,
+                send_sem=self.ssem.at[i],
+                recv_sem=self.rsem.at[i],
+                device_id=(gx, gy, gz),
+                device_id_type=MESH,
             )
 
-        add(src, self.xr, 1 - gx, gy, gz)
+        src = ref.at[pl.ds(self.first, self.count), tile_rows(start * lv.rows, lv.e * lv.rows), :]
+        self.copy_x = copy(src, self.xr, 0, 1 - gx, gy, gz)
         ys = [lax.rem(gy + ny - 1, ny), lax.rem(gy + 1, ny)]
         zs = [lax.rem(gz + nz - 1, nz), lax.rem(gz + 1, nz)]
-        for s in range(2):
-            add(self.yb.at[s], self.yr.at[1 - s], gx, ys[s], gz)
-        for s in range(2):
-            for t in range(2):
-                add(self.db.at[s, t], self.dr.at[1 - s, 1 - t], gx, ys[s], zs[t])
-        for t in range(2):
-            add(self.zb.at[t], self.zr.at[1 - t], gx, gy, zs[t])
+        targets = [(ys[0], gz), (ys[1], gz), (gy, zs[0]), (gy, zs[1])] + [(y, z) for y in ys for z in zs]
+        lands = [1, 0, 3, 2, 7, 6, 5, 4]
+        self.copies = [
+            copy(
+                self.out.at[:, pl.ds(self.starts[i], self.sizes[i]), :],
+                self.got.at[:, pl.ds(self.starts[lands[i]], self.sizes[i]), :],
+                1,
+                gx,
+                *targets[i],
+            )
+            for i in range(8)
+        ]
+        self.all = copy(self.out, self.got, 1, gx, *targets[0])
         self.has_y = [jnp.where(gy > 0, 1.0, 0.0).astype(F32), jnp.where(gy < ny - 1, 1.0, 0.0).astype(F32)]
         self.has_z = [jnp.where(gz > 0, 1.0, 0.0).astype(F32), jnp.where(gz < nz - 1, 1.0, 0.0).astype(F32)]
         self.has_x = [gx.astype(F32), (1 - gx).astype(F32)]
         return self
 
     def start_x(self):
-        self.copies[0].start()
+        self.copy_x.start()
 
     def finish_x(self):
         lv, ref = self.level, self.ref
         e, r = lv.e, lv.rows
-        self.copies[0].wait()
+        self.copy_x.wait()
         low = lanes(r) < 64
 
         def finish(a, j):
@@ -161,99 +162,97 @@
         lv = self.level
         slot = (lanes(rows) % lv.span) // width
         slots = lv.span // width
-        for k in range(-(-lv.planes // slots)):
+        for k in range(-(-lv.half // slots)):
             acc = None
-            for s in range(min(slots, lv.planes - k * slots)):
-                moved = [roll_lanes(value, s * width - shift) for value, shift in zip(plane(k * slots + s), shifts)]
+            for s in range(min(slots, lv.half - k * slots)):
+                moved = [roll_lanes(v, s * width - shift) for v, shift in zip(plane(lv.e + k * slots + s), shifts)]
                 acc = moved if s == 0 else [jnp.where(slot == s, new, old) for new, old in zip(moved, acc)]
             put(k, acc)
 
-    def start_yz(self):
+    def pack_yz(self, send):
         lv, ref = self.level, self.ref
         r, n, e, zo = lv.rows, lv.n, lv.e, lv.zo
         z_shifts = (zo, zo + n - e)
 
-        def pack_y(a, carry):
+        def put_at(first, rows, a):
+            def put(k, values):
+                for i, value in enumerate(values):
+                    self.out[a, pl.ds(self.starts[first + i] + k * rows, rows), :] = value
+
+            return put
+
+        def edges(a, p):
+            return [ref[self.first + a, pl.ds(p * r + row, e), :] for row in (e, n)]
+
+        def pack_d(a, carry):
             def plane(p):
-                return [ref[self.first + a, pl.ds(p * r + row, e), :] for row in (e, n)]
-
-            def put(k, values):
-                for s in range(2):
-                    self.yb[s, a, pl.ds(k * e, e), :] = values[s]
-
-            if lv.slots_y == 1:
-                for p in range(lv.planes):
-                    put(p, plane(p))
-            else:
-                self.pack(plane, e, lv.width_y, (zo, zo), put)
+                low, high = edges(a, p)
+                return low, low, high, high
+
+            self.pack(plane, e, lv.width, z_shifts * 2, put_at(4, e, a))
             return carry
-
-        lax.fori_loop(0, self.count, pack_y, 0)
-        self.copies[1].start()
-        self.copies[2].start()
 
         def pack_z(a, carry):
             def plane(p):
                 return [ref[self.first + a, pl.ds(p * r + e, n), :]] * 2
 
-            def put(k, values):
-                for t in range(2):
-                    self.zb[t, a, pl.ds(k * n, n), :] = values[t]
-
-            self.pack(plane, n, lv.width, z_shifts, put)
+            self.pack(plane, n, lv.width, z_shifts, put_at(2, n, a))
             return carry
 
-        lax.fori_loop(0, self.count, pack_z, 0)
-        self.copies[7].start()
-        self.copies[8].start()
-
-        def pack_d(a, carry):
-            def plane(p):
-                low, high = (ref[self.first + a, pl.ds(p * r + row, e), :] for row in (e, n))
-                return low, low, high, high
-
-            def put(k, values):
-                for i in range(4):
-                    self.db[i // 2, i % 2, a, pl.ds(k * e, e), :] = values[i]
-
-            self.pack(plane, e, lv.width, z_shifts * 2, put)
+        def pack_y(a, carry):
+            if lv.slots_y == 1:
+                for k in range(lv.half):
+                    put_at(0, e, a)(k, edges(a, e + k))
+            else:
+                self.pack(lambda p: edges(a, p), e, lv.width_y, (zo, zo), put_at(0, e, a))
             return carry
 
-        lax.fori_loop(0, self.count, pack_d, 0)
-        for i in range(3, 7):
+        for body, which in ((pack_d, range(4, 8)), (pack_z, (2, 3)), (pack_y, (0, 1))):
+            lax.fori_loop(0, self.count, body, 0)
+            if send:
+                for i in which:
+                    self.copies[i].start()
+
+    def send_yz(self):
+        for i in (4, 5, 6, 7, 2, 3, 0, 1):
             self.copies[i].start()
+
+    def start_yz(self):
+        self.pack_yz(True)
 
     def finish_yz(self):
         lv, ref = self.level, self.ref
         r, n, e, zo = lv.rows, lv.n, lv.e, lv.zo
-        for i in range(1, 9):
-            with jax.named_scope("copy" + str(i)):
-                self.copies[i].wait()
+        with jax.named_scope("arrive"):
+            self.all.wait()
         lane = lanes(r) % lv.span
         at_low = (lane >= zo - e) & (lane < zo)
         at_high = (lane >= zo + n) & (lane < zo + n + e)
 
         def unpack(a, carry):
+            def got(i, row, rows):
+                return self.got[a, pl.ds(self.starts[i] + row, rows), :]
+
             for s in range(2):
                 for k in range(lv.packs_y):
-                    got = self.yr[s, a, pl.ds(k * e, e), :] * self.has_y[s]
-                    for slot in range(min(lv.slots_y, lv.planes - k * lv.slots_y)):
-                        row = (k * lv.slots_y + slot) * r + (e + n) * s
-                        moved = roll_lanes(got, zo - slot * lv.width_y) if lv.slots_y > 1 else got
+                    value = got(s, k * e, e) * self.has_y[s]
+                    for slot in range(min(lv.slots_y, lv.half - k * lv.slots_y)):
+                        row = (e + k * lv.slots_y + slot) * r + (e + n) * s
+                        moved = roll_lanes(value, zo - slot * lv.width_y) if lv.slots_y > 1 else value
                         ref[self.first + a, pl.ds(row, e), :] = moved
             for k in range(lv.packs):
                 for t in range(2):
-                    self.zf[t, a, pl.ds(k * r + e, n), :] = self.zr[t, a, pl.ds(k * n, n), :] * self.has_z[t]
+                    self.zf[t, a, pl.ds(k * r + e, n), :] = got(2 + t, k * n, n) * self.has_z[t]
                     for s in range(2):
                         both = self.has_y[s] * self.has_z[t]
-                        self.zf[t, a, pl.ds(k * r + (e + n) * s, e), :] = self.dr[s, t, a, pl.ds(k * e, e), :] * both
+                        self.zf[t, a, pl.ds(k * r + (e + n) * s, e), :] = got(4 + 2 * s + t, k * e, e) * both
             for k in range(lv.packs):
-                got = [self.zf[t, a, pl.ds(k * r, r), :] for t in range(2)]
-                for s in range(min(lv.slots, lv.planes - k * lv.slots)):
-                    p = k * lv.slots + s
+                sides = [self.zf[t, a, pl.ds(k * r, r), :] for t in range(2)]
+                for s in range(min(lv.slots, lv.half - k * lv.slots)):
+                    p = e + k * lv.slots + s
                     value = ref[self.first + a, pl.ds(p * r, r), :]
-                    value = jnp.where(at_low, roll_lanes(got[0], zo - e - s * lv.width), value)
-                    value = jnp.where(at_high, roll_lanes(got[1], zo + n - s * lv.width), value)
+                    value = jnp.where(at_low, roll_lanes(sides[0], zo - e - s * lv.width), value)
+                    value = jnp.where(at_high, roll_lanes(sides[1], zo + n - s * lv.width), value)
                     ref[self.first + a, pl.ds(p * r, r), :] = value
             return carry
 
@@ -496,11 +495,7 @@
     return value
 
 
-def coarse_solve(ny, gathered, source, inverse, bottom, xs, ds):
-    nz = 16
-    fields = lambda a, g: gathered[g, :, a].reshape(128, 128)
-    f = lambda g: source[g].reshape(128, 128)
-
+def coarse_solve(ny, fields, f, inverse, bottom, xs, ds):
     def load(ref):
         return [ref[g] for g in range(ny)]
 
@@ -559,8 +554,7 @@
             xs[g] = xs[g] + update
 
 
-def coarse_fields(ny, gathered, bottom):
-    fields = lambda a, g: gathered[g, :, a].reshape(128, 128)
+def coarse_fields(ny, fields, bottom):
     rows = lax.broadcasted_iota(jnp.int32, (128, 128), 0)
     lane = lanes(128)
     even = (rows % 2 == 0) & (lane % 2 == 0) & ((lane // 6) % 2 == 0) & (lane < 72)
@@ -635,7 +629,7 @@
     ex = {k: Exchange(*v) for k, v in EXCHANGES.items()}
     targets = {"e0": f0, "c1": f1, "c2": f2, "e1": f1, "e2": f2, "x0": s["x0a"], "x1": s["x1a"], "x2": s["x2a"]}
     for k, target in targets.items():
-        ex[k].bind(here, target, [s[k + str(i)] for i in range(10)])
+        ex[k].bind(here, target, [s[k + str(i)] for i in range(6)])
 
     def partner(src, dst, i):
         return pltpu.make_async_remote_copy(
@@ -647,28 +641,27 @@
             device_id_type=MESH,
         )
 
-    def spread(src, slot, i):
-        def one(t, y, z):
-            oy, oz = other(t)
+    me = gy * nz + gz
+
+    def spread(src, whole, part, i):
+        def copy(src, dst, oy, oz):
             return pltpu.make_async_remote_copy(
                 src_ref=src,
-                dst_ref=slot(y, z),
-                send_sem=s["all_send"].at[i, t],
-                recv_sem=s["all_recv"].at[i, t],
+                dst_ref=dst,
+                send_sem=s["all_send"].at[i],
+                recv_sem=s["all_recv"].at[i],
                 device_id=(gx, oy, oz),
                 device_id_type=MESH,
             )
 
         def start():
             for t in order:
-                one(t, gy, gz).start()
+                copy(src, part(whole.at[me]), *other(t)).start()
 
         def finish():
-            def body(t, carry):
-                one(t, lax.rem(gy + ny - t // nz, ny), lax.rem(gz + nz - t % nz, nz)).wait()
-                return carry
-
-            lax.fori_loop(1, ny * nz, body, 0)
+            most = whole.at[pl.ds(0, ny * nz - 1)]
+            most = most.at[:, pl.ds(0, 2)] if i == 0 else most
+            copy(most, most, *other(1)).wait()
 
         return start, finish
 
@@ -694,19 +687,19 @@
         with scope("layout"):
             loop(0, 24, load, 0, 6)
 
+    with scope("e0_pack"):
+        ex["e0"].pack_yz(False)
     with scope("barrier"):
         pl.semaphore_wait(barrier, ny * nz)
-    ex["e0"].start_x()
+    ex["e0"].send_yz()
     with scope("coarsen_0"):
         coarsen_fields(L0, L1, f0, fields_put(L1, f1))
-    ex["c1"].start_x()
-    with scope("e0_finish_x"):
-        ex["e0"].finish_x()
-    with scope("e0_start_yz"):
-        ex["e0"].start_yz()
+    with scope("c1_start_yz"):
+        ex["c1"].start_yz()
     with scope("coarsen_1"):
         coarsen_fields(L1, L2, f1, fields_put(L2, f2))
-    ex["c2"].start_x()
+    with scope("c2_start_yz"):
+        ex["c2"].start_yz()
     with scope("coarsen_2"):
         coarsen_fields(L2, None, f2, block_put)
 
@@ -725,74 +718,76 @@
 
     with scope("square"):
         squares = loop(0, 24, square, jnp.zeros((48, 128), F32), 4)
-    with scope("c1_finish_x"):
-        ex["c1"].finish_x()
-    with scope("c1_start_yz"):
-        ex["c1"].start_yz()
-    with scope("c2_finish_x"):
-        ex["c2"].finish_x()
-    with scope("c2_start_yz"):
-        ex["c2"].start_yz()
+    with scope("e0_finish_yz"):
+        ex["e0"].finish_yz()
+    ex["e0"].start_x()
     g4, g1, gn = s["g4"], s["g1"], s["gn"]
     with scope("pair_coef"):
         pair_coef.wait()
     merged = s["merged4"]
     merged[...] = own4[...] + pair4[...]
     mine = pl.ds(2 * gx, 2)
-    g4[gy, gz, mine] = merged[mine]
-    coef_start, coef_finish = spread(merged.at[mine], lambda y, z: g4.at[y, z, mine], 0)
+    g4[me, mine] = merged[mine]
+    coef_start, coef_finish = spread(merged.at[mine], g4, lambda slot: slot.at[mine], 0)
     with scope("coef_start"):
         coef_start()
-    with scope("e0_finish_yz"):
-        ex["e0"].finish_yz()
+    with scope("e0_finish_x"):
+        ex["e0"].finish_x()
     with scope("scaling_0"):
         scaling(L0, f0, s["i0"], s["u0"], 3)
     with scope("smooth_0"):
         smooth_from_zero(L0, f0, s["i0"], s["u0"], s["x0a"], s["x0b"], s["d0"], 3)
     with scope("restrict_0"):
         restrict(L0, L1, f0, s["u0"], s["x0a"], s["sums"], fields_put(L1, f1))
-    ex["e1"].start_x()
+    with scope("e1_start_yz"):
+        ex["e1"].start_yz()
     with scope("c1_finish_yz"):
         ex["c1"].finish_yz()
+    ex["c1"].start_x()
+    with scope("x0_start_yz"):
+        ex["x0"].start_yz()
+    with scope("c1_finish_x"):
+        ex["c1"].finish_x()
+    with scope("scaling_1"):
+        scaling(L1, f1, s["i1"], s["u1"], 4)
+    with scope("e1_finish_yz"):
+        ex["e1"].finish_yz()
+    ex["e1"].start_x()
+    with scope("c2_finish_yz"):
+        ex["c2"].finish_yz()
     with scope("e1_finish_x"):
         ex["e1"].finish_x()
-    with scope("e1_start_yz"):
-        ex["e1"].start_yz()
-    ex["x0"].start_x()
-    with scope("c2_finish_yz"):
-        ex["c2"].finish_yz()
-    with scope("scaling_12"):
-        scaling(L1, f1, s["i1"], s["u1"], 4)
-        scaling(L2, f2, s["i2"], s["u2"], 5)
-    with scope("e1_finish_yz"):
-        ex["e1"].finish_yz()
     with scope("smooth_1"):
         smooth_from_zero(L1, f1, s["i1"], s["u1"], s["x1a"], s["x1b"], s["d1"], 3)
     with scope("restrict_1"):
         restrict(L1, L2, f1, s["u1"], s["x1a"], s["sums"], fields_put(L2, f2))
-    ex["e2"].start_x()
-    ex["x1"].start_x()
-    with scope("x0_finish_x"):
-        ex["x0"].finish_x()
-    with scope("e2_finish_x"):
-        ex["e2"].finish_x()
     with scope("e2_start_yz"):
         ex["e2"].start_yz()
+    ex["c2"].start_x()
+    with scope("x1_start_yz"):
+        ex["x1"].start_yz()
+    with scope("c2_finish_x"):
+        ex["c2"].finish_x()
+    with scope("scaling_2"):
+        scaling(L2, f2, s["i2"], s["u2"], 5)
     with scope("coef_finish"):
         coef_finish()
     other_half = pltpu.make_async_remote_copy(
-        src_ref=g4.at[:, :, mine],
-        dst_ref=g4.at[:, :, mine],
+        src_ref=g4.at[:, mine],
+        dst_ref=g4.at[:, mine],
         send_sem=s["pair_send"].at[3],
         recv_sem=s["pair_recv"].at[3],
         device_id=(1 - gx, gy, gz),
         device_id_type=MESH,
     )
-    other_half.start()
-    with scope("x0_start_yz"):
-        ex["x0"].start_yz()
     with scope("e2_finish_yz"):
         ex["e2"].finish_yz()
+    ex["e2"].start_x()
+    other_half.start()
+    with scope("x0_finish_yz"):
+        ex["x0"].finish_yz()
+    with scope("e2_finish_x"):
+        ex["e2"].finish_x()
     with scope("smooth_2"):
         smooth_from_zero(L2, f2, s["i2"], s["u2"], s["x2a"], s["x2b"], s["d2"], 3)
     with scope("restrict_2"):
@@ -800,40 +795,40 @@
     own1[...] = tile_of(4)
     pair_source = partner(own1, pair1, 1)
     pair_source.start()
-    ex["x2"].start_x()
-    with scope("other_half"):
-        other_half.wait()
+    ex["x0"].start_x()
+    with scope("x2_start_yz"):
+        ex["x2"].start_yz()
     with scope("pair_source"):
         pair_source.wait()
     s["merged1"][...] = own1[...] + pair1[...]
-    g1[gy, gz] = s["merged1"][...]
-    source_start, source_finish = spread(s["merged1"], lambda y, z: g1.at[y, z], 1)
+    g1[me] = s["merged1"][...]
+    source_start, source_finish = spread(s["merged1"], g1, lambda slot: slot, 1)
     with scope("source_start"):
         source_start()
-    gathered = lambda a, g: g4[g, :, a].reshape(128, 128)
+    with scope("other_half"):
+        other_half.wait()
+    gathered = lambda a, g: g4[pl.ds(g * nz, nz), a].reshape(128, 128)
     with scope("coarse_fields"):
         inverse = whole_inverse(ny, gathered)
         for g in range(ny):
             s["i3"][g] = inverse[g]
-        coarse_fields(ny, g4, s["bottom"])
+        coarse_fields(ny, gathered, s["bottom"])
     with scope("hidden"):
+        ex["x1"].finish_yz()
+        ex["x1"].start_x()
+        ex["x0"].finish_x()
+        ex["x2"].finish_yz()
+        ex["x2"].start_x()
         ex["x1"].finish_x()
-        ex["x1"].start_yz()
         ex["x2"].finish_x()
-        ex["x2"].start_yz()
-        ex["x0"].finish_yz()
     with scope("source_finish"):
         source_finish()
     with scope("coarse_solve"):
-        coarse_solve(ny, g4, g1, s["i3"], s["bottom"], s["x3"], s["d3"])
-    with scope("x2_finish_yz"):
-        ex["x2"].finish_yz()
+        coarse_solve(ny, gathered, lambda g: g1[pl.ds(g * nz, nz)].reshape(128, 128), s["i3"], s["bottom"], s["x3"], s["d3"])
     with scope("window"):
         window(L2, gx, gy, gz, ny, s["x3"], s["padded"], s["turned"], s["corner"], s["x2a"])
     with scope("post_2"):
         smooth(L2, f2, s["i2"], s["u2"], s["x2a"], s["x2b"], s["d2"], 6)
-    with scope("x1_finish_yz"):
-        ex["x1"].finish_yz()
     with scope("prolong_1"):
         prolong(L1, L2, s["x2b"], s["x1a"], 3)
     with scope("post_1"):
@@ -889,8 +884,8 @@
     with scope("pair_norm"):
         pair_norm.wait()
     s["merged_n"][...] = jnp.where(gx == 0, own_n[...] + pair_n[...], pair_n[...] + own_n[...])
-    gn[gy, gz] = s["merged_n"][...]
-    norm_start, norm_finish = spread(s["merged_n"], lambda y, z: gn.at[y, z], 2)
+    gn[me] = s["merged_n"][...]
+    norm_start, norm_finish = spread(s["merged_n"], gn, lambda slot: slot, 2)
     with scope("norm_start"):
         norm_start()
     with scope("unload_residual"):
@@ -899,7 +894,7 @@
     out1.start()
     with scope("norm_finish"):
         norm_finish()
-    all_n = jnp.sum(gn[...].reshape(ny * nz, 8, 128), axis=0)
+    all_n = jnp.sum(gn[...], axis=0)
     sums = jnp.sum(all_n, axis=1, keepdims=True)
     norm = jnp.sqrt(sums[1:2] / sums[0:1])
     norm_out[0, 0] = norm[0, 0]
@@ -936,13 +931,13 @@
         scratch[k] = vmem(4, 8, 128)
     for k in ("own1", "pair1", "merged1", "own_n", "pair_n", "merged_n"):
         scratch[k] = vmem(8, 128)
-    scratch["g4"] = vmem(ny, nz, 4, 8, 128)
-    scratch["g1"] = vmem(ny, nz, 8, 128)
-    scratch["gn"] = vmem(ny, nz, 8, 128)
+    scratch["g4"] = vmem(ny * nz, 4, 8, 128)
+    scratch["g1"] = vmem(ny * nz, 8, 128)
+    scratch["gn"] = vmem(ny * nz, 8, 128)
     for k in ("pair_send", "pair_recv"):
         scratch[k] = pltpu.SemaphoreType.DMA((4,))
     for k in ("all_send", "all_recv"):
-        scratch[k] = pltpu.SemaphoreType.DMA((3, ny * nz))
+        scratch[k] = pltpu.SemaphoreType.DMA((3,))
     for k in ("i3", "x3", "d3"):
         scratch[k] = vmem(ny, 128, 128)
     scratch["bottom"] = vmem(4, ny, 128, 128)

time: 101 us -> 90 us (0.89)
  Pallas kernels: 94.6 us -> 83.8 us
    pallas_call x1, Pallas kernels: 94.6 us -> 83.8 us  [shards(): pl.pallas_call(functools.partial(cycle, ny, nz, tuple(scratch)), out_shap...]
where the time goes in v3:
time: 90 us; the launch traced here: 89.8 us
  Pallas kernels  83.8 us (93%)
  local copies, waits for them, and re-layouts  3.47 us (4%)
  between operations  2.46 us (3%)
    pallas_call x1, Pallas kernels, shards(): pl.pallas_call(functools.partial(cycle, ny, nz, tuple(scratch)), out_shap...  83.8 us
    unnamed x4, local copies, waits for them, and re-layouts  3.47 us

profile of v3, /device:TPU:0, one launch (start us, length us, event | category | flops | bytes accessed | tf_op | source)
XLA Modules:
  0.0 89.8 jit_solution(6828738841852279301)
XLA Ops:
  0.6 83.8 %shard_map.58 = (f32[48,48,48]{2,1,0:T(8,128)}, f32[48,48,48]{2,1,0:T(8,128)}, f32[1,1]{1,0:T(1,128)}) custom-call(f32[48,48,48]{2,1,0:T(8,128)} %refs_0_.1, f32[3,48,48,48]{3,2,1,0:T(8,128)} %refs_1_.1, f32[48,48,48]{2,1,0:T(8,128)} %refs_2_.1), custom_call_target="tpu_custom_call" | custom-call | tf_op jit(solution)/shard_map/pallas_call | solution.py:959
  84.5 0.0 copy-start
  84.5 2.5 %copy.9 = f32[48,48,48]{2,1,0:T(8,128)} copy(f32[48,48,48]{2,1,0:T(8,128)} %get-tuple-element.12) | data formatting | bytes 884736
  86.9 0.0 copy-done
  86.9 1.0 %copy.10 = f32[48,48,48]{2,1,0:T(8,128)} copy(f32[48,48,48]{2,1,0:T(8,128)S(1)} %copy-done) | data formatting | bytes 884736
Async XLA Ops:
  84.5 2.5 %copy-start = (f32[48,48,48]{2,1,0:T(8,128)S(1)}, f32[48,48,48]{2,1,0:T(8,128)}, u32[]{:S(2)}) copy-start(f32[48,48,48]{2,1,0:T(8,128)} %get-tuple-element.13) | copy-start | bytes 1327108

commit v4 on v3

--- a/solution.py
+++ b/solution.py
@@ -85,13 +85,14 @@
             (na, lv.e * lv.rows, 128),
             (na, self.starts[8], 128),
             (na, self.starts[8], 128),
+            (na, self.starts[8], 128),
             (2, na, lv.packs * lv.rows, 128),
         ]
         return [pltpu.VMEM(s, F32) for s in shapes] + [pltpu.SemaphoreType.DMA((2,)), pltpu.SemaphoreType.DMA((2,))]
 
     def bind(self, here, ref, scratch):
         self.here, self.ref = here, ref
-        self.xr, self.out, self.got, self.zf, self.ssem, self.rsem = scratch
+        self.xr, self.out, self.got, self.spare, self.zf, self.ssem, self.rsem = scratch
         gx, gy, gz, ny, nz = here
         lv = self.level
         start = lv.e + (1 - gx) * (lv.half - lv.e if lv.ways == 2 else lv.n - lv.e)
@@ -122,11 +123,25 @@
             )
             for i in range(8)
         ]
+        y_side, z_side = [gy > 0, gy < ny - 1], [gz > 0, gz < nz - 1]
+        self.exists = y_side + z_side + [a & b for a in y_side for b in z_side]
         self.all = copy(self.out, self.got, 1, gx, *targets[0])
         self.has_y = [jnp.where(gy > 0, 1.0, 0.0).astype(F32), jnp.where(gy < ny - 1, 1.0, 0.0).astype(F32)]
         self.has_z = [jnp.where(gz > 0, 1.0, 0.0).astype(F32), jnp.where(gz < nz - 1, 1.0, 0.0).astype(F32)]
         self.has_x = [gx.astype(F32), (1 - gx).astype(F32)]
         return self
+
+    def send(self, i):
+        part = (slice(None), pl.ds(self.starts[i], self.sizes[i]), slice(None))
+
+        @pl.when(self.exists[i])
+        def _():
+            self.copies[i].start()
+
+        @pl.when(jnp.logical_not(self.exists[i]))
+        def _():
+            pltpu.make_async_copy(self.out.at[part], self.got.at[part], self.rsem.at[1]).start()
+            pltpu.make_async_copy(self.out.at[part], self.spare.at[part], self.ssem.at[1]).start()
 
     def start_x(self):
         self.copy_x.start()
@@ -148,12 +163,15 @@
             else:
                 below = got * self.has_x[0]
                 above = got * self.has_x[1]
-            ref[self.first + a, tile_rows(j * r, r), :] = below
-            ref[self.first + a, tile_rows((e + lv.half + j) * r, r), :] = above
+            return below, above
 
         def body(a, carry):
-            for j in range(e):
-                finish(a, j)
+            for first in range(0, e, 2):
+                planes = range(first, min(first + 2, e))
+                values = [finish(a, j) for j in planes]
+                for j, (below, above) in zip(planes, values):
+                    ref[self.first + a, tile_rows(j * r, r), :] = below
+                    ref[self.first + a, tile_rows((e + lv.half + j) * r, r), :] = above
             return carry
 
         lax.fori_loop(0, self.count, body, 0)
@@ -211,11 +229,11 @@
             lax.fori_loop(0, self.count, body, 0)
             if send:
                 for i in which:
-                    self.copies[i].start()
+                    self.send(i)
 
     def send_yz(self):
         for i in (4, 5, 6, 7, 2, 3, 0, 1):
-            self.copies[i].start()
+            self.send(i)
 
     def start_yz(self):
         self.pack_yz(True)
@@ -248,12 +266,16 @@
                         self.zf[t, a, pl.ds(k * r + (e + n) * s, e), :] = got(4 + 2 * s + t, k * e, e) * both
             for k in range(lv.packs):
                 sides = [self.zf[t, a, pl.ds(k * r, r), :] for t in range(2)]
-                for s in range(min(lv.slots, lv.half - k * lv.slots)):
-                    p = e + k * lv.slots + s
-                    value = ref[self.first + a, pl.ds(p * r, r), :]
-                    value = jnp.where(at_low, roll_lanes(sides[0], zo - e - s * lv.width), value)
-                    value = jnp.where(at_high, roll_lanes(sides[1], zo + n - s * lv.width), value)
-                    ref[self.first + a, pl.ds(p * r, r), :] = value
+                count = min(lv.slots, lv.half - k * lv.slots)
+                for first in range(0, count, 4):
+                    slots = range(first, min(first + 4, count))
+                    values = []
+                    for s in slots:
+                        value = ref[self.first + a, pl.ds((e + k * lv.slots + s) * r, r), :]
+                        value = jnp.where(at_low, roll_lanes(sides[0], zo - e - s * lv.width), value)
+                        values.append(jnp.where(at_high, roll_lanes(sides[1], zo + n - s * lv.width), value))
+                    for s, value in zip(slots, values):
+                        ref[self.first + a, pl.ds((e + k * lv.slots + s) * r, r), :] = value
             return carry
 
         lax.fori_loop(0, self.count, unpack, 0)
@@ -441,48 +463,47 @@
     loop(0, lv.half // 2 + 2 * reach, body, 0, 4)
 
 
-def whole_operator(ny, fields, v, scale):
-    rows = lax.broadcasted_iota(jnp.int32, (128, 128), 0)
-    z, y = rows % 8, lanes(128) % 6
-    last = 6 - scale
-    y_low, y_high, z_low, z_high = y == 0, y == last, z == 0, z == last
-    bottom, top = rows == 0, rows == 120 + last
-    zero = jnp.zeros((128, 128), F32)
-
-    def below_y(g):
-        other = roll_lanes(v[g - 1], -last) if g else zero
-        return jnp.where(y_low, other, roll_lanes(v[g], scale))
-
-    fluxes_y = [fields(1, g) * (v[g] - below_y(g)) for g in range(ny)]
+PAD = 8
+
+
+def row_of(rows):
+    return lax.broadcasted_iota(jnp.int32, (rows, 128), 0)
+
+
+def whole_neighbours(ny, value, rows):
+    z, y = row_of(128) % 8, lanes(128) % 6
     out = []
     for g in range(ny):
-        flux = fields(0, g) * (v[g] - roll_lanes(v[g], 6 * scale))
-        total = flux - roll_lanes(flux, -6 * scale)
-        other = roll_lanes(fluxes_y[g + 1], last) if g + 1 < ny else zero
-        total = total + (fluxes_y[g] - jnp.where(y_high, other, roll_lanes(fluxes_y[g], -scale)))
-        jump = 8 - last
-        other = jnp.where(bottom, 0.0, roll_rows(v[g], jump))
-        flux = fields(2, g) * (v[g] - jnp.where(z_low, other, roll_rows(v[g], scale)))
-        other = jnp.where(top, 0.0, roll_rows(flux, -jump))
-        total = total + (flux - jnp.where(z_high, other, roll_rows(flux, -scale)))
-        out.append(fields(3, g) * v[g] + total)
+        here = value(g)
+        low_y, high_y = roll_lanes(here, 1), roll_lanes(here, -1)
+        if g:
+            low_y = jnp.where(y == 0, roll_lanes(value(g - 1), -5), low_y)
+        if g + 1 < ny:
+            high_y = jnp.where(y == 5, roll_lanes(value(g + 1), 5), high_y)
+        low_z = jnp.where(z == 0, rows(g, -3), rows(g, -1))
+        high_z = jnp.where(z == 5, rows(g, 3), rows(g, 1))
+        out.append((roll_lanes(here, 6), roll_lanes(here, -6), low_y, high_y, low_z, high_z))
     return out
 
 
-def whole_inverse(ny, fields):
-    rows = lax.broadcasted_iota(jnp.int32, (128, 128), 0)
-    z, y = rows % 8, lanes(128) % 6
-    zero = jnp.zeros((128, 128), F32)
-    out = []
+def whole_prepare(ny, fields, coefs, diagonal, inverse):
+    z, y, row = row_of(128) % 8, lanes(128) % 6, row_of(128)
+    moved = lambda a: whole_neighbours(ny, lambda g: fields(a, g), lambda g, d: roll_rows(fields(a, g), -d))
+    high = [[near[1] for near in moved(0)], [near[3] for near in moved(1)], [near[5] for near in moved(2)]]
     for g in range(ny):
-        face_x, face_y, face_z, cells = (fields(a, g) for a in range(4))
-        total = cells + face_x + roll_lanes(face_x, -6)
-        other = roll_lanes(fields(1, g + 1), 5) if g + 1 < ny else zero
-        total = total + face_y + jnp.where(y == 5, other, roll_lanes(face_y, -1))
-        other = jnp.where(rows == 125, 0.0, roll_rows(face_z, -3))
-        total = total + face_z + jnp.where(z == 5, other, roll_rows(face_z, -1))
-        out.append(jnp.where(cells > 0.0, 1.0 / total, 0.0))
-    return out
+        inside = fields(3, g) > 0.0
+        high_y = jnp.where(y == 5, 0.0, high[1][g]) if g + 1 == ny else high[1][g]
+        high_z = jnp.where(row == 125, 0.0, high[2][g])
+        sides = [fields(0, g), high[0][g], fields(1, g), high_y, fields(2, g), high_z]
+        total = functools.reduce(lambda a, b: a + b, sides) + fields(3, g)
+        scale = jnp.where(inside, 1.0 / total, 0.0)
+        diagonal[g] = jnp.where(inside, total, 0.0)
+        inverse[g] = scale
+        if g == 0:
+            sides[2] = jnp.where(y == 0, 0.0, sides[2])
+        sides[4] = jnp.where(row == 0, 0.0, sides[4])
+        for i in range(6):
+            coefs[i, g] = sides[i] * scale
 
 
 def children(value, axes):
@@ -495,80 +516,124 @@
     return value
 
 
-def coarse_solve(ny, fields, f, inverse, bottom, xs, ds):
-    def load(ref):
-        return [ref[g] for g in range(ny)]
-
-    def residual(v):
-        applied = whole_operator(ny, fields, v, 1)
-        return [f(g) - applied[g] for g in range(ny)]
-
+def even_cells():
+    row, lane = row_of(128), lanes(128)
+    return (row % 2 == 0) & (row % 8 < 6) & (lane % 2 == 0) & ((lane // 6) % 2 == 0) & (lane < 72)
+
+
+def fold_level(values):
+    even = even_cells()
+    values = [jnp.where(even, v, 0.0) for v in values]
+    both = (values[0] + roll_lanes(values[1], 1)) + (roll_lanes(values[2], 6) + roll_lanes(values[3], 7))
+    return both[0:64] + roll_rows(both[64:128], 1)
+
+
+def unfold_level(value):
+    both = jnp.concatenate([value, roll_rows(value, -1)], axis=0)
+    even = even_cells()
+    return [jnp.where(even, roll_lanes(both, -shift), 0.0) for shift in (0, 1, 6, 7)]
+
+
+def bottom_neighbours(v):
+    row, lane = row_of(64), lanes(64)
+    z, y = (row % 8) // 2, (lane % 6) // 2
+    odd = lane % 2 == 1
+    low_y = jnp.where(y > 0, roll_lanes(v, 2), jnp.where(odd, roll_lanes(v, -3), roll_lanes(v, 1)))
+    high_y = jnp.where(y < 2, roll_lanes(v, -2), jnp.where(odd, roll_lanes(v, -1), roll_lanes(v, 3)))
+    low_z = jnp.where(z > 0, roll_rows(v, 2), jnp.where(row == 1, roll_rows(v, 5), roll_rows(v, 4)))
+    high_z = jnp.where(z < 2, roll_rows(v, -2), jnp.where(row == 60, roll_rows(v, -5), roll_rows(v, -4)))
+    return roll_lanes(v, 12), roll_lanes(v, -12), low_y, high_y, low_z, high_z
+
+
+def bottom_prepare(ny, fields, bottom):
+    row, lane = row_of(64), lanes(64)
+    y = (lane % 6) // 2
+    first = (lane % 2 == 0) & ((lane // 6) % 2 == 0)
+    last = (lane % 2 == 1) & ((lane // 6) % 2 == 1)
+    faces = []
+    for a, axes in enumerate(("yz", "xz", "xy", "xyz")):
+        factor = 0.125 if a == 3 else 0.0625
+        faces.append(fold_level([children(fields(a, g), axes) * factor for g in range(ny)]))
+    inside = faces[3] > 0.0
+    high_x = bottom_neighbours(faces[0])[1]
+    high_y = jnp.where(last & (y == 2), 0.0, bottom_neighbours(faces[1])[3])
+    high_z = jnp.where(row == 61, 0.0, bottom_neighbours(faces[2])[5])
+    sides = [faces[0], high_x, faces[1], high_y, faces[2], high_z]
+    total = functools.reduce(lambda a, b: a + b, sides) + faces[3]
+    sides[2] = jnp.where(first & (y == 0), 0.0, sides[2])
+    sides[4] = jnp.where(row == 0, 0.0, sides[4])
+    for i, value in enumerate(sides + [total]):
+        bottom[i] = jnp.where(inside, value, 0.0)
+
+
+def coarse_solve(ny, coefs, diagonal, inverse, f, bottom, xa, xb, ds, g3):
+    def rows(x, g, offset=0):
+        return x[g, pl.ds(PAD + offset, 128)]
+
+    def scaled(x):
+        near = whole_neighbours(ny, lambda g: rows(x, g), lambda g, d: rows(x, g, d))
+        out = []
+        for g in range(ny):
+            parts = [coefs[i, g] * near[g][i] for i in range(6)]
+            total = ((parts[0] + parts[1]) + (parts[2] + parts[3])) + (parts[4] + parts[5])
+            out.append((g3[g] - rows(x, g)) + total)
+        return out
+
+    def advance(x, to, coef, first, keep=True):
+        for g, value in enumerate(scaled(x)):
+            update = value * (1.0 / THETA) if first else coef[0] * ds[g] + coef[1] * value
+            if keep:
+                ds[g] = update
+            to[g, pl.ds(PAD, 128)] = rows(x, g) + update
+
+    for x in (xa, xb):
+        for g in range(ny):
+            x[g, pl.ds(0, PAD)] = jnp.zeros((PAD, 128), F32)
+            x[g, pl.ds(PAD + 128, PAD)] = jnp.zeros((PAD, 128), F32)
     for g in range(ny):
-        xs[g] = inverse[g] * f(g) * (1.0 / THETA)
-        ds[g] = xs[g]
-    for coefs in (STEP1, STEP2):
-        remainder = residual(load(xs))
-        for g in range(ny):
-            update = coefs[0] * ds[g] + coefs[1] * (inverse[g] * remainder[g])
-            ds[g] = update
-            xs[g] = xs[g] + update
-    remainder = residual(load(xs))
-    inside = lambda g, value: jnp.where(bottom[3, g] > 0.0, value, 0.0)
-    r = [inside(g, children(remainder[g], "xyz") * 0.125) for g in range(ny)]
-
-    def total(values):
-        values = functools.reduce(lambda a, b: a + b, values)
-        return jnp.sum(jnp.sum(values, axis=0, keepdims=True), axis=1, keepdims=True)
-
-    coarse = lambda a, g: bottom[a, g]
-    e = [jnp.zeros((128, 128), F32)] * ny
-    norm = total([a * a for a in r])
-
-    def body(i, carry):
-        e, r, p, norm = carry
-        q = [inside(g, a) for g, a in enumerate(whole_operator(ny, coarse, p, 2))]
-        size = norm / total([a * b for a, b in zip(p, q)])
-        e = [a + size * b for a, b in zip(e, p)]
-        r = [a - size * b for a, b in zip(r, q)]
-        after = total([a * a for a in r])
-        p = [a + after / norm * b for a, b in zip(r, p)]
-        return e, r, p, after
-
-    e, r, p, norm = lax.fori_loop(0, BOTTOM - 1, body, (e, r, r, norm))
-    q = [inside(g, a) for g, a in enumerate(whole_operator(ny, coarse, p, 2))]
-    size = norm / total([a * b for a, b in zip(p, q)])
-    for g in range(ny):
-        value = e[g] + size * p[g]
+        g3[g] = inverse[g] * f(g)
+        ds[g] = g3[g] * (1.0 / THETA)
+        xa[g, pl.ds(PAD, 128)] = ds[g]
+    advance(xa, xb, STEP1, False)
+    advance(xb, xa, STEP2, False, False)
+    remainder = scaled(xa)
+    r = fold_level([children(remainder[g] * diagonal[g], "xyz") * 0.125 for g in range(ny)])
+    r = jnp.where(bottom[6] > 0.0, r, 0.0)
+
+    def total(value):
+        value = jnp.sum(value.reshape(8, 8, 128), axis=0)
+        return jnp.sum(jnp.sum(value, axis=1, keepdims=True), axis=0, keepdims=True)
+
+    def applied(v):
+        near = bottom_neighbours(v)
+        parts = [bottom[i] * near[i] for i in range(6)]
+        return bottom[6] * v - (((parts[0] + parts[1]) + (parts[2] + parts[3])) + (parts[4] + parts[5]))
+
+    e = jnp.zeros((64, 128), F32)
+    p, norm = r, total(r * r)
+    for i in range(BOTTOM):
+        q = applied(p)
+        size = norm / total(p * q)
+        e = e + size * p
+        if i + 1 < BOTTOM:
+            r = r - size * q
+            after = total(r * r)
+            p = r + after / norm * p
+            norm = after
+    for g, value in enumerate(unfold_level(e)):
         value = value + roll_lanes(value, 1)
         value = value + roll_lanes(value, 6)
-        xs[g] = xs[g] + (value + roll_rows(value, 1))
-    for number, coefs in enumerate((None, STEP1, STEP2)):
-        remainder = residual(load(xs))
-        for g in range(ny):
-            update = inverse[g] * remainder[g]
-            if number == 0:
-                update = update * (1.0 / THETA)
-            else:
-                update = coefs[0] * ds[g] + coefs[1] * update
-            ds[g] = update
-            xs[g] = xs[g] + update
-
-
-def coarse_fields(ny, fields, bottom):
-    rows = lax.broadcasted_iota(jnp.int32, (128, 128), 0)
-    lane = lanes(128)
-    even = (rows % 2 == 0) & (lane % 2 == 0) & ((lane // 6) % 2 == 0) & (lane < 72)
-    for g in range(ny):
-        for a, axes in enumerate(("yz", "xz", "xy", "xyz")):
-            factor = 0.125 if a == 3 else 0.0625
-            bottom[a, g] = jnp.where(even, children(fields(a, g), axes) * factor, 0.0)
+        xa[g, pl.ds(PAD, 128)] = rows(xa, g) + (value + roll_rows(value, 1))
+    advance(xa, xb, None, True)
+    advance(xb, xa, STEP1, False)
+    advance(xa, xb, STEP2, False, False)
 
 
 def window(lv, gx, gy, gz, ny, xs, padded, turned, corner, x):
     nz = 16
     padded[...] = jnp.zeros_like(padded)
     for g in range(ny):
-        padded[g + 1, pl.ds(1, nz)] = xs[g].reshape(nz, 8, 128)
+        padded[g + 1, pl.ds(1, nz)] = xs[g, pl.ds(PAD, 128)].reshape(nz, 8, 128)
     for dy in range(3):
         tiles = padded[gy + dy, pl.ds(gz, 3)].reshape(24, 128)
         tiles = jnp.concatenate([tiles, jnp.zeros((104, 128), F32)], axis=0)
@@ -622,14 +687,15 @@
     with scope("greet"):
         for t in order:
             oy, oz = other(t)
-            pl.semaphore_signal(barrier, inc=1, device_id=(gx, oy, oz), device_id_type=MESH)
+            for ox in (gx, 1 - gx):
+                pl.semaphore_signal(barrier, inc=1, device_id=(ox, oy, oz), device_id_type=MESH)
         pl.semaphore_signal(barrier, inc=1, device_id=(1 - gx, gy, gz), device_id_type=MESH)
 
     f0, f1, f2 = s["f0"], s["f1"], s["f2"]
     ex = {k: Exchange(*v) for k, v in EXCHANGES.items()}
     targets = {"e0": f0, "c1": f1, "c2": f2, "e1": f1, "e2": f2, "x0": s["x0a"], "x1": s["x1a"], "x2": s["x2a"]}
     for k, target in targets.items():
-        ex[k].bind(here, target, [s[k + str(i)] for i in range(6)])
+        ex[k].bind(here, target, [s[k + str(i)] for i in range(7)])
 
     def partner(src, dst, i):
         return pltpu.make_async_remote_copy(
@@ -643,7 +709,7 @@
 
     me = gy * nz + gz
 
-    def spread(src, whole, part, i):
+    def spread(src, whole, i):
         def copy(src, dst, oy, oz):
             return pltpu.make_async_remote_copy(
                 src_ref=src,
@@ -656,11 +722,10 @@
 
         def start():
             for t in order:
-                copy(src, part(whole.at[me]), *other(t)).start()
+                copy(src, whole.at[me], *other(t)).start()
 
         def finish():
             most = whole.at[pl.ds(0, ny * nz - 1)]
-            most = most.at[:, pl.ds(0, 2)] if i == 0 else most
             copy(most, most, *other(1)).wait()
 
         return start, finish
@@ -690,23 +755,23 @@
     with scope("e0_pack"):
         ex["e0"].pack_yz(False)
     with scope("barrier"):
-        pl.semaphore_wait(barrier, ny * nz)
+        pl.semaphore_wait(barrier, 2 * ny * nz - 1)
     ex["e0"].send_yz()
     with scope("coarsen_0"):
         coarsen_fields(L0, L1, f0, fields_put(L1, f1))
-    with scope("c1_start_yz"):
+    with scope("c1_pack"):
         ex["c1"].start_yz()
     with scope("coarsen_1"):
         coarsen_fields(L1, L2, f1, fields_put(L2, f2))
-    with scope("c2_start_yz"):
-        ex["c2"].start_yz()
+    with scope("c2_pack"):
+        ex["c2"].pack_yz(False)
     with scope("coarsen_2"):
         coarsen_fields(L2, None, f2, block_put)
 
     def tile_of(field):
         return roll_lanes(block[field].T[0:8], gx * 36)
 
-    own4, pair4, own1, pair1, own_n, pair_n = (s[k] for k in ("own4", "pair4", "own1", "pair1", "own_n", "pair_n"))
+    own4, pair4, own1, pair1, own_n = (s[k] for k in ("own4", "pair4", "own1", "pair1", "own_n"))
     for field in range(4):
         own4[field] = tile_of(field)
     pair_coef = partner(own4, pair4, 0)
@@ -721,18 +786,56 @@
     with scope("e0_finish_yz"):
         ex["e0"].finish_yz()
     ex["e0"].start_x()
+    ex["c2"].send_yz()
     g4, g1, gn = s["g4"], s["g1"], s["gn"]
     with scope("pair_coef"):
         pair_coef.wait()
     merged = s["merged4"]
     merged[...] = own4[...] + pair4[...]
     mine = pl.ds(2 * gx, 2)
-    g4[me, mine] = merged[mine]
-    coef_start, coef_finish = spread(merged.at[mine], g4, lambda slot: slot.at[mine], 0)
-    with scope("coef_start"):
-        coef_start()
+    g4[gy, gz, mine] = merged[mine]
+    row, column = gz // 4, gz % 4
+
+    def coef_part(stage):
+        if stage == 0:
+            return g4.at[gy, gz, mine]
+        if stage == 1:
+            return g4.at[:, gz, mine]
+        return g4.at[:, pl.ds(4 * row, 4), mine]
+
+    def coef_copy(stage, src, oy, oz):
+        return pltpu.make_async_remote_copy(
+            src_ref=src,
+            dst_ref=src,
+            send_sem=s["coef_send"].at[stage],
+            recv_sem=s["coef_recv"].at[stage],
+            device_id=(gx, oy, oz),
+            device_id_type=MESH,
+        )
+
+    def coef_start(stage):
+        for d in (2, 1, 3):
+            oy, oz = gy, gz
+            if stage == 0:
+                oy = lax.rem(gy + d, ny)
+            elif stage == 1:
+                oz = 4 * row + lax.rem(column + d, 4)
+            else:
+                oz = lax.rem(gz + 4 * d, nz)
+            coef_copy(stage, coef_part(stage), oy, oz).start()
+
+    def coef_wait(stage):
+        two = pl.ds(0, 2)
+        most = (g4.at[pl.ds(0, 3), 0, two], g4.at[:, pl.ds(0, 3), two], g4.at[:, pl.ds(0, 12), two])[stage]
+        coef_copy(stage, most, lax.rem(gy + 1, ny), gz).wait()
+
+    with scope("coef_0"):
+        coef_start(0)
+    with scope("c1_finish_yz"):
+        ex["c1"].finish_yz()
     with scope("e0_finish_x"):
         ex["e0"].finish_x()
+    ex["c1"].start_x()
     with scope("scaling_0"):
         scaling(L0, f0, s["i0"], s["u0"], 3)
     with scope("smooth_0"):
@@ -741,22 +844,25 @@
         restrict(L0, L1, f0, s["u0"], s["x0a"], s["sums"], fields_put(L1, f1))
     with scope("e1_start_yz"):
         ex["e1"].start_yz()
-    with scope("c1_finish_yz"):
-        ex["c1"].finish_yz()
-    ex["c1"].start_x()
+    with scope("coef_1"):
+        coef_wait(0)
+        coef_start(1)
     with scope("x0_start_yz"):
         ex["x0"].start_yz()
     with scope("c1_finish_x"):
         ex["c1"].finish_x()
     with scope("scaling_1"):
         scaling(L1, f1, s["i1"], s["u1"], 4)
+    with scope("c2_finish_yz"):
+        ex["c2"].finish_yz()
     with scope("e1_finish_yz"):
         ex["e1"].finish_yz()
     ex["e1"].start_x()
-    with scope("c2_finish_yz"):
-        ex["c2"].finish_yz()
     with scope("e1_finish_x"):
         ex["e1"].finish_x()
+    with scope("coef_2"):
+        coef_wait(1)
+        coef_start(2)
     with scope("smooth_1"):
         smooth_from_zero(L1, f1, s["i1"], s["u1"], s["x1a"], s["x1b"], s["d1"], 3)
     with scope("restrict_1"):
@@ -770,22 +876,19 @@
         ex["c2"].finish_x()
     with scope("scaling_2"):
         scaling(L2, f2, s["i2"], s["u2"], 5)
-    with scope("coef_finish"):
-        coef_finish()
     other_half = pltpu.make_async_remote_copy(
-        src_ref=g4.at[:, mine],
-        dst_ref=g4.at[:, mine],
+        src_ref=g4.at[:, :, mine],
+        dst_ref=g4.at[:, :, mine],
         send_sem=s["pair_send"].at[3],
         recv_sem=s["pair_recv"].at[3],
         device_id=(1 - gx, gy, gz),
         device_id_type=MESH,
     )
+    with scope("x0_finish_yz"):
+        ex["x0"].finish_yz()
     with scope("e2_finish_yz"):
         ex["e2"].finish_yz()
     ex["e2"].start_x()
-    other_half.start()
-    with scope("x0_finish_yz"):
-        ex["x0"].finish_yz()
     with scope("e2_finish_x"):
         ex["e2"].finish_x()
     with scope("smooth_2"):
@@ -796,23 +899,18 @@
     pair_source = partner(own1, pair1, 1)
     pair_source.start()
     ex["x0"].start_x()
+    with scope("coef_finish"):
+        coef_wait(2)
+    other_half.start()
     with scope("x2_start_yz"):
         ex["x2"].start_yz()
     with scope("pair_source"):
         pair_source.wait()
     s["merged1"][...] = own1[...] + pair1[...]
     g1[me] = s["merged1"][...]
-    source_start, source_finish = spread(s["merged1"], g1, lambda slot: slot, 1)
+    source_start, source_finish = spread(s["merged1"], g1, 1)
     with scope("source_start"):
         source_start()
-    with scope("other_half"):
-        other_half.wait()
-    gathered = lambda a, g: g4[pl.ds(g * nz, nz), a].reshape(128, 128)
-    with scope("coarse_fields"):
-        inverse = whole_inverse(ny, gathered)
-        for g in range(ny):
-            s["i3"][g] = inverse[g]
-        coarse_fields(ny, gathered, s["bottom"])
     with scope("hidden"):
         ex["x1"].finish_yz()
         ex["x1"].start_x()
@@ -821,12 +919,20 @@
         ex["x2"].start_x()
         ex["x1"].finish_x()
         ex["x2"].finish_x()
+    with scope("other_half"):
+        other_half.wait()
+    gathered = lambda a, g: g4[g, :, a].reshape(128, 128)
+    with scope("coarse_fields"):
+        whole_prepare(ny, gathered, s["c3"], s["w3"], s["i3"])
+        bottom_prepare(ny, gathered, s["bottom"])
     with scope("source_finish"):
         source_finish()
     with scope("coarse_solve"):
-        coarse_solve(ny, gathered, lambda g: g1[pl.ds(g * nz, nz)].reshape(128, 128), s["i3"], s["bottom"], s["x3"], s["d3"])
+        source = lambda g: g1[pl.ds(g * nz, nz)].reshape(128, 128)
+        whole = [s[k] for k in ("c3", "w3", "i3")]
+        coarse_solve(ny, *whole, source, s["bottom"], s["x3a"], s["x3b"], s["d3"], s["g3"])
     with scope("window"):
-        window(L2, gx, gy, gz, ny, s["x3"], s["padded"], s["turned"], s["corner"], s["x2a"])
+        window(L2, gx, gy, gz, ny, s["x3b"], s["padded"], s["turned"], s["corner"], s["x2a"])
     with scope("post_2"):
         smooth(L2, f2, s["i2"], s["u2"], s["x2a"], s["x2b"], s["d2"], 6)
     with scope("prolong_1"):
@@ -860,9 +966,30 @@
     def fold(value):
         return jnp.sum(value, axis=0, keepdims=True)
 
-    own_n[...] = jnp.concatenate([fold(squares), fold(ends), jnp.zeros((6, 128), F32)], axis=0)
-    pair_norm = partner(own_n, pair_n, 2)
-    pair_norm.start()
+    def squares_of(value):
+        return jnp.sum(fold(value), axis=1, keepdims=True)
+
+    lane1 = lax.broadcasted_iota(jnp.int32, (1, 128), 1)
+    pair = jnp.where(lane1 == 0, squares_of(squares), jnp.where(lane1 == 1, squares_of(ends), 0.0))
+    own_n[...] = pair
+    mine_n = gx * (ny * nz) + me
+    gn[mine_n] = pair
+
+    def norm_copy(src, dst, ox, oy, oz):
+        return pltpu.make_async_remote_copy(
+            src_ref=src,
+            dst_ref=dst,
+            send_sem=s["all_send"].at[2],
+            recv_sem=s["all_recv"].at[2],
+            device_id=(ox, oy, oz),
+            device_id_type=MESH,
+        )
+
+    with scope("norm_start"):
+        for t in order:
+            for ox in (gx, 1 - gx):
+                norm_copy(own_n, gn.at[mine_n], ox, *other(t)).start()
+        norm_copy(own_n, gn.at[mine_n], 1 - gx, gy, gz).start()
 
     def unload(slot, i, value):
         for half in range(2):
@@ -881,22 +1008,15 @@
         loop(0, 24, out_solution, 0, 6)
     out0 = pltpu.make_async_copy(land.at[0], solution_hbm, s["out_sem"].at[0])
     out0.start()
-    with scope("pair_norm"):
-        pair_norm.wait()
-    s["merged_n"][...] = jnp.where(gx == 0, own_n[...] + pair_n[...], pair_n[...] + own_n[...])
-    gn[me] = s["merged_n"][...]
-    norm_start, norm_finish = spread(s["merged_n"], gn, lambda slot: slot, 2)
-    with scope("norm_start"):
-        norm_start()
     with scope("unload_residual"):
         loop(0, 24, out_residual, 0, 6)
     out1 = pltpu.make_async_copy(land.at[1], residual_hbm, s["out_sem"].at[1])
     out1.start()
     with scope("norm_finish"):
-        norm_finish()
-    all_n = jnp.sum(gn[...], axis=0)
-    sums = jnp.sum(all_n, axis=1, keepdims=True)
-    norm = jnp.sqrt(sums[1:2] / sums[0:1])
+        most = gn.at[pl.ds(0, 2 * ny * nz - 1)]
+        norm_copy(most, most, 1 - gx, gy, gz).wait()
+    sums = jnp.sum(gn[...], axis=0)
+    norm = jnp.sqrt(sums[:, 1:2] / sums[:, 0:1])
     norm_out[0, 0] = norm[0, 0]
     with scope("out_wait"):
         out0.wait()
@@ -929,18 +1049,22 @@
     scratch["block"] = vmem(5, 128, 128)
     for k in ("own4", "pair4", "merged4"):
         scratch[k] = vmem(4, 8, 128)
-    for k in ("own1", "pair1", "merged1", "own_n", "pair_n", "merged_n"):
+    for k in ("own1", "pair1", "merged1"):
         scratch[k] = vmem(8, 128)
-    scratch["g4"] = vmem(ny * nz, 4, 8, 128)
+    scratch["g4"] = vmem(ny, nz, 4, 8, 128)
     scratch["g1"] = vmem(ny * nz, 8, 128)
-    scratch["gn"] = vmem(ny * nz, 8, 128)
+    scratch["gn"] = vmem(2 * ny * nz, 1, 128)
+    scratch["own_n"] = vmem(1, 128)
     for k in ("pair_send", "pair_recv"):
         scratch[k] = pltpu.SemaphoreType.DMA((4,))
-    for k in ("all_send", "all_recv"):
+    for k in ("all_send", "all_recv", "coef_send", "coef_recv"):
         scratch[k] = pltpu.SemaphoreType.DMA((3,))
-    for k in ("i3", "x3", "d3"):
+    for k in ("i3", "w3", "d3", "g3"):
         scratch[k] = vmem(ny, 128, 128)
-    scratch["bottom"] = vmem(4, ny, 128, 128)
+    for k in ("x3a", "x3b"):
+        scratch[k] = vmem(ny, 128 + 2 * PAD, 128)
+    scratch["c3"] = vmem(6, ny, 128, 128)
+    scratch["bottom"] = vmem(7, 64, 128)
     scratch["padded"] = vmem(ny + 2, nz + 2, 8, 128)
     scratch["turned"] = vmem(3, 152, 128)
     scratch["corner"] = vmem(16, 128)
@@ -958,8 +1082,8 @@
         field = jax.ShapeDtypeStruct((48, 48, 48), F32)
         solved, residual, norm = pl.pallas_call(
             functools.partial(cycle, ny, nz, tuple(scratch)),
-            out_shape=(field, field, jax.ShapeDtypeStruct((1, 1), F32)),
-            in_specs=[pl.BlockSpec(memory_space=pl.ANY)] * 3,
+            out_shape=(pltpu.VMEM((48, 48, 48), F32), pltpu.VMEM((48, 48, 48), F32), jax.ShapeDtypeStruct((1, 1), F32)),
+            in_specs=[pl.BlockSpec(memory_space=pltpu.HBM)] * 3,
             out_specs=(
                 pl.BlockSpec(memory_space=pl.ANY),
                 pl.BlockSpec(memory_space=pl.ANY),
@@ -967,7 +1091,7 @@
             ),
             scratch_shapes=list(scratch.values()),
             compiler_params=pltpu.CompilerParams(
-                collective_id=0, has_side_effects=True, vmem_limit_bytes=62 * 1024 * 1024
+                collective_id=0, has_side_effects=True, vmem_limit_bytes=57000 * 1024
             ),
         )(right_side, face_coef, absorption)
         return solved, residual, norm[0, 0]

time: 90 us -> 79.6 us (0.88)
  Pallas kernels: 83.8 us -> 74.4 us
  local copies, waits for them, and re-layouts: 3.47 us -> 2.03 us
    pallas_call x1, Pallas kernels: 83.8 us -> 74.4 us  [shards(): pl.pallas_call(functools.partial(cycle, ny, nz, tuple(scratch)), out_shap...]
    unnamed x4 -> x2, local copies, waits for them, and re-layouts: 3.47 us -> 2.03 us
where the time goes in v4:
time: 79.6 us; the launch traced here: 78.8 us
  Pallas kernels  74.4 us (93%)
  between operations  2.33 us (3%)
  local copies, waits for them, and re-layouts  2.03 us (3%)
    pallas_call x1, Pallas kernels, shards(): pl.pallas_call(functools.partial(cycle, ny, nz, tuple(scratch)), out_shap...  74.4 us
    unnamed x2, local copies, waits for them, and re-layouts  2.03 us

profile of v4, /device:TPU:0, one launch (start us, length us, event | category | flops | bytes accessed | tf_op | source)
XLA Modules:
  0.0 78.8 jit_solution(8405856413779818047)
XLA Ops:
  0.6 74.4 %shard_map.58 = (f32[48,48,48]{2,1,0:T(8,128)S(1)}, f32[48,48,48]{2,1,0:T(8,128)S(1)}, f32[1,1]{1,0:T(1,128)}) custom-call(f32[48,48,48]{2,1,0:T(8,128)} %refs_0_.1, f32[3,48,48,48]{3,2,1,0:T(8,128)} %refs_1_.1, f32[48,48,48]{2,1,0:T(8,128)} %refs_2_.1), custom_call_target="tpu_custom_call" | custom-call | tf_op jit(solution)/shard_map/pallas_call | solution.py:1083
  75.0 1.0 %copy.9 = f32[48,48,48]{2,1,0:T(8,128)} copy(f32[48,48,48]{2,1,0:T(8,128)S(1)} %get-tuple-element.9) | data formatting | bytes 884736
  76.1 1.0 %copy.10 = f32[48,48,48]{2,1,0:T(8,128)} copy(f32[48,48,48]{2,1,0:T(8,128)S(1)} %get-tuple-element.10) | data formatting | bytes 884736

commit v5 on v4

--- a/solution.py
+++ b/solution.py
@@ -308,10 +308,8 @@
         row = pl.multiple_of(p * r, 8)
         after = x[0, pl.ds(row + r, r), :]
         flux_after = fields[0, pl.ds(row + r, r), :] * (after - here)
-        low_y = x[0, pl.ds(row - 1, r), :]
-        high_y = x[0, pl.ds(row + 1, r), :]
-        flux_y = fields[1, pl.ds(row, r), :] * (here - low_y)
-        flux_y = flux_y - fields[1, pl.ds(row + 1, r), :] * (high_y - here)
+        flux_y = fields[1, pl.ds(row, r), :] * (here - roll_rows(here, 1))
+        flux_y = flux_y - fields[1, pl.ds(row + 1, r), :] * (roll_rows(here, -1) - here)
         flux_z = fields[2, pl.ds(row, r), :] * (here - roll_lanes(here, 1))
         flux_z = flux_z - upper[0, pl.ds(row, r), :] * (roll_lanes(here, -1) - here)
         applied = fields[3, pl.ds(row, r), :] * here + ((flux - flux_after) + flux_y + flux_z)
@@ -693,7 +691,7 @@
 
     f0, f1, f2 = s["f0"], s["f1"], s["f2"]
     ex = {k: Exchange(*v) for k, v in EXCHANGES.items()}
-    targets = {"e0": f0, "c1": f1, "c2": f2, "e1": f1, "e2": f2, "x0": s["x0a"], "x1": s["x1a"], "x2": s["x2a"]}
+    targets = {"e0a": f0, "e0b": f0, "e0c": f0, "c1": f1, "c2": f2, "e1": f1, "e2": f2, "x0": s["x0a"], "x1": s["x1a"], "x2": s["x2a"]}
     for k, target in targets.items():
         ex[k].bind(here, target, [s[k + str(i)] for i in range(7)])
 
@@ -750,17 +748,20 @@
             return carry
 
         with scope("layout"):
-            loop(0, 24, load, 0, 6)
+            loop(0, 24, load, 0, 12)
 
     with scope("e0_pack"):
-        ex["e0"].pack_yz(False)
+        ex["e0a"].pack_yz(False)
     with scope("barrier"):
         pl.semaphore_wait(barrier, 2 * ny * nz - 1)
-    ex["e0"].send_yz()
+    ex["e0a"].send_yz()
+    with scope("e0_start_yz"):
+        ex["e0b"].start_yz()
+        ex["e0c"].start_yz()
     with scope("coarsen_0"):
         coarsen_fields(L0, L1, f0, fields_put(L1, f1))
     with scope("c1_pack"):
-        ex["c1"].start_yz()
+        ex["c1"].pack_yz(False)
     with scope("coarsen_1"):
         coarsen_fields(L1, L2, f1, fields_put(L2, f2))
     with scope("c2_pack"):
@@ -783,9 +784,11 @@
 
     with scope("square"):
         squares = loop(0, 24, square, jnp.zeros((48, 128), F32), 4)
-    with scope("e0_finish_yz"):
-        ex["e0"].finish_yz()
-    ex["e0"].start_x()
+    for k in ("e0a", "e0b", "e0c"):
+        with scope(k + "_finish_yz"):
+            ex[k].finish_yz()
+        ex[k].start_x()
+    ex["c1"].send_yz()
     ex["c2"].send_yz()
     g4, g1, gn = s["g4"], s["g1"], s["gn"]
     with scope("pair_coef"):
@@ -831,13 +834,13 @@
 
     with scope("coef_0"):
         coef_start(0)
-    with scope("c1_finish_yz"):
-        ex["c1"].finish_yz()
     with scope("e0_finish_x"):
-        ex["e0"].finish_x()
-    ex["c1"].start_x()
+        ex["e0a"].finish_x()
+        ex["e0b"].finish_x()
     with scope("scaling_0"):
         scaling(L0, f0, s["i0"], s["u0"], 3)
+    with scope("e0c_finish_x"):
+        ex["e0c"].finish_x()
     with scope("smooth_0"):
         smooth_from_zero(L0, f0, s["i0"], s["u0"], s["x0a"], s["x0b"], s["d0"], 3)
     with scope("restrict_0"):
@@ -847,17 +850,20 @@
     with scope("coef_1"):
         coef_wait(0)
         coef_start(1)
-    with scope("x0_start_yz"):
-        ex["x0"].start_yz()
+    with scope("c1_finish_yz"):
+        ex["c1"].finish_yz()
+    ex["c1"].start_x()
+    with scope("c2_finish_yz"):
+        ex["c2"].finish_yz()
     with scope("c1_finish_x"):
         ex["c1"].finish_x()
     with scope("scaling_1"):
         scaling(L1, f1, s["i1"], s["u1"], 4)
-    with scope("c2_finish_yz"):
-        ex["c2"].finish_yz()
     with scope("e1_finish_yz"):
         ex["e1"].finish_yz()
     ex["e1"].start_x()
+    with scope("x0_start_yz"):
+        ex["x0"].start_yz()
     with scope("e1_finish_x"):
         ex["e1"].finish_x()
     with scope("coef_2"):
@@ -1024,7 +1030,9 @@
 
 
 EXCHANGES = {
-    "e0": (L0, 0, 5),
+    "e0a": (L0, 0, 2),
+    "e0b": (L0, 2, 2),
+    "e0c": (L0, 4, 1),
     "c1": (L1, 0, 4),
     "c2": (L2, 0, 4),
     "e1": (L1, 4, 1),

time: 79.6 us -> 74.6 us (0.937)
  Pallas kernels: 74.4 us -> 69.4 us
    pallas_call x1, Pallas kernels: 74.4 us -> 69.4 us  [shards(): pl.pallas_call(functools.partial(cycle, ny, nz, tuple(scratch)), out_shap...]
where the time goes in v5:
time: 74.6 us; the launch traced here: 73.8 us
  Pallas kernels  69.4 us (93%)
  between operations  2.33 us (3%)
  local copies, waits for them, and re-layouts  2.03 us (3%)
    pallas_call x1, Pallas kernels, shards(): pl.pallas_call(functools.partial(cycle, ny, nz, tuple(scratch)), out_shap...  69.4 us
    unnamed x2, local copies, waits for them, and re-layouts  2.03 us

profile of v5, /device:TPU:0, one launch (start us, length us, event | category | flops | bytes accessed | tf_op | source)
XLA Modules:
  0.0 73.8 jit_solution(3529204569781505161)
XLA Ops:
  0.6 69.4 %shard_map.58 = (f32[48,48,48]{2,1,0:T(8,128)S(1)}, f32[48,48,48]{2,1,0:T(8,128)S(1)}, f32[1,1]{1,0:T(1,128)}) custom-call(f32[48,48,48]{2,1,0:T(8,128)} %refs_0_.1, f32[3,48,48,48]{3,2,1,0:T(8,128)} %refs_1_.1, f32[48,48,48]{2,1,0:T(8,128)} %refs_2_.1), custom_call_target="tpu_custom_call" | custom-call | tf_op jit(solution)/shard_map/pallas_call | solution.py:1091
  70.1 1.0 %copy.9 = f32[48,48,48]{2,1,0:T(8,128)} copy(f32[48,48,48]{2,1,0:T(8,128)S(1)} %get-tuple-element.9) | data formatting | bytes 884736
  71.1 1.0 %copy.10 = f32[48,48,48]{2,1,0:T(8,128)} copy(f32[48,48,48]{2,1,0:T(8,128)S(1)} %get-tuple-element.10) | data formatting | bytes 884736

commit v6 on v5

--- a/solution.py
+++ b/solution.py
@@ -728,10 +728,7 @@
 
         return start, finish
 
-    f1[...] = jnp.zeros_like(f1)
-    f2[...] = jnp.zeros_like(f2)
     block = s["block"]
-    block[...] = jnp.zeros_like(block)
 
     def block_put(field, plane, value):
         block[field, pl.ds(plane * 6, 6), :] = value
@@ -758,6 +755,9 @@
     with scope("e0_start_yz"):
         ex["e0b"].start_yz()
         ex["e0c"].start_yz()
+    f1[...] = jnp.zeros_like(f1)
+    f2[...] = jnp.zeros_like(f2)
+    block[...] = jnp.zeros_like(block)
     with scope("coarsen_0"):
         coarsen_fields(L0, L1, f0, fields_put(L1, f1))
     with scope("c1_pack"):
@@ -789,7 +789,6 @@
             ex[k].finish_yz()
         ex[k].start_x()
     ex["c1"].send_yz()
-    ex["c2"].send_yz()
     g4, g1, gn = s["g4"], s["g1"], s["gn"]
     with scope("pair_coef"):
         pair_coef.wait()
@@ -847,14 +846,15 @@
         restrict(L0, L1, f0, s["u0"], s["x0a"], s["sums"], fields_put(L1, f1))
     with scope("e1_start_yz"):
         ex["e1"].start_yz()
+    ex["c2"].send_yz()
+    with scope("c1_finish_yz"):
+        ex["c1"].finish_yz()
+    ex["c1"].start_x()
     with scope("coef_1"):
         coef_wait(0)
         coef_start(1)
-    with scope("c1_finish_yz"):
-        ex["c1"].finish_yz()
-    ex["c1"].start_x()
-    with scope("c2_finish_yz"):
-        ex["c2"].finish_yz()
+    with scope("x0_start_yz"):
+        ex["x0"].start_yz()
     with scope("c1_finish_x"):
         ex["c1"].finish_x()
     with scope("scaling_1"):
@@ -862,8 +862,6 @@
     with scope("e1_finish_yz"):
         ex["e1"].finish_yz()
     ex["e1"].start_x()
-    with scope("x0_start_yz"):
-        ex["x0"].start_yz()
     with scope("e1_finish_x"):
         ex["e1"].finish_x()
     with scope("coef_2"):
@@ -875,6 +873,8 @@
         restrict(L1, L2, f1, s["u1"], s["x1a"], s["sums"], fields_put(L2, f2))
     with scope("e2_start_yz"):
         ex["e2"].start_yz()
+    with scope("c2_finish_yz"):
+        ex["c2"].finish_yz()
     ex["c2"].start_x()
     with scope("x1_start_yz"):
         ex["x1"].start_yz()
@@ -890,11 +890,11 @@
         device_id=(1 - gx, gy, gz),
         device_id_type=MESH,
     )
-    with scope("x0_finish_yz"):
-        ex["x0"].finish_yz()
     with scope("e2_finish_yz"):
         ex["e2"].finish_yz()
     ex["e2"].start_x()
+    with scope("x0_finish_yz"):
+        ex["x0"].finish_yz()
     with scope("e2_finish_x"):
         ex["e2"].finish_x()
     with scope("smooth_2"):
@@ -905,9 +905,6 @@
     pair_source = partner(own1, pair1, 1)
     pair_source.start()
     ex["x0"].start_x()
-    with scope("coef_finish"):
-        coef_wait(2)
-    other_half.start()
     with scope("x2_start_yz"):
         ex["x2"].start_yz()
     with scope("pair_source"):
@@ -917,26 +914,31 @@
     source_start, source_finish = spread(s["merged1"], g1, 1)
     with scope("source_start"):
         source_start()
-    with scope("hidden"):
+    with scope("coef_finish"):
+        coef_wait(2)
+    other_half.start()
+    with scope("hidden_1"):
         ex["x1"].finish_yz()
         ex["x1"].start_x()
         ex["x0"].finish_x()
-        ex["x2"].finish_yz()
-        ex["x2"].start_x()
-        ex["x1"].finish_x()
-        ex["x2"].finish_x()
     with scope("other_half"):
         other_half.wait()
     gathered = lambda a, g: g4[g, :, a].reshape(128, 128)
     with scope("coarse_fields"):
         whole_prepare(ny, gathered, s["c3"], s["w3"], s["i3"])
         bottom_prepare(ny, gathered, s["bottom"])
+    with scope("hidden_2"):
+        ex["x1"].finish_x()
+        ex["x2"].finish_yz()
+        ex["x2"].start_x()
     with scope("source_finish"):
         source_finish()
     with scope("coarse_solve"):
         source = lambda g: g1[pl.ds(g * nz, nz)].reshape(128, 128)
         whole = [s[k] for k in ("c3", "w3", "i3")]
         coarse_solve(ny, *whole, source, s["bottom"], s["x3a"], s["x3b"], s["d3"], s["g3"])
+    with scope("x2_finish_x"):
+        ex["x2"].finish_x()
     with scope("window"):
         window(L2, gx, gy, gz, ny, s["x3b"], s["padded"], s["turned"], s["corner"], s["x2a"])
     with scope("post_2"):

time: 74.6 us -> 73.4 us (0.984)
  Pallas kernels: 69.4 us -> 68.3 us
    pallas_call x1, Pallas kernels: 69.4 us -> 68.3 us  [shards(): pl.pallas_call(functools.partial(cycle, ny, nz, tuple(scratch)), out_shap...]
where the time goes in v6:
time: 73.4 us; the launch traced here: 72.6 us
  Pallas kernels  68.3 us (93%)
  between operations  2.33 us (3%)
  local copies, waits for them, and re-layouts  2.03 us (3%)
    pallas_call x1, Pallas kernels, shards(): pl.pallas_call(functools.partial(cycle, ny, nz, tuple(scratch)), out_shap...  68.3 us
    unnamed x2, local copies, waits for them, and re-layouts  2.03 us

profile of v6, /device:TPU:0, one launch (start us, length us, event | category | flops | bytes accessed | tf_op | source)
XLA Modules:
  0.0 72.6 jit_solution(17777594705783263405)
XLA Ops:
  0.6 68.3 %shard_map.58 = (f32[48,48,48]{2,1,0:T(8,128)S(1)}, f32[48,48,48]{2,1,0:T(8,128)S(1)}, f32[1,1]{1,0:T(1,128)}) custom-call(f32[48,48,48]{2,1,0:T(8,128)} %refs_0_.1, f32[3,48,48,48]{3,2,1,0:T(8,128)} %refs_1_.1, f32[48,48,48]{2,1,0:T(8,128)} %refs_2_.1), custom_call_target="tpu_custom_call" | custom-call | tf_op jit(solution)/shard_map/pallas_call | solution.py:1093
  68.9 1.0 %copy.9 = f32[48,48,48]{2,1,0:T(8,128)} copy(f32[48,48,48]{2,1,0:T(8,128)S(1)} %get-tuple-element.9) | data formatting | bytes 884736
  69.9 1.0 %copy.10 = f32[48,48,48]{2,1,0:T(8,128)} copy(f32[48,48,48]{2,1,0:T(8,128)S(1)} %get-tuple-element.10) | data formatting | bytes 884736

commit v7 on v6

--- a/solution.py
+++ b/solution.py
@@ -83,10 +83,10 @@
         lv, na = self.level, self.count
         shapes = [
             (na, lv.e * lv.rows, 128),
-            (na, self.starts[8], 128),
-            (na, self.starts[8], 128),
-            (na, self.starts[8], 128),
-            (2, na, lv.packs * lv.rows, 128),
+            (na, self.starts[8] + 8, 128),
+            (na, self.starts[8] + 8, 128),
+            (na, self.starts[8] + 8, 128),
+            (2, na, lv.packs * lv.rows + 8, 128),
         ]
         return [pltpu.VMEM(s, F32) for s in shapes] + [pltpu.SemaphoreType.DMA((2,)), pltpu.SemaphoreType.DMA((2,))]
 
@@ -125,7 +125,8 @@
         ]
         y_side, z_side = [gy > 0, gy < ny - 1], [gz > 0, gz < nz - 1]
         self.exists = y_side + z_side + [a & b for a in y_side for b in z_side]
-        self.all = copy(self.out, self.got, 1, gx, *targets[0])
+        whole = pl.ds(0, self.starts[8])
+        self.all = copy(self.out.at[:, whole, :], self.got.at[:, whole, :], 1, gx, *targets[0])
         self.has_y = [jnp.where(gy > 0, 1.0, 0.0).astype(F32), jnp.where(gy < ny - 1, 1.0, 0.0).astype(F32)]
         self.has_z = [jnp.where(gz > 0, 1.0, 0.0).astype(F32), jnp.where(gz < nz - 1, 1.0, 0.0).astype(F32)]
         self.has_x = [gx.astype(F32), (1 - gx).astype(F32)]
@@ -648,7 +649,7 @@
         corner[pl.ds(0, 3), :] = turned[0, pl.ds(base + 3, 3), :]
         corner[pl.ds(3, 6), :] = turned[1, pl.ds(base, 6), :]
         corner[pl.ds(9, 3), :] = turned[2, pl.ds(base, 3), :]
-        value = jnp.where(inside, gather_lanes(corner[...], source), 0.0)[0:12]
+        value = jnp.where(inside, gather_lanes(corner[0:16], source), 0.0)[0:12]
         for plane in range(2):
             at = (lv.e - 6 + 2 * i + plane) * lv.rows + lv.e - 6
             for odd in range(2):
@@ -1047,7 +1048,7 @@
 
 def scratch_of(ny, nz):
     vmem = lambda *shape: pltpu.VMEM(shape, F32)
-    size = lambda lv: lv.planes * lv.rows
+    size = lambda lv: lv.planes * lv.rows + 16
     scratch = {"land": vmem(5, 48, 48, 48), "load_sem": pltpu.SemaphoreType.DMA((5,)), "out_sem": pltpu.SemaphoreType.DMA((2,))}
     for i, lv in enumerate((L0, L1, L2)):
         scratch[f"f{i}"] = vmem(5, size(lv), 128)
@@ -1055,7 +1056,7 @@
             scratch[f"{k}{i}"] = vmem(1, size(lv), 128)
         scratch[f"x{i}a"] = vmem(1, size(lv), 128)
         scratch[f"x{i}b"] = vmem(1, size(lv), 128)
-    scratch["sums"] = vmem(1, 24 * 56, 128)
+    scratch["sums"] = vmem(1, 24 * 56 + 16, 128)
     scratch["block"] = vmem(5, 128, 128)
     for k in ("own4", "pair4", "merged4"):
         scratch[k] = vmem(4, 8, 128)
@@ -1076,8 +1077,8 @@
     scratch["c3"] = vmem(6, ny, 128, 128)
     scratch["bottom"] = vmem(7, 64, 128)
     scratch["padded"] = vmem(ny + 2, nz + 2, 8, 128)
-    scratch["turned"] = vmem(3, 152, 128)
-    scratch["corner"] = vmem(16, 128)
+    scratch["turned"] = vmem(3, 160, 128)
+    scratch["corner"] = vmem(24, 128)
     for k, v in EXCHANGES.items():
         for i, shape in enumerate(Exchange(*v).scratch()):
             scratch[k + str(i)] = shape

time: 73.4 us -> 74.2 us (1.011)
    pallas_call x1, Pallas kernels: 68.3 us -> 69 us  [shards(): pl.pallas_call(functools.partial(cycle, ny, nz, tuple(scratch)), out_shap...]
where the time goes in v7:
time: 74.2 us; the launch traced here: 73.4 us
  Pallas kernels  69 us (93%)
  between operations  2.33 us (3%)
  local copies, waits for them, and re-layouts  2.03 us (3%)
    pallas_call x1, Pallas kernels, shards(): pl.pallas_call(functools.partial(cycle, ny, nz, tuple(scratch)), out_shap...  69 us
    unnamed x2, local copies, waits for them, and re-layouts  2.03 us

profile of v7, /device:TPU:0, one launch (start us, length us, event | category | flops | bytes accessed | tf_op | source)
XLA Modules:
  0.0 73.4 jit_solution(10463698407164642203)
XLA Ops:
  0.6 69.0 %shard_map.58 = (f32[48,48,48]{2,1,0:T(8,128)S(1)}, f32[48,48,48]{2,1,0:T(8,128)S(1)}, f32[1,1]{1,0:T(1,128)}) custom-call(f32[48,48,48]{2,1,0:T(8,128)} %refs_0_.1, f32[3,48,48,48]{3,2,1,0:T(8,128)} %refs_1_.1, f32[48,48,48]{2,1,0:T(8,128)} %refs_2_.1), custom_call_target="tpu_custom_call" | custom-call | tf_op jit(solution)/shard_map/pallas_call | solution.py:1094
  69.7 1.0 %copy.9 = f32[48,48,48]{2,1,0:T(8,128)} copy(f32[48,48,48]{2,1,0:T(8,128)S(1)} %get-tuple-element.9) | data formatting | bytes 884736
  70.7 1.0 %copy.10 = f32[48,48,48]{2,1,0:T(8,128)} copy(f32[48,48,48]{2,1,0:T(8,128)S(1)} %get-tuple-element.10) | data formatting | bytes 884736

commit v8 on v7

--- a/solution.py
+++ b/solution.py
@@ -858,11 +858,11 @@
         ex["x0"].start_yz()
     with scope("c1_finish_x"):
         ex["c1"].finish_x()
-    with scope("scaling_1"):
-        scaling(L1, f1, s["i1"], s["u1"], 4)
     with scope("e1_finish_yz"):
         ex["e1"].finish_yz()
     ex["e1"].start_x()
+    with scope("scaling_1"):
+        scaling(L1, f1, s["i1"], s["u1"], 4)
     with scope("e1_finish_x"):
         ex["e1"].finish_x()
     with scope("coef_2"):
@@ -881,8 +881,6 @@
         ex["x1"].start_yz()
     with scope("c2_finish_x"):
         ex["c2"].finish_x()
-    with scope("scaling_2"):
-        scaling(L2, f2, s["i2"], s["u2"], 5)
     other_half = pltpu.make_async_remote_copy(
         src_ref=g4.at[:, :, mine],
         dst_ref=g4.at[:, :, mine],
@@ -896,6 +894,8 @@
     ex["e2"].start_x()
     with scope("x0_finish_yz"):
         ex["x0"].finish_yz()
+    with scope("scaling_2"):
+        scaling(L2, f2, s["i2"], s["u2"], 5)
     with scope("e2_finish_x"):
         ex["e2"].finish_x()
     with scope("smooth_2"):

time: 74.2 us -> 74.2 us (level)
  no operation moved by 1% of the time
where the time goes in v8:
time: 74.2 us; the launch traced here: 73.4 us
  Pallas kernels  69 us (93%)
  between operations  2.33 us (3%)
  local copies, waits for them, and re-layouts  2.03 us (3%)
    pallas_call x1, Pallas kernels, shards(): pl.pallas_call(functools.partial(cycle, ny, nz, tuple(scratch)), out_shap...  69 us
    unnamed x2, local copies, waits for them, and re-layouts  2.03 us

profile of v8, /device:TPU:0, one launch (start us, length us, event | category | flops | bytes accessed | tf_op | source)
XLA Modules:
  0.0 73.4 jit_solution(14204195428942474196)
XLA Ops:
  0.6 69.0 %shard_map.58 = (f32[48,48,48]{2,1,0:T(8,128)S(1)}, f32[48,48,48]{2,1,0:T(8,128)S(1)}, f32[1,1]{1,0:T(1,128)}) custom-call(f32[48,48,48]{2,1,0:T(8,128)} %refs_0_.1, f32[3,48,48,48]{3,2,1,0:T(8,128)} %refs_1_.1, f32[48,48,48]{2,1,0:T(8,128)} %refs_2_.1), custom_call_target="tpu_custom_call" | custom-call | tf_op jit(solution)/shard_map/pallas_call | solution.py:1094
  69.7 1.0 %copy.9 = f32[48,48,48]{2,1,0:T(8,128)} copy(f32[48,48,48]{2,1,0:T(8,128)S(1)} %get-tuple-element.9) | data formatting | bytes 884736
  70.7 1.0 %copy.10 = f32[48,48,48]{2,1,0:T(8,128)} copy(f32[48,48,48]{2,1,0:T(8,128)S(1)} %get-tuple-element.10) | data formatting | bytes 884736
